TPU v7x, 128 devices: a whole 4x4x4 slice. The times are simulated.
128 devices in a mesh: keys: 32 (over y, z, core), view: 4 (over x).
Axes of the slice: x: 4, y: 4, z: 4, core: 2. Of those that a mesh axis runs over, the one named last changes fastest.
Arguments:
- key_slot: int32 [16384], replicated, may hold values from 0 to 16383, as said below
- a_slot: int32 [524288], P(('keys', 'view')), may hold values from 0 to 511
- a_group: int32 [524288], P(('keys', 'view')), may hold values from 0 to 4095
- a_weight: int32 [524288], P(('keys', 'view')), may hold values from 1 to 3
- a_payload: bfloat16 [524288, 256], P(('keys', 'view')), may hold values from -1.1953125 to 1.1953125
- b_slot: int32 [524288], P(('keys', 'view')), may hold values from 0 to 511
- b_weight: int32 [524288], P(('keys', 'view')), may hold values from 1 to 3
- b_payload: bfloat16 [524288, 256], P(('keys', 'view')), may hold values from -0.59765625 to 0.59765625
- da_key: int32 [131072], P(('keys', 'view')), may hold values from 0 to 16383, as said below
- da_group: int32 [131072], P(('keys', 'view')), may hold values from 0 to 4095
- da_mult: int32 [131072], P(('keys', 'view')), may hold values from -1 to 1, as said below
- da_payload: bfloat16 [131072, 256], P(('keys', 'view')), may hold values from -1.796875 to 1.796875
- da_count: int32 [128], P(('keys', 'view')), may hold values from 768 to 1024, as said below
- db_key: int32 [131072], P(('keys', 'view')), may hold values from 0 to 16383, as said below
- db_mult: int32 [131072], P(('keys', 'view')), may hold values from -1 to 1, as said below
- db_payload: bfloat16 [131072, 256], P(('keys', 'view')), may hold values from -1.1953125 to 1.1953125
- db_count: int32 [128], P(('keys', 'view')), may hold values from 768 to 1024, as said below
Outputs:
- view_delta: float32 [4096, 256], P(('keys', 'view'))
Inputs may be any that keep to these rules, and one draw needn't show every extreme that they name: `key_slot`: A permutation of 0 to 16383. `da_key`: among the 1024 slots of one device, at most 64 have keys held by one keys index; in every draw one keys index gets exactly 64 live rows from every device. `db_key`: among the 1024 slots of one device, at most 64 have keys held by one keys index; in every draw one keys index gets exactly 64 live rows from every device. `da_mult`: each entry is -1 or 1. `db_mult`: each entry is -1 or 1. `da_count`: some device has all 1024 rows live. `db_count`: some device has all 1024 rows live.
All inputs are finite; a program needn't handle non-finite values.
Results may differ from a plain program's by a relative error of at most 0.0029.
Values may be sent and summed in bfloat16 or wider, within the bound.
No kernel may reach another device: no remote copies, remote signals or barrier semaphores. Data moves between devices by JAX's collectives and lax.ppermute only.
A program may use at most 64 MiB of HBM per device.

v0:
```python
import jax
import jax.numpy as jnp
from jax import lax
from jax.sharding import Mesh
from jax.sharding import PartitionSpec as P

KEYS_DEV = 512
GROUPS_DEV = 32
DELTA_DEV = 1024
KEYS = ("keys_0", "keys_1", "keys_2")
KEYS_VIEW = ("keys_0", "keys_1", "keys_2", "view")


def sent_to_all(shard, axis):
    size = lax.axis_size(axis)
    return lax.all_to_all(
        jnp.broadcast_to(shard[None], (size, *shard.shape)), axis, 0, 0, tiled=True
    )


def of_everyone(shard, axis):
    return sent_to_all(shard, axis).sum(axis=0)


def together(arrays, axis):
    vector, at, gathered = (jnp.concatenate([a.reshape(-1) for a in arrays]), 0, [])
    so_far = of_everyone(vector, axis)
    for a in arrays:
        gathered.append(so_far[at : at + a.size].reshape(a.shape))
        at += a.size
    return tuple(gathered)


def own_block(blocks, axes, order):
    inside = blocks.shape[1:]
    blocks = blocks.reshape(*(lax.axis_size(a) for a in axes), *inside)
    blocks = jnp.moveaxis(blocks, order, range(len(axes))).reshape(-1, *inside)
    for k in order:
        blocks = lax.psum_scatter(blocks, axes[k], scatter_dimension=0, tiled=True)
    return blocks[0]


def in_blocks(shard, dim, size):
    dims = shard.shape
    blocks = shard.reshape(*dims[:dim], size, dims[dim] // size, *dims[dim + 1 :])
    return jnp.moveaxis(blocks, dim, 0)


def sum_by_axis(shard, axes, order, dim):
    size = lax.axis_size(axes)
    return own_block(in_blocks(shard, dim, size), axes, order)


def pack_rows(key_slot, row_keys, row_mult, row_count, payload, extra_columns, owners):
    capacity = 2 * DELTA_DEV // owners
    alive_rows = jnp.arange(DELTA_DEV, dtype=jnp.int32) < row_count[0]
    slots = jnp.take(key_slot, row_keys)
    target = slots // KEYS_DEV
    marks = (target[:, None] == jnp.arange(owners, dtype=jnp.int32)[None, :]).astype(
        jnp.int32
    ) * alive_rows[:, None].astype(jnp.int32)
    before = jnp.cumsum(marks, axis=0) - marks
    slot_rank = jnp.take_along_axis(before, target[:, None], axis=1)[:, 0]
    position = jnp.where(alive_rows, target * capacity + slot_rank, owners * capacity)
    columns = jnp.stack(
        [slots % KEYS_DEV, row_mult * alive_rows.astype(jnp.int32)] + extra_columns, axis=1
    )
    sent_payload = (
        jnp.zeros((owners * capacity + 1, payload.shape[1]), payload.dtype)
        .at[position]
        .set(payload)
    )
    sent_columns = (
        jnp.zeros((owners * capacity + 1, columns.shape[1]), jnp.int32).at[position].set(columns)
    )
    return (
        sent_payload[:-1].reshape(owners, capacity, payload.shape[1]),
        sent_columns[:-1].reshape(owners, capacity, columns.shape[1]),
    )


def shards(
    key_slot,
    a_slot,
    a_group,
    a_weight,
    a_payload,
    b_slot,
    b_weight,
    b_payload,
    da_key,
    da_group,
    da_mult,
    da_payload,
    da_count,
    db_key,
    db_mult,
    db_payload,
    db_count,
):
    owners = lax.axis_size(KEYS)
    width = a_payload.shape[1]
    a_sent, a_columns = pack_rows(
        key_slot, da_key, da_mult, da_count, da_payload, [da_group], owners
    )
    a_payload_in, a_columns_in = (
        lax.all_to_all(a_sent, KEYS, split_axis=0, concat_axis=0, tiled=True),
        lax.all_to_all(a_columns, KEYS, split_axis=0, concat_axis=0, tiled=True),
    )
    weighted_b = b_weight[:, None].astype(jnp.float32) * b_payload.astype(jnp.float32)
    local_b = jax.ops.segment_sum(weighted_b, b_slot, num_segments=KEYS_DEV)
    b_sent, b_columns = pack_rows(key_slot, db_key, db_mult, db_count, db_payload, [], owners)
    b_payload_in, b_columns_in = (
        lax.all_to_all(b_sent, KEYS, split_axis=0, concat_axis=0, tiled=True),
        lax.all_to_all(b_columns, KEYS, split_axis=0, concat_axis=0, tiled=True),
    )
    flat_columns = b_columns_in.reshape(-1, 2)
    terms = flat_columns[:, 1:2].astype(jnp.float32) * b_payload_in.reshape(-1, width).astype(
        jnp.float32
    )
    local_db = jax.ops.segment_sum(terms, flat_columns[:, 0], num_segments=KEYS_DEV)
    total_b, total_db = together((local_b, local_db), "view")
    whole_table = total_b + total_db
    a_terms = (
        a_weight[:, None].astype(jnp.float32)
        * a_payload.astype(jnp.float32)
        * jnp.take(total_db, a_slot, axis=0)
    ).astype(jnp.bfloat16)
    delta_columns = a_columns_in.reshape(-1, 3)
    delta_terms = (
        delta_columns[:, 1:2].astype(jnp.float32)
        * a_payload_in.reshape(-1, width).astype(jnp.float32)
        * jnp.take(whole_table, delta_columns[:, 0], axis=0)
    ).astype(jnp.bfloat16)
    all_terms = jnp.concatenate([a_terms, delta_terms], axis=0)
    all_groups = jnp.concatenate([a_group, delta_columns[:, 2]])
    row_total = GROUPS_DEV * lax.axis_size(KEYS_VIEW)
    shifted = all_groups - jnp.int32(0)
    inside = (shifted >= 0) & (shifted < row_total)
    segment_index = jnp.where(inside, shifted, row_total)
    summed = jax.ops.segment_sum(
        all_terms.astype(jnp.float32), segment_index, num_segments=row_total + 1
    )
    return sum_by_axis(summed[:row_total], KEYS_VIEW, (2, 0, 1, 3), 0)


def solution(mesh):
    split = Mesh(
        mesh.devices.reshape(4, 4, 2, mesh.shape["view"]), ("keys_0", "keys_1", "keys_2", "view")
    )
    placed = (
        P(),
        P(KEYS_VIEW),
        P(KEYS_VIEW),
        P(KEYS_VIEW),
        P(KEYS_VIEW, None),
        P(KEYS_VIEW),
        P(KEYS_VIEW),
        P(KEYS_VIEW, None),
        P(KEYS_VIEW),
        P(KEYS_VIEW),
        P(KEYS_VIEW),
        P(KEYS_VIEW, None),
        P(KEYS_VIEW),
        P(KEYS_VIEW),
        P(KEYS_VIEW),
        P(KEYS_VIEW, None),
        P(KEYS_VIEW),
    )
    return jax.shard_map(
        shards, mesh=split, in_specs=placed, out_specs=P(KEYS_VIEW, None), check_vma=False
    )
```

profile of v0, /device:TPU:0, one launch (start us, length us, event | category | flops | bytes accessed | tf_op | source)
XLA Modules:
  0.0 392.7 jit_solution(4001793434923842289)
XLA Ops:
  7.4 6.1 %gather_fusion.4 = s32[1024]{0:T(1024)S(1)} fusion(s32[16384]{0:T(1024)S(1)} %copy-done, s32[1024]{0:T(1024)S(1)} %fusion.48), kind=kCustom, calls=%fused_computation.2.clone | custom fusion | bytes 12288 | tf_op jit(solution)/shard_map/jit(_take)/gather | solution.py:57
  14.2 9.0 %reduce-window.16 = s32[32,8,128]{2,1,0:T(8,128)S(1)} reduce-window(s32[32,8,128]{2,1,0:T(8,128)S(1)} %fusion.27, s32[]{:T(128)} %constant.102.clone.1), window={size=1x1x128 pad=0_0x0_0x127_0}, to_apply=%region_4.7 | reduce-window | flops 4161536 | bytes 262148 | tf_op jit(solution)/shard_map/reduce-window.2
  23.7 6.2 %gather_fusion.2 = s32[1024]{0:T(1024)S(1)} fusion(s32[16384]{0:T(1024)S(1)} %copy-done, s32[1024]{0:T(1024)S(1)} %fusion.47), kind=kCustom, calls=%fused_computation.clone | custom fusion | bytes 12288 | tf_op jit(solution)/shard_map/jit(_take)/gather | solution.py:57
  30.1 8.6 %gather_fusion.5 = s32[1024]{0:T(1024)S(1)} fusion(s32[1024,32]{0,1:T(8,128)S(1)} %fusion.24, s32[1024]{0:T(1024)S(1)} %bitcast.84), kind=kCustom, calls=%fused_computation.3.clone | custom fusion | bytes 16384 | tf_op jit(solution)/shard_map/jit(take_along_axis)/gather | solution.py:63
  39.0 3.3 scatter_custom_fusion.2
  43.5 8.4 %all-to-all-start.1 = ((s32[32,1,128]{2,1,0:T(1,128)}), s32[32,1,128]{2,1,0:T(1,128)S(1)}, u32[]{:S(2)}, u32[]{:S(2)}) async-start(s32[32,1,128]{2,1,0:T(1,128)} %reshape.388), calls=%async_computation.1 | async-start | bytes 32768 | tf_op jit(solution)/shard_map/all_to_all | solution.py:115
  52.7 9.0 %reduce-window.14 = s32[32,8,128]{2,1,0:T(8,128)S(1)} reduce-window(s32[32,8,128]{2,1,0:T(8,128)S(1)} %fusion.26, s32[]{:T(128)} %constant.102.clone.1), window={size=1x1x128 pad=0_0x0_0x127_0}, to_apply=%region_0.0 | reduce-window | flops 4161536 | bytes 262148 | tf_op jit(solution)/shard_map/reduce-window
  62.2 5.6 %scatter_custom_fusion.3 = bf16[2049,256]{1,0:T(8,128)(2,1)S(1)} fusion(s32[1024]{0:T(1024)S(1)} %get-tuple-element.23, bf16[1024,256]{1,0:T(8,128)(2,1)} %param.36, bf16[]{:T(256)} %constant.113.clone.1), kind=kCustom, calls=%fused_computation.33 | custom fusion | bytes 1049600 | tf_op jit(solution)/shard_map/scatter | solution.py:71
  68.9 7.4 %all-to-all-start.2 = ((bf16[32,64,256]{2,1,0:T(8,128)(2,1)}), bf16[32,64,256]{2,1,0:T(8,128)(2,1)S(1)}, u32[]{:S(2)}, u32[]{:S(2)}) async-start(bf16[32,64,256]{2,1,0:T(8,128)(2,1)} %bitcast.31), calls=%async_computation.2 | async-start | bytes 2097152 | tf_op jit(solution)/shard_map/all_to_all | solution.py:114
  76.3 25.2 %scatter_custom_fusion.1 = f32[512,256]{1,0:T(8,128)S(1)} fusion(s32[4096]{0:T(1024)} %param.26, bf16[4096,256]{1,0:T(8,128)(2,1)} %param.28, f32[4096]{0:T(1024)S(1)} %convert_element_type.71, f32[]{:T(128)} %constant.101.clone.1), kind=kCustom, calls=%fused_computation.16 | custom fusion | flops 3145728 | bytes 2638336 | tf_op jit(solution)/shard_map/scatter-add | solution.py:111
  102.6 8.6 %gather_fusion.3 = s32[1024]{0:T(1024)S(1)} fusion(s32[1024,32]{0,1:T(8,128)S(1)} %fusion.25, s32[1024]{0:T(1024)S(1)} %bitcast.83), kind=kCustom, calls=%fused_computation.1.clone | custom fusion | bytes 16384 | tf_op jit(solution)/shard_map/jit(take_along_axis)/gather | solution.py:63
  111.6 3.3 scatter_custom_fusion
  117.5 7.4 %all-to-all-start = ((s32[32,1,192]{2,1,0:T(1,128)}), s32[32,1,192]{2,1,0:T(1,128)S(1)}, u32[]{:S(2)}, u32[]{:S(2)}) async-start(s32[32,1,192]{2,1,0:T(1,128)} %reshape.386), calls=%async_computation | async-start | bytes 65536 | tf_op jit(solution)/shard_map/all_to_all | solution.py:108
  124.9 13.7 %scatter_custom_fusion.4 = f32[512,256]{1,0:T(8,128)S(1)} fusion(s32[2048]{0:T(1024)S(1)} %bitcast.121, bf16[2048,256]{1,0:T(8,128)(2,1)S(1)} %bitcast.87, f32[2048]{0:T(1024)S(1)} %bitcast.107, f32[]{:T(128)} %constant.101.clone.1), kind=kCustom, calls=%fused_computation.27 | custom fusion | flops 1572864 | bytes 1581060 | tf_op jit(solution)/shard_map/scatter-add | solution.py:121
  140.1 4.6 %broadcast_in_dim.89 = f32[4,1,262144]{2,1,0:T(1,128)} broadcast(f32[262144]{0:T(1024)S(1)} %pad_maximum_fusion), dimensions={2} | broadcast | bytes 5242880 | tf_op jit(solution)/shard_map/broadcast_in_dim | solution.py:17
  144.7 5.0 %all-to-all-start.3 = ((f32[4,1,262144]{2,1,0:T(1,128)}), f32[4,1,262144]{2,1,0:T(1,128)}, u32[]{:S(2)}, u32[]{:S(2)}) async-start(f32[4,1,262144]{2,1,0:T(1,128)} %broadcast_in_dim.89), calls=%async_computation.3 | async-start | bytes 8388608 | tf_op jit(solution)/shard_map/all_to_all | solution.py:16
  149.7 5.6 %scatter_custom_fusion.5 = bf16[2049,256]{1,0:T(8,128)(2,1)S(1)} fusion(s32[1024]{0:T(1024)S(1)} %get-tuple-element.21, bf16[1024,256]{1,0:T(8,128)(2,1)} %param.32, bf16[]{:T(256)} %constant.113.clone.1), kind=kCustom, calls=%fused_computation.31 | custom fusion | bytes 1049600 | tf_op jit(solution)/shard_map/scatter | solution.py:71
  155.4 1.1 slice.118
  157.6 41.8 %all-to-all-done.3 = f32[4,1,262144]{2,1,0:T(1,128)} async-done(((f32[4,1,262144]{2,1,0:T(1,128)}), f32[4,1,262144]{2,1,0:T(1,128)}, u32[]{:S(2)}, u32[]{:S(2)}) %all-to-all-start.3) | async-done | bytes 4194336 | tf_op jit(solution)/shard_map/all_to_all | solution.py:16
  199.4 7.1 %all-to-all-start.4 = ((bf16[32,64,256]{2,1,0:T(8,128)(2,1)}), bf16[32,64,256]{2,1,0:T(8,128)(2,1)}, u32[]{:S(2)}, u32[]{:S(2)}) async-start(bf16[32,64,256]{2,1,0:T(8,128)(2,1)} %bitcast.34), calls=%async_computation.4 | async-start | bytes 2097152 | tf_op jit(solution)/shard_map/all_to_all | solution.py:107
  206.7 9.8 %reduce_sum.9 = f32[262144]{0:T(1024)S(1)} reduce(f32[4,1,262144]{2,1,0:T(1,128)} %all-to-all-done.3, f32[]{:T(128)} %constant.101.clone.1), dimensions={0,1}, to_apply=%region_9.12 | reduce | flops 786432 | bytes 5242884 | tf_op jit(solution)/shard_map/reduce_sum | solution.py:22
  216.9 16.1 %gather_fusion = f32[4096,256]{1,0:T(8,128)} fusion(f32[512,256]{1,0:T(8,128)S(1)} %slice.79, s32[4096]{0:T(1024)S(1)} %fusion.28), kind=kCustom, calls=%fused_computation.4 | custom fusion | bytes 8404992 | tf_op jit(solution)/shard_map/jit(_take)/gather | solution.py:127
  233.1 6.6 %gather_fusion.1 = f32[2048,256]{1,0:T(8,128)S(1)} fusion(f32[512,256]{1,0:T(8,128)S(1)} %add.85, s32[2048]{0:T(1024)S(1)} %broadcast_clamp_fusion), kind=kCustom, calls=%fused_computation.5 | custom fusion | bytes 4202496 | tf_op jit(solution)/shard_map/jit(_take)/gather | solution.py:133
  239.7 5.9 %multiply_convert_fusion = bf16[4096,256]{1,0:T(8,128)(2,1)} fusion(f32[4096,256]{1,0:T(8,128)} %gather_fusion, bf16[4096,256]{1,0:T(8,128)(2,1)} %param.25, f32[4096]{0:T(1024)S(1)} %convert_element_type.69, pred[4096]{0:T(1024)(128)(4,1)S(1)} %compare_and_fusion), kind=kLoop, calls=%fused_computation.15 | loop fusion | flops 5242880 | bytes 8409088 | tf_op jit(solution)/shard_map/convert_element_type | solution.py:128
  245.6 1.8 fusion.10
  247.4 40.1 %scatter_custom_fusion.6 = f32[4097,256]{1,0:T(8,128)} fusion(s32[6144]{0:T(1024)S(1)} %bitcast.109, bf16[2048,256]{1,0:T(8,128)(2,1)S(1)} %fusion.10, bf16[]{:T(256)} %constant.156, bf16[4096,256]{1,0:T(8,128)(2,1)} %multiply_convert_fusion, f32[]{:T(128)} %constant.101.clone.1), kind=kCustom, calls=%fused_computation.13 | custom fusion | flops 7864320 | bytes 7341062 | tf_op jit(solution)/shard_map/scatter-add | solution.py:141
  287.4 2.2 slice-done
  289.6 2.2 copy.74
  291.9 14.3 %reduce-scatter.5.cloned.1.call-done = f32[64,32,256]{2,1,0:T(8,128)} async-done(((f32[128,32,256]{2,1,0:T(8,128)}), f32[64,32,256]{2,1,0:T(8,128)}) %reduce-scatter.5.cloned.1.call-update) | async-done | bytes 2097168 | tf_op jit(solution)/shard_map/reduce_scatter | solution.py:39
  306.4 33.5 %reduce-scatter.7.cloned.1.call-done = f32[16,32,256]{2,1,0:T(8,128)} async-done(((f32[64,32,256]{2,1,0:T(8,128)}), f32[16,32,256]{2,1,0:T(8,128)}) %reduce-scatter.7.cloned.1.call-update) | async-done | bytes 524304 | tf_op jit(solution)/shard_map/reduce_scatter | solution.py:39
  339.9 23.9 %reduce-scatter.9.cloned.1.call-done = f32[4,32,256]{2,1,0:T(8,128)} async-done(((f32[16,32,256]{2,1,0:T(8,128)}), f32[4,32,256]{2,1,0:T(8,128)}) %reduce-scatter.9.cloned.1.call-update) | async-done | bytes 131088 | tf_op jit(solution)/shard_map/reduce_scatter | solution.py:39
  363.8 22.4 %reduce-scatter.11.cloned.1.call-done = f32[1,32,256]{2,1,0:T(8,128)} async-done(((f32[4,32,256]{2,1,0:T(8,128)}), f32[1,32,256]{2,1,0:T(8,128)}) %reduce-scatter.11.cloned.1.call-update) | async-done | bytes 32784 | tf_op jit(solution)/shard_map/reduce_scatter | solution.py:39
  (103 shorter events, 11.7 us)
Async XLA Ops:
  6.5 0.8 copy-start
  7.4 6.2 %copy-start.5 = (s32[1024]{0:T(1024)S(1)}, s32[1024]{0:T(1024)}, u32[]{:S(2)}) copy-start(s32[1024]{0:T(1024)} %param.34) | copy-start | bytes 12292
  7.4 16.3 %copy-start.6 = (s32[1024]{0:T(1024)S(1)}, s32[1024]{0:T(1024)}, u32[]{:S(2)}) copy-start(s32[1024]{0:T(1024)} %param.29) | copy-start | bytes 12292
  30.1 8.7 %copy-start.8 = (s32[1024]{0:T(1024)S(1)}, s32[1024]{0:T(1024)}, u32[]{:S(2)}) copy-start(s32[1024]{0:T(1024)} %param.35) | copy-start | bytes 12292
  43.5 25.4 %all-to-all-start.1 = ((s32[32,1,128]{2,1,0:T(1,128)}), s32[32,1,128]{2,1,0:T(1,128)S(1)}, u32[]{:S(2)}, u32[]{:S(2)}) async-start(s32[32,1,128]{2,1,0:T(1,128)} %reshape.388), calls=%async_computation.1 | async-start | bytes 32768 | tf_op jit(solution)/shard_map/all_to_all | solution.py:115
  67.8 8.5 %copy-start.3 = (s32[4096]{0:T(1024)S(1)}, s32[4096]{0:T(1024)}, u32[]{:S(2)}) copy-start(s32[4096]{0:T(1024)} %param.27) | copy-start | bytes 49156
  68.9 48.6 %all-to-all-start.2 = ((bf16[32,64,256]{2,1,0:T(8,128)(2,1)}), bf16[32,64,256]{2,1,0:T(8,128)(2,1)S(1)}, u32[]{:S(2)}, u32[]{:S(2)}) async-start(bf16[32,64,256]{2,1,0:T(8,128)(2,1)} %bitcast.31), calls=%async_computation.2 | async-start | bytes 2097152 | tf_op jit(solution)/shard_map/all_to_all | solution.py:114
  102.6 8.7 %copy-start.9 = (s32[1024]{0:T(1024)S(1)}, s32[1024]{0:T(1024)}, u32[]{:S(2)}) copy-start(s32[1024]{0:T(1024)} %param.31) | copy-start | bytes 12292
  102.6 8.7 %copy-start.7 = (s32[1024]{0:T(1024)S(1)}, s32[1024]{0:T(1024)}, u32[]{:S(2)}) copy-start(s32[1024]{0:T(1024)} %param.30) | copy-start | bytes 12292
  117.5 22.5 %all-to-all-start = ((s32[32,1,192]{2,1,0:T(1,128)}), s32[32,1,192]{2,1,0:T(1,128)S(1)}, u32[]{:S(2)}, u32[]{:S(2)}) async-start(s32[32,1,192]{2,1,0:T(1,128)} %reshape.386), calls=%async_computation | async-start | bytes 65536 | tf_op jit(solution)/shard_map/all_to_all | solution.py:108
  144.7 5.0 %copy-start.4 = (s32[4096]{0:T(1024)S(1)}, s32[4096]{0:T(1024)}, u32[]{:S(2)}) copy-start(s32[4096]{0:T(1024)} %param.24) | copy-start | bytes 49156
  144.7 54.7 %all-to-all-start.3 = ((f32[4,1,262144]{2,1,0:T(1,128)}), f32[4,1,262144]{2,1,0:T(1,128)}, u32[]{:S(2)}, u32[]{:S(2)}) async-start(f32[4,1,262144]{2,1,0:T(1,128)} %broadcast_in_dim.89), calls=%async_computation.3 | async-start | bytes 8388608 | tf_op jit(solution)/shard_map/all_to_all | solution.py:16
  149.7 6.8 %copy-start.1 = (s32[4096]{0:T(1024)S(1)}, s32[4096]{0:T(1024)}, u32[]{:S(2)}) copy-start(s32[4096]{0:T(1024)} %param.22) | copy-start | bytes 49156
  149.7 7.8 %copy-start.2 = (s32[4096]{0:T(1024)S(1)}, s32[4096]{0:T(1024)}, u32[]{:S(2)}) copy-start(s32[4096]{0:T(1024)} %param.23) | copy-start | bytes 49156
  199.4 46.3 %all-to-all-start.4 = ((bf16[32,64,256]{2,1,0:T(8,128)(2,1)}), bf16[32,64,256]{2,1,0:T(8,128)(2,1)}, u32[]{:S(2)}, u32[]{:S(2)}) async-start(bf16[32,64,256]{2,1,0:T(8,128)(2,1)} %bitcast.34), calls=%async_computation.4 | async-start | bytes 2097152 | tf_op jit(solution)/shard_map/all_to_all | solution.py:107
  206.5 99.8 %reduce-scatter.5.cloned.1.call-start = ((), (), s32[]{:S(2)}) async-start(), calls=%async_computation.9 | async-start | bytes 6291456 | tf_op jit(solution)/shard_map/reduce_scatter | solution.py:39
  287.4 2.2 slice-start
  291.9 47.9 %reduce-scatter.7.cloned.1.call-start = ((), (), s32[]{:S(2)}) async-start(), calls=%async_computation.10 | async-start | bytes 2621440 | tf_op jit(solution)/shard_map/reduce_scatter | solution.py:39
  306.3 57.5 %reduce-scatter.9.cloned.1.call-start = ((), (), s32[]{:S(2)}) async-start(), calls=%async_computation.11 | async-start | bytes 655360 | tf_op jit(solution)/shard_map/reduce_scatter | solution.py:39
  339.8 46.4 %reduce-scatter.11.cloned.1.call-start = ((), (), s32[]{:S(2)}) async-start(), calls=%async_computation.12 | async-start | bytes 163840 | tf_op jit(solution)/shard_map/reduce_scatter | solution.py:39
Sparse Core Ops, SparseCore 0:
  292.0 14.2 reduce-scatter.4
  308.7 31.0 reduce-scatter.6
  342.2 21.5 reduce-scatter.8
  366.0 20.1 reduce-scatter.10
where the time goes:
time: 394 us; the launch traced here: 393 us
  waiting for transfers between devices  136 us (35%)
  other arithmetic  118 us (30%)
  local copies, waits for them, and re-layouts  87.7 us (22%)
  starting transfers between devices  35.7 us (9%)
  between operations  15.1 us (4%)
    reduce_scatter x4, waiting for transfers between devices, own_block(): blocks = lax.psum_scatter(blocks, axes[k], scatter_dimension=0, tiled=True)  94.1 us
    all_to_all x1, waiting for transfers between devices, sent_to_all(): lax.all_to_all(jnp.broadcast_to(shard[None], (size, *shard.shape)), axis,...  41.8 us
    scatter-add x1, other arithmetic, shards(): jax.ops.segment_sum(all_terms.astype(jnp.float32), segment_index, num_seg...  40.1 us
    scatter-add x1, other arithmetic, shards(): local_b = jax.ops.segment_sum(weighted_b, b_slot, num_segments=KEYS_DEV)  25.2 us
    another operation x6, other arithmetic  18.3 us
    gather x2, local copies, waits for them, and re-layouts, pack_rows(): slot_rank = jnp.take_along_axis(before, target[:, None], axis=1)[:, 0]  17.3 us
    gather x1, local copies, waits for them, and re-layouts, shards(): jnp.take(total_db, a_slot, axis=0)  16.1 us
    scatter-add x1, other arithmetic, shards(): jax.ops.segment_sum(terms, flat_columns[:, 0], num_segments=KEYS_DEV)  13.7 us
  transfers between devices with their start and end apart: 9, of which 5 were waited for; matrix products, arithmetic and copies ran while one was open for 30% of the time, Pallas kernels for 0%

commit v1 on v0

v1 whole, which is shorter than its diff:
```python
import jax
import jax.numpy as jnp
from jax import lax
from jax.experimental import pallas as pl
from jax.experimental.pallas import tpu as pltpu
from jax.sharding import Mesh
from jax.sharding import PartitionSpec as P

KEYS_DEV = 512
GROUPS_DEV = 32
GROUPS = 4096
DELTA_DEV = 1024
A_DEV = 4096
D = 256
OWNERS = 32
CAP = 64
BLOCK = CAP + 8
KEYS = ("keys_0", "keys_1", "keys_2")
KEYS_VIEW = ("keys_0", "keys_1", "keys_2", "view")
F32, BF16, I32 = jnp.float32, jnp.bfloat16, jnp.int32
NN = (((1,), (0,)), ((), ()))
NT = (((1,), (1,)), ((), ()))
TN = (((0,), (0,)), ((), ()))
VMEM = pl.BlockSpec(memory_space=pltpu.VMEM)
SMEM = pl.BlockSpec(memory_space=pltpu.SMEM)


def dot(x, y, dims=NN):
    return lax.dot_general(x, y, dims, preferred_element_type=F32)


def rows_of(shape):
    return lax.broadcasted_iota(I32, shape, 0)


def lanes_of(shape):
    return lax.broadcasted_iota(I32, shape, 1)


def flat(x):
    return jnp.concatenate([x[j : j + 1, :] for j in range(x.shape[0])], axis=1)


def pick(condition, value):
    return jnp.where(condition, value, 0.0).astype(BF16)


def pack_kernel(with_group, me_ref, count_ref, table_ref, key_ref, mult_ref, *rest):
    group_ref = rest[0] if with_group else None
    payload_ref, out_ref = rest[-2:]
    rows = DELTA_DEV
    key = flat(key_ref[...])
    key_hi, key_lo = key >> 7, key & 127
    low = pick(rows_of((128, rows)) == key_lo, 1.0)
    table = table_ref[...]
    found = dot((table >> 7).astype(F32).astype(BF16), low) * 128.0 + dot(
        (table & 127).astype(F32).astype(BF16), low
    )
    slot = jnp.sum(jnp.where(rows_of((128, rows)) == key_hi, found, 0.0), axis=0, keepdims=True)
    slot = slot.astype(I32)
    owner, local = slot >> 9, slot & 511
    live = lanes_of((1, rows)) < count_ref[0]
    owner = jnp.where(live, owner, -1)
    marks = jnp.where(rows_of((OWNERS, rows)) == owner, 1.0, 0.0)
    step = jnp.where(
        (rows_of((128, 256)) < lanes_of((128, 256))) | (lanes_of((128, 256)) >= 128), 1.0, 0.0
    ).astype(BF16)
    before, carry = [], jnp.zeros((OWNERS, 128), F32)
    for j in range(rows // 128):
        counted = dot(marks[:, 128 * j : 128 * (j + 1)].astype(BF16), step)
        before.append(counted[:, :128] + carry)
        carry = carry + counted[:, 128:]
    rank = jnp.sum(marks * jnp.concatenate(before, axis=1), axis=0, keepdims=True).astype(I32)
    position = jnp.where(live, owner * CAP + rank, -1)
    sign = flat(mult_ref[...]).astype(F32)
    payload = payload_ref[...]
    for c in range(OWNERS // 4):
        chosen = pick(rows_of((4 * CAP, rows)) + 4 * CAP * c == position, sign)
        packed = dot(chosen, payload).astype(BF16)
        for j in range(4):
            out_ref[pl.ds((4 * c + j) * BLOCK, CAP), :] = packed[CAP * j : CAP * (j + 1)]
    field = rows_of((8, rows))
    value = jnp.where(field == 0, local & 255, jnp.where(field == 1, local >> 8, 0))
    if with_group:
        group = flat(group_ref[...])
        value = jnp.where(field == 2, group & 255, jnp.where(field == 3, group >> 8, value))
    value = jnp.broadcast_to(value.astype(F32)[None], (OWNERS, 8, rows)).reshape(8 * OWNERS, rows)
    sent = pick((rows_of((8 * OWNERS, rows)) >> 3) == owner, value)
    place = pick(rows_of((4 * CAP, rows)) == rank + CAP * (me_ref[0] % 4), 1.0)
    fields = dot(sent, place, NT).astype(BF16)
    for k in range(OWNERS):
        out_ref[pl.ds(k * BLOCK + CAP, 8), :] = fields[8 * k : 8 * k + 8]


def pack(me, count, table, key, mult, group, payload):
    extra = [] if group is None else [group.reshape(8, 128)]
    return pl.pallas_call(
        lambda *refs: pack_kernel(group is not None, *refs),
        out_shape=jax.ShapeDtypeStruct((OWNERS * BLOCK, D), BF16),
        in_specs=[SMEM, SMEM] + [VMEM] * (4 + len(extra)),
        out_specs=VMEM,
        name="pack_a" if extra else "pack_b",
    )(me, count, table, key.reshape(8, 128), mult.reshape(8, 128), *extra, payload)


def fields_of(ref, c):
    total = ref[pl.ds(4 * c * BLOCK + CAP, 8), :].astype(F32)
    for j in range(1, 4):
        total = total + ref[pl.ds((4 * c + j) * BLOCK + CAP, 8), :].astype(F32)
    total = total.astype(I32)
    return total[0:1] + 256 * total[1:2], total[2:3] + 256 * total[3:4]


def payload_of(ref, c):
    return jnp.concatenate(
        [ref[pl.ds((4 * c + j) * BLOCK, CAP), :] for j in range(4)], axis=0
    )


def spread(total_ref, view, outs):
    for s in range(4):
        outs[s][...] = total_ref[pl.ds(((view + s) % 4) * 128, 128), :]


def sum_b_kernel(view_ref, slot_ref, weight_ref, payload_ref, *rest):
    outs, total_ref = rest[:4], rest[4]
    total_ref[...] = jnp.zeros_like(total_ref)
    for c in range(4):
        slot = flat(slot_ref[8 * c : 8 * c + 8, :])
        weight = flat(weight_ref[8 * c : 8 * c + 8, :]).astype(F32)
        chosen = pick(rows_of((KEYS_DEV, 1024)) == slot, weight)
        total_ref[...] += dot(chosen, payload_ref[1024 * c : 1024 * (c + 1), :])
    spread(total_ref, view_ref[0], outs)


def sum_db_kernel(view_ref, in_ref, *rest):
    outs, total_ref = rest[:4], rest[4]
    total_ref[...] = jnp.zeros_like(total_ref)
    for c in range(8):
        slot, _ = fields_of(in_ref, c)
        chosen = pick(rows_of((KEYS_DEV, 256)) == slot, 1.0)
        total_ref[...] += dot(chosen, payload_of(in_ref, c))
    spread(total_ref, view_ref[0], outs)


def slices(kernel, name, view, *args):
    return pl.pallas_call(
        kernel,
        out_shape=[jax.ShapeDtypeStruct((128, D), F32)] * 4,
        in_specs=[SMEM] + [VMEM] * len(args),
        out_specs=[VMEM] * 4,
        scratch_shapes=[pltpu.VMEM((KEYS_DEV, D), F32)],
        name=name,
    )(view, *args)


def shift(x, s):
    return lax.ppermute(x, "view", [(j, (j + s) % 4) for j in range(4)])


def own_total(parts):
    got = [parts[0]] + [shift(parts[s], s) for s in (1, 2, 3)]
    return (got[0] + got[1]) + (got[2] + got[3])


def everyone(x):
    return [x] + [shift(x, s) for s in (1, 2, 3)]


def join_kernel(view_ref, *refs):
    db, b = refs[:4], refs[4:8]
    slot_ref, group_ref, weight_ref, payload_ref, in_ref = refs[8:13]
    out_ref, table_ref, whole_ref, term_ref, groups_ref = refs[13:]
    view = view_ref[0]
    for s in range(4):
        at = pl.ds(((view + 4 - s) % 4) * 128, 128)
        table = db[s][...]
        whole = b[s][...] + table
        for ref, value in ((table_ref, table), (whole_ref, whole)):
            high = value.astype(BF16)
            ref[at, :D] = high
            ref[at, D:] = (value - high.astype(F32)).astype(BF16)

    def terms(ref, slot, weight, payload):
        chosen = pick(rows_of((KEYS_DEV, 256)) == slot, weight)
        got = dot(chosen, ref[...], TN)
        return (payload.astype(F32) * (got[:, :D] + got[:, D:])).astype(BF16)

    for c in range(16):
        slot = flat(slot_ref[2 * c : 2 * c + 2, :])
        weight = flat(weight_ref[2 * c : 2 * c + 2, :]).astype(F32)
        at = pl.ds(256 * c, 256)
        term_ref[at, :] = terms(table_ref, slot, weight, payload_ref[at, :])
        groups_ref[:, at] = flat(group_ref[2 * c : 2 * c + 2, :])
    for c in range(8):
        slot, group = fields_of(in_ref, c)
        at = pl.ds(A_DEV + 256 * c, 256)
        term_ref[at, :] = terms(whole_ref, slot, 1.0, payload_of(in_ref, c))
        groups_ref[:, at] = group

    def block(g, carry):
        rows = groups_ref.shape[1]
        chosen = pick(rows_of((256, rows)) + 256 * g == groups_ref[...], 1.0)
        out_ref[pl.ds(256 * g, 256), :] = dot(chosen, term_ref[...]).astype(BF16)
        return carry

    lax.fori_loop(0, GROUPS // 256, block, 0)


def join(view, db, b, slot, group, weight, payload, received):
    rows = A_DEV + OWNERS * CAP
    return pl.pallas_call(
        join_kernel,
        out_shape=jax.ShapeDtypeStruct((GROUPS, D), BF16),
        in_specs=[SMEM] + [VMEM] * 13,
        out_specs=VMEM,
        scratch_shapes=[
            pltpu.VMEM((KEYS_DEV, 2 * D), BF16),
            pltpu.VMEM((KEYS_DEV, 2 * D), BF16),
            pltpu.VMEM((rows, D), BF16),
            pltpu.VMEM((1, rows), I32),
        ],
        name="join",
    )(
        view, *db, *b, slot.reshape(32, 128), group.reshape(32, 128), weight.reshape(32, 128),
        payload, received,
    )


def exchange(packed):
    blocks = packed.reshape(OWNERS, BLOCK, D)
    return lax.all_to_all(blocks, KEYS, 0, 0, tiled=True).reshape(OWNERS * BLOCK, D)


def shards(
    key_slot,
    a_slot,
    a_group,
    a_weight,
    a_payload,
    b_slot,
    b_weight,
    b_payload,
    da_key,
    da_group,
    da_mult,
    da_payload,
    da_count,
    db_key,
    db_mult,
    db_payload,
    db_count,
):
    me = lax.axis_index(KEYS).astype(I32).reshape(1)
    view = lax.axis_index("view").astype(I32).reshape(1)
    table = key_slot.reshape(128, 128)
    db_in = exchange(pack(me, db_count, table, db_key, db_mult, None, db_payload))
    da_in = exchange(pack(me, da_count, table, da_key, da_mult, da_group, da_payload))
    b_parts = slices(
        sum_b_kernel, "sum_b", view, b_slot.reshape(32, 128), b_weight.reshape(32, 128), b_payload
    )
    b = everyone(own_total(b_parts))
    db = everyone(own_total(slices(sum_db_kernel, "sum_db", view, db_in)))
    partial = join(view, db, b, a_slot, a_group, a_weight, a_payload, da_in)
    blocks = partial.reshape(GROUPS // GROUPS_DEV, GROUPS_DEV, D)
    blocks = lax.all_to_all(blocks, KEYS_VIEW, 0, 0, tiled=True)
    return jnp.sum(blocks.astype(F32), axis=0)


def solution(mesh):
    split = Mesh(
        mesh.devices.reshape(4, 4, 2, mesh.shape["view"]), ("keys_0", "keys_1", "keys_2", "view")
    )
    one, two = P(KEYS_VIEW), P(KEYS_VIEW, None)
    placed = (
        P(), one, one, one, two, one, one, two, one, one, one, two, one, one, one, two, one,
    )
    return jax.shard_map(shards, mesh=split, in_specs=placed, out_specs=two, check_vma=False)
```

time: 394 us -> 134 us (0.34)
  other arithmetic: 118 us -> 2.86 us
  waiting for transfers between devices: 136 us -> 24.4 us
  local copies, waits for them, and re-layouts: 87.7 us -> 0.62 us
  blocking collectives: 0 us -> 38 us
  Pallas kernels: 0 us -> 37.5 us
  between operations: 15.1 us -> 1.41 us
  starting transfers between devices: 35.7 us -> 27.9 us
    reduce_scatter x4 -> x0, waiting for transfers between devices: 94.1 us -> none  [own_block(): blocks = lax.psum_scatter(blocks, axes[k], scatter_dimension=0, tiled=True)]
    scatter-add x3 -> x0, other arithmetic: 79 us -> none  [the longest x1 40.1 us: shards(): jax.ops.segment_sum(all_terms.astype(jnp.float32), segment_index, num_seg...]
    gather x6 -> x0, local copies, waits for them, and re-layouts: 52.3 us -> none  [the longest x2 17.3 us: pack_rows(): slot_rank = jnp.take_along_axis(before, target[:, None], axis=1)[:, 0]]
    all_to_all x0 -> x1, blocking collectives: none -> 38 us  [shards(): blocks = lax.all_to_all(blocks, KEYS_VIEW, 0, 0, tiled=True)]
    pallas_call x0 -> x5, Pallas kernels: none -> 37.5 us  [the longest x1 23 us: join(): pl.pallas_call(join_kernel, out_shape=jax.ShapeDtypeStruct((GROUPS, D), B...]
    all_to_all x5 -> x2, waiting for transfers between devices: 41.8 us -> 13.5 us  [exchange(): lax.all_to_all(blocks, KEYS, 0, 0, tiled=True).reshape(OWNERS * BLOCK, D)]
    all_to_all x5 -> x2, starting transfers between devices: 35.3 us -> 12.5 us  [exchange(): lax.all_to_all(blocks, KEYS, 0, 0, tiled=True).reshape(OWNERS * BLOCK, D)]
    another operation x8 -> x0, other arithmetic: 18.3 us -> none
  transfers between devices with their start and end apart: 9 -> 14, of which waited for: 5 -> 7; matrix products, arithmetic and copies ran while one was open for 30% -> 1% of each run, Pallas kernels for 0% -> 8%
where the time goes in v1:
time: 134 us; the launch traced here: 133 us
  blocking collectives  38 us (28%)
  Pallas kernels  37.5 us (28%)
  starting transfers between devices  27.9 us (21%)
  waiting for transfers between devices  24.4 us (18%)
  other arithmetic  2.86 us (2%)
  between operations  1.41 us (1%)
    all_to_all x1, blocking collectives, shards(): blocks = lax.all_to_all(blocks, KEYS_VIEW, 0, 0, tiled=True)  38 us
    pallas_call x1, Pallas kernels, join(): pl.pallas_call(join_kernel, out_shape=jax.ShapeDtypeStruct((GROUPS, D), B...  23 us
    ppermute x12, starting transfers between devices, shift(): return lax.ppermute(x, 'view', [(j, (j + s) % 4) for j in range(4)])  15.5 us
    all_to_all x2, waiting for transfers between devices, exchange(): lax.all_to_all(blocks, KEYS, 0, 0, tiled=True).reshape(OWNERS * BLOCK, D)  13.5 us
    all_to_all x2, starting transfers between devices, exchange(): lax.all_to_all(blocks, KEYS, 0, 0, tiled=True).reshape(OWNERS * BLOCK, D)  12.5 us
    ppermute x12, waiting for transfers between devices, shift(): return lax.ppermute(x, 'view', [(j, (j + s) % 4) for j in range(4)])  10.8 us
    pallas_call x2, Pallas kernels, pack(): pl.pallas_call(lambda *refs: pack_kernel(group is not None, *refs), out_s...  8.04 us
    pallas_call x2, Pallas kernels, slices(): pl.pallas_call(kernel, out_shape=[jax.ShapeDtypeStruct((128, D), F32)] *...  6.47 us
  transfers between devices with their start and end apart: 14, of which 7 were waited for; matrix products, arithmetic and copies ran while one was open for 1% of the time, Pallas kernels for 8%

profile of v1, /device:TPU:0, one launch (start us, length us, event | category | flops | bytes accessed | tf_op | source)
XLA Modules:
  0.0 132.7 jit_solution(13882825790331244349)
XLA Ops:
  0.7 4.0 %pack_b.1 = bf16[2304,256]{1,0:T(8,128)(2,1)} custom-call(s32[1]{0:T(128)} %bitcast.1.refs_0_, s32[1]{0:T(128)S(6)} %copy.19.refs_1_, s32[128,128]{1,0:T(8,128)} %bitcast.23, s32[8,128]{1,0:T(8,128)} %bitcast.30, s32[8,128]{1,0:T(8,128)} %bitcast.31, bf16[1024,256]{1,0:T(8,128)(2,1)} %refs_5_.1), custom_call_target="tpu_custom_call" | custom-call | tf_op jit(solution)/shard_map/pack_b/pallas_call | solution.py:97
  4.6 8.5 %all-to-all-start = ((bf16[32,72,256]{2,1,0:T(8,128)(2,1)}), bf16[32,72,256]{2,1,0:T(8,128)(2,1)S(1)}, u32[]{:S(2)}, u32[]{:S(2)}) async-start(bf16[32,72,256]{2,1,0:T(8,128)(2,1)} %bitcast.22), calls=%async_computation | async-start | bytes 2359296 | tf_op jit(solution)/shard_map/all_to_all | solution.py:232
  13.8 4.0 %pack_a.1 = bf16[2304,256]{1,0:T(8,128)(2,1)} custom-call(s32[1]{0:T(128)} %bitcast.1.refs_0_, s32[1]{0:T(128)S(6)} %copy.18.refs_1_, s32[128,128]{1,0:T(8,128)} %bitcast.24, s32[8,128]{1,0:T(8,128)} %bitcast.32, s32[8,128]{1,0:T(8,128)} %bitcast.33, s32[8,128]{1,0:T(8,128)} %bitcast.34, bf16[1024,256]{1,0:T(8,128)(2,1)} %refs_6_.1), custom_call_target="tpu_custom_call" | custom-call | tf_op jit(solution)/shard_map/pack_a/pallas_call | solution.py:97
  17.8 13.5 %all-to-all-done = bf16[32,72,256]{2,1,0:T(8,128)(2,1)S(1)} async-done(((bf16[32,72,256]{2,1,0:T(8,128)(2,1)}), bf16[32,72,256]{2,1,0:T(8,128)(2,1)S(1)}, u32[]{:S(2)}, u32[]{:S(2)}) %all-to-all-start) | async-done | bytes 1179680 | tf_op jit(solution)/shard_map/all_to_all | solution.py:232
  31.3 4.0 %all-to-all-start.1 = ((bf16[32,72,256]{2,1,0:T(8,128)(2,1)}), bf16[32,72,256]{2,1,0:T(8,128)(2,1)S(1)}, u32[]{:S(2)}, u32[]{:S(2)}) async-start(bf16[32,72,256]{2,1,0:T(8,128)(2,1)} %bitcast.20), calls=%async_computation.1 | async-start | bytes 2359296 | tf_op jit(solution)/shard_map/all_to_all | solution.py:232
  35.4 3.7 %sum_b.1 = (f32[128,256]{1,0:T(8,128)}, f32[128,256]{1,0:T(8,128)}, f32[128,256]{1,0:T(8,128)}, f32[128,256]{1,0:T(8,128)}) custom-call(s32[1]{0:T(128)} %bitcast.view_ref, s32[32,128]{1,0:T(8,128)} %bitcast.25, s32[32,128]{1,0:T(8,128)} %bitcast.26, bf16[4096,256]{1,0:T(8,128)(2,1)} %payload_ref.1), custom_call_target="tpu_custom_call" | custom-call | tf_op jit(solution)/shard_map/sum_b/pallas_call | solution.py:147
  39.0 1.5 %collective-permute-start.6 = (f32[128,256]{1,0:T(8,128)}, f32[128,256]{1,0:T(8,128)S(1)}, u32[]{:S(2)}, u32[]{:S(2)}) collective-permute-start(f32[128,256]{1,0:T(8,128)} %get-tuple-element.18), channel_id=1, source_target_pairs={{0,1},{1,2},{2,3},{3,0},{4,5},{5,6},{6,7},{7,4},{8,9},{9,10},{10,1... | collective-permute-start | bytes 393224 | tf_op jit(solution)/shard_map/ppermute | solution.py:158
  40.5 2.7 %collective-permute-start.7 = (f32[128,256]{1,0:T(8,128)}, f32[128,256]{1,0:T(8,128)S(1)}, u32[]{:S(2)}, u32[]{:S(2)}) collective-permute-start(f32[128,256]{1,0:T(8,128)} %get-tuple-element.19), channel_id=1, source_target_pairs={{0,2},{1,3},{2,0},{3,1},{4,6},{5,7},{6,4},{7,5},{8,10},{9,11},{10,... | collective-permute-start | bytes 393224 | tf_op jit(solution)/shard_map/ppermute | solution.py:158
  43.3 1.4 %collective-permute-start.8 = (f32[128,256]{1,0:T(8,128)}, f32[128,256]{1,0:T(8,128)S(1)}, u32[]{:S(2)}, u32[]{:S(2)}) collective-permute-start(f32[128,256]{1,0:T(8,128)} %get-tuple-element.20), channel_id=1, source_target_pairs={{0,3},{1,0},{2,1},{3,2},{4,7},{5,4},{6,5},{7,6},{8,11},{9,8},{10,9... | collective-permute-start | bytes 393224 | tf_op jit(solution)/shard_map/ppermute | solution.py:158
  44.7 2.8 %sum_db.1 = (f32[128,256]{1,0:T(8,128)}, f32[128,256]{1,0:T(8,128)}, f32[128,256]{1,0:T(8,128)}, f32[128,256]{1,0:T(8,128)}) custom-call(s32[1]{0:T(128)} %bitcast.view_ref, bf16[2304,256]{1,0:T(8,128)(2,1)} %bitcast.21), custom_call_target="tpu_custom_call" | custom-call | tf_op jit(solution)/shard_map/sum_db/pallas_call | solution.py:147
  47.5 0.6 collective-permute-start
  48.1 0.9 collective-permute-start.1
  49.0 1.8 %collective-permute-start.2 = (f32[128,256]{1,0:T(8,128)}, f32[128,256]{1,0:T(8,128)S(1)}, u32[]{:S(2)}, u32[]{:S(2)}) collective-permute-start(f32[128,256]{1,0:T(8,128)} %get-tuple-element.16), channel_id=1, source_target_pairs={{0,3},{1,0},{2,1},{3,2},{4,7},{5,4},{6,5},{7,6},{8,11},{9,8},{10,9... | collective-permute-start | bytes 393224 | tf_op jit(solution)/shard_map/ppermute | solution.py:158
  50.8 0.0 collective-permute-done.7
  50.8 0.0 collective-permute-done.8
  50.8 0.9 add_add_fusion.refs_4_
  51.7 1.5 %collective-permute-start.11 = (f32[128,256]{1,0:T(8,128)S(1)}, f32[128,256]{1,0:T(8,128)S(1)}, u32[]{:S(2)}, u32[]{:S(2)}) collective-permute-start(f32[128,256]{1,0:T(8,128)S(1)} %add_add_fusion.refs_4_), channel_id=1, source_target_pairs={{0,3},{1,0},{2,1},{3,2},{4,7},{5,4},{6,5},{7,6},{8,11},{9,8},{10,9... | collective-permute-start | bytes 393224 | tf_op jit(solution)/shard_map/ppermute | solution.py:158
  53.2 1.5 %collective-permute-start.10 = (f32[128,256]{1,0:T(8,128)S(1)}, f32[128,256]{1,0:T(8,128)S(1)}, u32[]{:S(2)}, u32[]{:S(2)}) collective-permute-start(f32[128,256]{1,0:T(8,128)S(1)} %add_add_fusion.refs_4_), channel_id=1, source_target_pairs={{0,2},{1,3},{2,0},{3,1},{4,6},{5,7},{6,4},{7,5},{8,10},{9,11},{10,... | collective-permute-start | bytes 393224 | tf_op jit(solution)/shard_map/ppermute | solution.py:158
  54.8 3.2 %collective-permute-done = f32[128,256]{1,0:T(8,128)S(1)} collective-permute-done((f32[128,256]{1,0:T(8,128)}, f32[128,256]{1,0:T(8,128)S(1)}, u32[]{:S(2)}, u32[]{:S(2)}) %collective-permute-start) | collective-permute-done | bytes 131104 | tf_op jit(solution)/shard_map/ppermute | solution.py:158
  58.0 1.0 collective-permute-done.2
  58.9 0.9 add_add_fusion.1.refs_0_
  59.9 2.3 %collective-permute-start.5 = (f32[128,256]{1,0:T(8,128)S(1)}, f32[128,256]{1,0:T(8,128)S(1)}, u32[]{:S(2)}, u32[]{:S(2)}) collective-permute-start(f32[128,256]{1,0:T(8,128)S(1)} %add_add_fusion.1.refs_0_), channel_id=1, source_target_pairs={{0,3},{1,0},{2,1},{3,2},{4,7},{5,4},{6,5},{7,6},{8,11},{9,8},{10,9... | collective-permute-start | bytes 393224 | tf_op jit(solution)/shard_map/ppermute | solution.py:158
  62.2 0.0 collective-permute-start.4
  62.2 1.2 collective-permute-start.3
  63.4 2.2 %collective-permute-done.9.refs_5_ = f32[128,256]{1,0:T(8,128)S(1)} collective-permute-done((f32[128,256]{1,0:T(8,128)S(1)}, f32[128,256]{1,0:T(8,128)S(1)}, u32[]{:S(2)}, u32[]{:S(2)}) %collective-permute-start.9) | collective-permute-done | bytes 131104 | tf_op jit(solution)/shard_map/ppermute | solution.py:158
  65.6 1.4 %collective-permute-done.5.refs_3_ = f32[128,256]{1,0:T(8,128)S(1)} collective-permute-done((f32[128,256]{1,0:T(8,128)S(1)}, f32[128,256]{1,0:T(8,128)S(1)}, u32[]{:S(2)}, u32[]{:S(2)}) %collective-permute-start.5) | collective-permute-done | bytes 131104 | tf_op jit(solution)/shard_map/ppermute | solution.py:158
  67.0 1.8 %collective-permute-done.4.refs_2_ = f32[128,256]{1,0:T(8,128)S(1)} collective-permute-done((f32[128,256]{1,0:T(8,128)S(1)}, f32[128,256]{1,0:T(8,128)S(1)}, u32[]{:S(2)}, u32[]{:S(2)}) %collective-permute-start.4) | collective-permute-done | bytes 131104 | tf_op jit(solution)/shard_map/ppermute | solution.py:158
  68.8 1.3 collective-permute-done.3.refs_1_
  70.1 0.6 copy-done.9
  70.7 23.0 %join.1 = bf16[4096,256]{1,0:T(8,128)(2,1)} custom-call(s32[1]{0:T(128)} %bitcast.view_ref, f32[128,256]{1,0:T(8,128)} %copy-done.3, f32[128,256]{1,0:T(8,128)} %copy-done.9, f32[128,256]{1,0:T(8,128)} %copy-done.8, f32[128,256]{1,0:T(8,128)} %copy-done.7, f32[128,256]{1,0:T(8,128)} %copy-done.2, f32[128,256]{1,0:T(8,128)} %copy-done.6, ...), custom_call_target="tpu_custom_call" | custom-call | tf_op jit(solution)/shard_map/join/pallas_call | solution.py:212
  93.7 38.0 %all_to_all.15 = bf16[128,32,256]{2,1,0:T(8,128)(2,1)S(1)} all-to-all(bf16[128,32,256]{2,1,0:T(8,128)(2,1)} %bitcast.18), channel_id=1, replica_groups=mesh['keys_0'=4,'keys_1'=4,'keys_2'=2,'view'=4] {'keys_0','keys_1','keys..., dimensions={0} | all-to-all | bytes 4194304 | tf_op jit(solution)/shard_map/all_to_all | solution.py:266
  131.7 1.0 convert_reduce_fusion
  (25 shorter events, 0.1 us)
Async XLA Ops:
  4.6 26.7 %all-to-all-start = ((bf16[32,72,256]{2,1,0:T(8,128)(2,1)}), bf16[32,72,256]{2,1,0:T(8,128)(2,1)S(1)}, u32[]{:S(2)}, u32[]{:S(2)}) async-start(bf16[32,72,256]{2,1,0:T(8,128)(2,1)} %bitcast.22), calls=%async_computation | async-start | bytes 2359296 | tf_op jit(solution)/shard_map/all_to_all | solution.py:232
  31.3 7.7 %copy-start.1 = (bf16[32,72,256]{2,1,0:T(8,128)(2,1)}, bf16[32,72,256]{2,1,0:T(8,128)(2,1)S(1)}, u32[]{:S(2)}) copy-start(bf16[32,72,256]{2,1,0:T(8,128)(2,1)S(1)} %all-to-all-done) | copy-start | bytes 3538948
  31.3 34.3 %all-to-all-start.1 = ((bf16[32,72,256]{2,1,0:T(8,128)(2,1)}), bf16[32,72,256]{2,1,0:T(8,128)(2,1)S(1)}, u32[]{:S(2)}, u32[]{:S(2)}) async-start(bf16[32,72,256]{2,1,0:T(8,128)(2,1)} %bitcast.20), calls=%async_computation.1 | async-start | bytes 2359296 | tf_op jit(solution)/shard_map/all_to_all | solution.py:232
  39.0 9.9 %collective-permute-start.6 = (f32[128,256]{1,0:T(8,128)}, f32[128,256]{1,0:T(8,128)S(1)}, u32[]{:S(2)}, u32[]{:S(2)}) collective-permute-start(f32[128,256]{1,0:T(8,128)} %get-tuple-element.18), channel_id=1, source_target_pairs={{0,1},{1,2},{2,3},{3,0},{4,5},{5,6},{6,7},{7,4},{8,9},{9,10},{10,1... | collective-permute-start | bytes 393224 | tf_op jit(solution)/shard_map/ppermute | solution.py:158
  40.5 10.2 %collective-permute-start.7 = (f32[128,256]{1,0:T(8,128)}, f32[128,256]{1,0:T(8,128)S(1)}, u32[]{:S(2)}, u32[]{:S(2)}) collective-permute-start(f32[128,256]{1,0:T(8,128)} %get-tuple-element.19), channel_id=1, source_target_pairs={{0,2},{1,3},{2,0},{3,1},{4,6},{5,7},{6,4},{7,5},{8,10},{9,11},{10,... | collective-permute-start | bytes 393224 | tf_op jit(solution)/shard_map/ppermute | solution.py:158
  43.3 7.5 %collective-permute-start.8 = (f32[128,256]{1,0:T(8,128)}, f32[128,256]{1,0:T(8,128)S(1)}, u32[]{:S(2)}, u32[]{:S(2)}) collective-permute-start(f32[128,256]{1,0:T(8,128)} %get-tuple-element.20), channel_id=1, source_target_pairs={{0,3},{1,0},{2,1},{3,2},{4,7},{5,4},{6,5},{7,6},{8,11},{9,8},{10,9... | collective-permute-start | bytes 393224 | tf_op jit(solution)/shard_map/ppermute | solution.py:158
  47.5 10.5 %collective-permute-start = (f32[128,256]{1,0:T(8,128)}, f32[128,256]{1,0:T(8,128)S(1)}, u32[]{:S(2)}, u32[]{:S(2)}) collective-permute-start(f32[128,256]{1,0:T(8,128)} %get-tuple-element.14), channel_id=1, source_target_pairs={{0,1},{1,2},{2,3},{3,0},{4,5},{5,6},{6,7},{7,4},{8,9},{9,10},{10,1... | collective-permute-start | bytes 393224 | tf_op jit(solution)/shard_map/ppermute | solution.py:158
  48.1 9.9 %collective-permute-start.1 = (f32[128,256]{1,0:T(8,128)}, f32[128,256]{1,0:T(8,128)S(1)}, u32[]{:S(2)}, u32[]{:S(2)}) collective-permute-start(f32[128,256]{1,0:T(8,128)} %get-tuple-element.15), channel_id=1, source_target_pairs={{0,2},{1,3},{2,0},{3,1},{4,6},{5,7},{6,4},{7,5},{8,10},{9,11},{10,... | collective-permute-start | bytes 393224 | tf_op jit(solution)/shard_map/ppermute | solution.py:158
  49.0 10.0 %collective-permute-start.2 = (f32[128,256]{1,0:T(8,128)}, f32[128,256]{1,0:T(8,128)S(1)}, u32[]{:S(2)}, u32[]{:S(2)}) collective-permute-start(f32[128,256]{1,0:T(8,128)} %get-tuple-element.16), channel_id=1, source_target_pairs={{0,3},{1,0},{2,1},{3,2},{4,7},{5,4},{6,5},{7,6},{8,11},{9,8},{10,9... | collective-permute-start | bytes 393224 | tf_op jit(solution)/shard_map/ppermute | solution.py:158
  51.7 18.4 %copy-start.2 = (f32[128,256]{1,0:T(8,128)}, f32[128,256]{1,0:T(8,128)S(1)}, u32[]{:S(2)}) copy-start(f32[128,256]{1,0:T(8,128)S(1)} %add_add_fusion.refs_4_) | copy-start | bytes 393220
  51.7 10.5 %collective-permute-start.11 = (f32[128,256]{1,0:T(8,128)S(1)}, f32[128,256]{1,0:T(8,128)S(1)}, u32[]{:S(2)}, u32[]{:S(2)}) collective-permute-start(f32[128,256]{1,0:T(8,128)S(1)} %add_add_fusion.refs_4_), channel_id=1, source_target_pairs={{0,3},{1,0},{2,1},{3,2},{4,7},{5,4},{6,5},{7,6},{8,11},{9,8},{10,9... | collective-permute-start | bytes 393224 | tf_op jit(solution)/shard_map/ppermute | solution.py:158
  53.2 10.2 %collective-permute-start.10 = (f32[128,256]{1,0:T(8,128)S(1)}, f32[128,256]{1,0:T(8,128)S(1)}, u32[]{:S(2)}, u32[]{:S(2)}) collective-permute-start(f32[128,256]{1,0:T(8,128)S(1)} %add_add_fusion.refs_4_), channel_id=1, source_target_pairs={{0,2},{1,3},{2,0},{3,1},{4,6},{5,7},{6,4},{7,5},{8,10},{9,11},{10,... | collective-permute-start | bytes 393224 | tf_op jit(solution)/shard_map/ppermute | solution.py:158
  58.0 7.7 %collective-permute-start.9 = (f32[128,256]{1,0:T(8,128)S(1)}, f32[128,256]{1,0:T(8,128)S(1)}, u32[]{:S(2)}, u32[]{:S(2)}) collective-permute-start(f32[128,256]{1,0:T(8,128)S(1)} %add_add_fusion.refs_4_), channel_id=1, source_target_pairs={{0,1},{1,2},{2,3},{3,0},{4,5},{5,6},{6,7},{7,4},{8,9},{9,10},{10,1... | collective-permute-start | bytes 393224 | tf_op jit(solution)/shard_map/ppermute | solution.py:158
  59.9 10.2 %copy-start.3 = (f32[128,256]{1,0:T(8,128)}, f32[128,256]{1,0:T(8,128)S(1)}, u32[]{:S(2)}) copy-start(f32[128,256]{1,0:T(8,128)S(1)} %add_add_fusion.1.refs_0_) | copy-start | bytes 393220
  59.9 7.1 %collective-permute-start.5 = (f32[128,256]{1,0:T(8,128)S(1)}, f32[128,256]{1,0:T(8,128)S(1)}, u32[]{:S(2)}, u32[]{:S(2)}) collective-permute-start(f32[128,256]{1,0:T(8,128)S(1)} %add_add_fusion.1.refs_0_), channel_id=1, source_target_pairs={{0,3},{1,0},{2,1},{3,2},{4,7},{5,4},{6,5},{7,6},{8,11},{9,8},{10,9... | collective-permute-start | bytes 393224 | tf_op jit(solution)/shard_map/ppermute | solution.py:158
  62.2 6.6 %collective-permute-start.4 = (f32[128,256]{1,0:T(8,128)S(1)}, f32[128,256]{1,0:T(8,128)S(1)}, u32[]{:S(2)}, u32[]{:S(2)}) collective-permute-start(f32[128,256]{1,0:T(8,128)S(1)} %add_add_fusion.1.refs_0_), channel_id=1, source_target_pairs={{0,2},{1,3},{2,0},{3,1},{4,6},{5,7},{6,4},{7,5},{8,10},{9,11},{10,... | collective-permute-start | bytes 393224 | tf_op jit(solution)/shard_map/ppermute | solution.py:158
  62.2 7.8 %copy-start.4 = (f32[128,256]{1,0:T(8,128)}, f32[128,256]{1,0:T(8,128)S(1)}, u32[]{:S(2)}) copy-start(f32[128,256]{1,0:T(8,128)S(1)} %collective-permute-done.11.refs_7_) | copy-start | bytes 393220
  62.2 7.8 %collective-permute-start.3 = (f32[128,256]{1,0:T(8,128)S(1)}, f32[128,256]{1,0:T(8,128)S(1)}, u32[]{:S(2)}, u32[]{:S(2)}) collective-permute-start(f32[128,256]{1,0:T(8,128)S(1)} %add_add_fusion.1.refs_0_), channel_id=1, source_target_pairs={{0,1},{1,2},{2,3},{3,0},{4,5},{5,6},{6,7},{7,4},{8,9},{9,10},{10,1... | collective-permute-start | bytes 393224 | tf_op jit(solution)/shard_map/ppermute | solution.py:158
  63.4 6.7 %copy-start.5 = (f32[128,256]{1,0:T(8,128)}, f32[128,256]{1,0:T(8,128)S(1)}, u32[]{:S(2)}) copy-start(f32[128,256]{1,0:T(8,128)S(1)} %collective-permute-done.10.refs_6_) | copy-start | bytes 393220
  65.6 4.5 %copy-start.6 = (f32[128,256]{1,0:T(8,128)}, f32[128,256]{1,0:T(8,128)S(1)}, u32[]{:S(2)}) copy-start(f32[128,256]{1,0:T(8,128)S(1)} %collective-permute-done.9.refs_5_) | copy-start | bytes 393220
  65.6 4.5 %copy-start = (bf16[32,72,256]{2,1,0:T(8,128)(2,1)}, bf16[32,72,256]{2,1,0:T(8,128)(2,1)S(1)}, u32[]{:S(2)}) copy-start(bf16[32,72,256]{2,1,0:T(8,128)(2,1)S(1)} %all-to-all-done.1) | copy-start | bytes 3538948
  67.0 3.1 %copy-start.7 = (f32[128,256]{1,0:T(8,128)}, f32[128,256]{1,0:T(8,128)S(1)}, u32[]{:S(2)}) copy-start(f32[128,256]{1,0:T(8,128)S(1)} %collective-permute-done.5.refs_3_) | copy-start | bytes 393220
  68.8 1.3 copy-start.8
  70.1 0.6 copy-start.9

commit v2 on v1

--- a/solution.py
+++ b/solution.py
@@ -5,6 +5,7 @@
 from jax.experimental.pallas import tpu as pltpu
 from jax.sharding import Mesh
 from jax.sharding import PartitionSpec as P
+
 
 KEYS_DEV = 512
 GROUPS_DEV = 32
@@ -143,14 +144,13 @@
     spread(total_ref, view_ref[0], outs)
 
 
-def slices(kernel, name, view, *args):
+def slices(kernel, view, *args):
     return pl.pallas_call(
         kernel,
         out_shape=[jax.ShapeDtypeStruct((128, D), F32)] * 4,
         in_specs=[SMEM] + [VMEM] * len(args),
         out_specs=[VMEM] * 4,
         scratch_shapes=[pltpu.VMEM((KEYS_DEV, D), F32)],
-        name=name,
     )(view, *args)
 
 
@@ -167,64 +167,102 @@
     return [x] + [shift(x, s) for s in (1, 2, 3)]
 
 
-def join_kernel(view_ref, *refs):
-    db, b = refs[:4], refs[4:8]
-    slot_ref, group_ref, weight_ref, payload_ref, in_ref = refs[8:13]
-    out_ref, table_ref, whole_ref, term_ref, groups_ref = refs[13:]
-    view = view_ref[0]
+def terms_of(ref, slot, weight, payload):
+    chosen = pick(rows_of((KEYS_DEV, 256)) == slot, weight)
+    got = dot(chosen, ref[...], TN)
+    return (payload.astype(F32) * (got[:, :D] + got[:, D:])).astype(BF16)
+
+
+def fill(ref, view, pieces):
     for s in range(4):
         at = pl.ds(((view + 4 - s) % 4) * 128, 128)
-        table = db[s][...]
-        whole = b[s][...] + table
-        for ref, value in ((table_ref, table), (whole_ref, whole)):
-            high = value.astype(BF16)
-            ref[at, :D] = high
-            ref[at, D:] = (value - high.astype(F32)).astype(BF16)
-
-    def terms(ref, slot, weight, payload):
-        chosen = pick(rows_of((KEYS_DEV, 256)) == slot, weight)
-        got = dot(chosen, ref[...], TN)
-        return (payload.astype(F32) * (got[:, :D] + got[:, D:])).astype(BF16)
-
+        value = pieces(s)
+        high = value.astype(BF16)
+        ref[at, :D] = high
+        ref[at, D:] = (value - high.astype(F32)).astype(BF16)
+
+
+def half_row(group, core):
+    row = ((group >> 8) << 7) | (group & 127)
+    return jnp.where(((group >> 7) & 1) == core, row, -1)
+
+
+def half_sum(pieces, out_ref):
+    def block(g, carry):
+        total = None
+        for at, terms in pieces:
+            chosen = pick(rows_of((256, at.shape[1])) + 256 * g == at[...], 1.0)
+            part = dot(chosen, terms[...])
+            total = part if total is None else total + part
+        out_ref[pl.ds(256 * g, 256), :] = total
+        return carry
+
+    lax.fori_loop(0, GROUPS // 512, block, 0)
+
+
+def join_a_kernel(view_ref, *refs):
+    db, (slot_ref, weight_ref, payload_ref), (out_ref, table_ref) = refs[:4], refs[4:7], refs[7:]
+    fill(table_ref, view_ref[0], lambda s: db[s][...])
     for c in range(16):
         slot = flat(slot_ref[2 * c : 2 * c + 2, :])
         weight = flat(weight_ref[2 * c : 2 * c + 2, :]).astype(F32)
         at = pl.ds(256 * c, 256)
-        term_ref[at, :] = terms(table_ref, slot, weight, payload_ref[at, :])
-        groups_ref[:, at] = flat(group_ref[2 * c : 2 * c + 2, :])
+        out_ref[at, :] = terms_of(table_ref, slot, weight, payload_ref[at, :])
+
+
+def join_d_kernel(view_ref, core_ref, *refs):
+    db, b, (group_ref, in_ref, a_ref) = refs[:4], refs[4:8], refs[8:11]
+    peer_ref, term_ref, own_a_ref, own_d_ref, whole_ref, peer_a_ref, peer_d_ref = refs[11:]
+    core = core_ref[0]
+    fill(whole_ref, view_ref[0], lambda s: b[s][...] + db[s][...])
+    for c in range(4):
+        at = pl.ds(1024 * c, 1024)
+        group = flat(group_ref[8 * c : 8 * c + 8, :])
+        own_a_ref[:, at] = half_row(group, core)
+        peer_a_ref[:, at] = half_row(group, 1 - core)
     for c in range(8):
         slot, group = fields_of(in_ref, c)
-        at = pl.ds(A_DEV + 256 * c, 256)
-        term_ref[at, :] = terms(whole_ref, slot, 1.0, payload_of(in_ref, c))
-        groups_ref[:, at] = group
-
-    def block(g, carry):
-        rows = groups_ref.shape[1]
-        chosen = pick(rows_of((256, rows)) + 256 * g == groups_ref[...], 1.0)
-        out_ref[pl.ds(256 * g, 256), :] = dot(chosen, term_ref[...]).astype(BF16)
-        return carry
-
-    lax.fori_loop(0, GROUPS // 256, block, 0)
-
-
-def join(view, db, b, slot, group, weight, payload, received):
-    rows = A_DEV + OWNERS * CAP
-    return pl.pallas_call(
-        join_kernel,
-        out_shape=jax.ShapeDtypeStruct((GROUPS, D), BF16),
-        in_specs=[SMEM] + [VMEM] * 13,
+        at = pl.ds(256 * c, 256)
+        own_d_ref[:, at] = half_row(group, core)
+        peer_d_ref[:, at] = half_row(group, 1 - core)
+        term_ref[at, :] = terms_of(whole_ref, slot, 1.0, payload_of(in_ref, c))
+    half_sum(((peer_a_ref, a_ref), (peer_d_ref, term_ref)), peer_ref)
+
+
+def own_kernel(own_a_ref, a_ref, own_d_ref, d_ref, out_ref):
+    half_sum(((own_a_ref, a_ref), (own_d_ref, d_ref)), out_ref)
+
+
+def join(view, core, db, b, slot, group, weight, payload, received):
+    rows = OWNERS * CAP
+    table = pltpu.VMEM((KEYS_DEV, 2 * D), BF16)
+    half = jax.ShapeDtypeStruct((GROUPS // 2, D), F32)
+    a_terms = pl.pallas_call(
+        join_a_kernel,
+        out_shape=jax.ShapeDtypeStruct((A_DEV, D), BF16),
+        in_specs=[SMEM] + [VMEM] * 7,
         out_specs=VMEM,
-        scratch_shapes=[
-            pltpu.VMEM((KEYS_DEV, 2 * D), BF16),
-            pltpu.VMEM((KEYS_DEV, 2 * D), BF16),
-            pltpu.VMEM((rows, D), BF16),
-            pltpu.VMEM((1, rows), I32),
+        scratch_shapes=[table],
+        name="join_a",
+    )(view, *db, slot.reshape(32, 128), weight.reshape(32, 128), payload)
+    peer, d_terms, own_a, own_d = pl.pallas_call(
+        join_d_kernel,
+        out_shape=[
+            half,
+            jax.ShapeDtypeStruct((rows, D), BF16),
+            jax.ShapeDtypeStruct((1, A_DEV), I32),
+            jax.ShapeDtypeStruct((1, rows), I32),
         ],
-        name="join",
-    )(
-        view, *db, *b, slot.reshape(32, 128), group.reshape(32, 128), weight.reshape(32, 128),
-        payload, received,
-    )
+        in_specs=[SMEM] * 2 + [VMEM] * 11,
+        out_specs=[VMEM] * 4,
+        scratch_shapes=[table, pltpu.VMEM((1, A_DEV), I32), pltpu.VMEM((1, rows), I32)],
+        name="join_d",
+    )(view, core, *db, *b, group.reshape(32, 128), received, a_terms)
+    other = lax.ppermute(peer, "keys_2", [(0, 1), (1, 0)])
+    own = pl.pallas_call(
+        own_kernel, out_shape=half, in_specs=[VMEM] * 4, out_specs=VMEM, name="join_own"
+    )(own_a, a_terms, own_d, d_terms)
+    return (own + other).astype(BF16)
 
 
 def exchange(packed):
@@ -254,16 +292,19 @@
     me = lax.axis_index(KEYS).astype(I32).reshape(1)
     view = lax.axis_index("view").astype(I32).reshape(1)
     table = key_slot.reshape(128, 128)
-    db_in = exchange(pack(me, db_count, table, db_key, db_mult, None, db_payload))
-    da_in = exchange(pack(me, da_count, table, da_key, da_mult, da_group, da_payload))
+    core = lax.axis_index("keys_2").astype(I32).reshape(1)
+    db_out = pack(me, db_count, table, db_key, db_mult, None, db_payload)
+    da_out = pack(me, da_count, table, da_key, da_mult, da_group, da_payload)
+    db_in = exchange(db_out)
+    da_in = exchange(da_out)
     b_parts = slices(
-        sum_b_kernel, "sum_b", view, b_slot.reshape(32, 128), b_weight.reshape(32, 128), b_payload
+        sum_b_kernel, view, b_slot.reshape(32, 128), b_weight.reshape(32, 128), b_payload
     )
     b = everyone(own_total(b_parts))
-    db = everyone(own_total(slices(sum_db_kernel, "sum_db", view, db_in)))
-    partial = join(view, db, b, a_slot, a_group, a_weight, a_payload, da_in)
-    blocks = partial.reshape(GROUPS // GROUPS_DEV, GROUPS_DEV, D)
-    blocks = lax.all_to_all(blocks, KEYS_VIEW, 0, 0, tiled=True)
+    db = everyone(own_total(slices(sum_db_kernel, view, db_in)))
+    partial = join(view, core, db, b, a_slot, a_group, a_weight, a_payload, da_in)
+    blocks = partial.reshape(GROUPS // 2 // GROUPS_DEV, GROUPS_DEV, D)
+    blocks = lax.all_to_all(blocks, ("keys_0", "keys_1", "view"), 0, 0, tiled=True)
     return jnp.sum(blocks.astype(F32), axis=0)
 
 

time: 134 us -> 130 us (0.970)
  blocking collectives: 38 us -> 27.3 us
  Pallas kernels: 37.5 us -> 44.3 us
  waiting for transfers between devices: 24.4 us -> 22.2 us
    all_to_all x1, blocking collectives: 38 us -> 27.3 us  [shards(): lax.all_to_all(blocks, ('keys_0', 'keys_1', 'view'), 0, 0, tiled=True)]
    pallas_call x1 -> x3, Pallas kernels: 23 us -> 29.8 us  [the longest x1 13 us: join(): pl.pallas_call(join_d_kernel, out_shape=[half, jax.ShapeDtypeStruct((rows...]
    ppermute x12, waiting for transfers between devices: 10.8 us -> 8.63 us  [shift(): return lax.ppermute(x, 'view', [(j, (j + s) % 4) for j in range(4)])]
    convert_element_type x0 -> x1, other arithmetic: none -> 1.8 us  [join(): return (own + other).astype(BF16)]
  transfers between devices with their start and end apart: 14 -> 15, of which waited for: 7 -> 3; matrix products, arithmetic and copies ran while one was open for 1% -> 1% of each run, Pallas kernels for 8% -> 21%
where the time goes in v2:
time: 130 us; the launch traced here: 129 us
  Pallas kernels  44.3 us (34%)
  starting transfers between devices  28.7 us (22%)
  blocking collectives  27.3 us (21%)
  waiting for transfers between devices  22.2 us (17%)
  other arithmetic  3.57 us (3%)
  local copies, waits for them, and re-layouts  1.81 us (1%)
  between operations  1.45 us (1%)
    all_to_all x1, blocking collectives, shards(): lax.all_to_all(blocks, ('keys_0', 'keys_1', 'view'), 0, 0, tiled=True)  27.3 us
    ppermute x12, starting transfers between devices, shift(): return lax.ppermute(x, 'view', [(j, (j + s) % 4) for j in range(4)])  16.2 us
    all_to_all x2, waiting for transfers between devices, exchange(): lax.all_to_all(blocks, KEYS, 0, 0, tiled=True).reshape(OWNERS * BLOCK, D)  13.6 us
    pallas_call x1, Pallas kernels, join(): pl.pallas_call(join_d_kernel, out_shape=[half, jax.ShapeDtypeStruct((rows...  13 us
    all_to_all x2, starting transfers between devices, exchange(): lax.all_to_all(blocks, KEYS, 0, 0, tiled=True).reshape(OWNERS * BLOCK, D)  12.4 us
    pallas_call x1, Pallas kernels, join(): pl.pallas_call(own_kernel, out_shape=half, in_specs=[VMEM] * 4, out_specs...  11.1 us
    ppermute x12, waiting for transfers between devices, shift(): return lax.ppermute(x, 'view', [(j, (j + s) % 4) for j in range(4)])  8.63 us
    pallas_call x2, Pallas kernels, pack(): pl.pallas_call(lambda *refs: pack_kernel(group is not None, *refs), out_s...  8.06 us
  transfers between devices with their start and end apart: 15, of which 3 were waited for; matrix products, arithmetic and copies ran while one was open for 1% of the time, Pallas kernels for 21%

profile of v2, /device:TPU:0, one launch (start us, length us, event | category | flops | bytes accessed | tf_op | source)
XLA Modules:
  0.0 129.3 jit_solution(14783927242705762118)
XLA Ops:
  0.7 4.0 %pack_b.1 = bf16[2304,256]{1,0:T(8,128)(2,1)} custom-call(s32[1]{0:T(128)} %bitcast.2.refs_0_, s32[1]{0:T(128)S(6)} %copy.19.refs_1_, s32[128,128]{1,0:T(8,128)} %bitcast.24, s32[8,128]{1,0:T(8,128)} %bitcast.31, s32[8,128]{1,0:T(8,128)} %bitcast.32, bf16[1024,256]{1,0:T(8,128)(2,1)} %refs_5_.1), custom_call_target="tpu_custom_call" | custom-call | tf_op jit(solution)/shard_map/pack_b/pallas_call | solution.py:98
  4.7 8.4 %all-to-all-start = ((bf16[32,72,256]{2,1,0:T(8,128)(2,1)}), bf16[32,72,256]{2,1,0:T(8,128)(2,1)S(1)}, u32[]{:S(2)}, u32[]{:S(2)}) async-start(bf16[32,72,256]{2,1,0:T(8,128)(2,1)} %bitcast.22), calls=%async_computation | async-start | bytes 2359296 | tf_op jit(solution)/shard_map/all_to_all | solution.py:270
  13.8 4.0 %pack_a.1 = bf16[2304,256]{1,0:T(8,128)(2,1)} custom-call(s32[1]{0:T(128)} %bitcast.2.refs_0_, s32[1]{0:T(128)S(6)} %copy.18.refs_1_, s32[128,128]{1,0:T(8,128)} %bitcast.25, s32[8,128]{1,0:T(8,128)} %bitcast.33, s32[8,128]{1,0:T(8,128)} %bitcast.34, s32[8,128]{1,0:T(8,128)} %bitcast.35, bf16[1024,256]{1,0:T(8,128)(2,1)} %refs_6_.2), custom_call_target="tpu_custom_call" | custom-call | tf_op jit(solution)/shard_map/pack_a/pallas_call | solution.py:98
  17.8 13.6 %all-to-all-done = bf16[32,72,256]{2,1,0:T(8,128)(2,1)S(1)} async-done(((bf16[32,72,256]{2,1,0:T(8,128)(2,1)}), bf16[32,72,256]{2,1,0:T(8,128)(2,1)S(1)}, u32[]{:S(2)}, u32[]{:S(2)}) %all-to-all-start) | async-done | bytes 1179680 | tf_op jit(solution)/shard_map/all_to_all | solution.py:270
  31.4 4.0 %all-to-all-start.1 = ((bf16[32,72,256]{2,1,0:T(8,128)(2,1)}), bf16[32,72,256]{2,1,0:T(8,128)(2,1)S(1)}, u32[]{:S(2)}, u32[]{:S(2)}) async-start(bf16[32,72,256]{2,1,0:T(8,128)(2,1)} %bitcast.20), calls=%async_computation.1 | async-start | bytes 2359296 | tf_op jit(solution)/shard_map/all_to_all | solution.py:270
  35.4 2.8 %shard_map.163 = (f32[128,256]{1,0:T(8,128)}, f32[128,256]{1,0:T(8,128)}, f32[128,256]{1,0:T(8,128)}, f32[128,256]{1,0:T(8,128)}) custom-call(s32[1]{0:T(128)} %bitcast.view_ref, bf16[2304,256]{1,0:T(8,128)(2,1)} %bitcast.21), custom_call_target="tpu_custom_call" | custom-call | tf_op jit(solution)/shard_map/pallas_call | solution.py:148
  38.2 1.5 %collective-permute-start = (f32[128,256]{1,0:T(8,128)}, f32[128,256]{1,0:T(8,128)S(1)}, u32[]{:S(2)}, u32[]{:S(2)}) collective-permute-start(f32[128,256]{1,0:T(8,128)} %get-tuple-element.18), channel_id=1, source_target_pairs={{0,1},{1,2},{2,3},{3,0},{4,5},{5,6},{6,7},{7,4},{8,9},{9,10},{10,1... | collective-permute-start | bytes 393224 | tf_op jit(solution)/shard_map/ppermute | solution.py:158
  39.7 2.7 %collective-permute-start.1 = (f32[128,256]{1,0:T(8,128)}, f32[128,256]{1,0:T(8,128)S(1)}, u32[]{:S(2)}, u32[]{:S(2)}) collective-permute-start(f32[128,256]{1,0:T(8,128)} %get-tuple-element.19), channel_id=1, source_target_pairs={{0,2},{1,3},{2,0},{3,1},{4,6},{5,7},{6,4},{7,5},{8,10},{9,11},{10,... | collective-permute-start | bytes 393224 | tf_op jit(solution)/shard_map/ppermute | solution.py:158
  42.4 1.4 %collective-permute-start.2 = (f32[128,256]{1,0:T(8,128)}, f32[128,256]{1,0:T(8,128)S(1)}, u32[]{:S(2)}, u32[]{:S(2)}) collective-permute-start(f32[128,256]{1,0:T(8,128)} %get-tuple-element.20), channel_id=1, source_target_pairs={{0,3},{1,0},{2,1},{3,2},{4,7},{5,4},{6,5},{7,6},{8,11},{9,8},{10,9... | collective-permute-start | bytes 393224 | tf_op jit(solution)/shard_map/ppermute | solution.py:158
  43.8 3.7 %shard_map.164 = (f32[128,256]{1,0:T(8,128)}, f32[128,256]{1,0:T(8,128)}, f32[128,256]{1,0:T(8,128)}, f32[128,256]{1,0:T(8,128)}) custom-call(s32[1]{0:T(128)} %bitcast.view_ref, s32[32,128]{1,0:T(8,128)} %bitcast.26, s32[32,128]{1,0:T(8,128)} %bitcast.27, bf16[4096,256]{1,0:T(8,128)(2,1)} %payload_ref.1), custom_call_target="tpu_custom_call" | custom-call | tf_op jit(solution)/shard_map/pallas_call | solution.py:148
  47.5 0.6 collective-permute-start.6
  48.1 0.9 collective-permute-start.7
  49.0 0.0 collective-permute-done
  49.0 1.8 %collective-permute-start.8 = (f32[128,256]{1,0:T(8,128)}, f32[128,256]{1,0:T(8,128)S(1)}, u32[]{:S(2)}, u32[]{:S(2)}) collective-permute-start(f32[128,256]{1,0:T(8,128)} %get-tuple-element.24), channel_id=1, source_target_pairs={{0,3},{1,0},{2,1},{3,2},{4,7},{5,4},{6,5},{7,6},{8,11},{9,8},{10,9... | collective-permute-start | bytes 393224 | tf_op jit(solution)/shard_map/ppermute | solution.py:158
  50.9 1.5 %collective-permute-start.5 = (f32[128,256]{1,0:T(8,128)S(1)}, f32[128,256]{1,0:T(8,128)S(1)}, u32[]{:S(2)}, u32[]{:S(2)}) collective-permute-start(f32[128,256]{1,0:T(8,128)S(1)} %add_add_fusion.1.refs_0_), channel_id=1, source_target_pairs={{0,3},{1,0},{2,1},{3,2},{4,7},{5,4},{6,5},{7,6},{8,11},{9,8},{10,9... | collective-permute-start | bytes 393224 | tf_op jit(solution)/shard_map/ppermute | solution.py:158
  52.4 1.6 %collective-permute-start.4 = (f32[128,256]{1,0:T(8,128)S(1)}, f32[128,256]{1,0:T(8,128)S(1)}, u32[]{:S(2)}, u32[]{:S(2)}) collective-permute-start(f32[128,256]{1,0:T(8,128)S(1)} %add_add_fusion.1.refs_0_), channel_id=1, source_target_pairs={{0,2},{1,3},{2,0},{3,1},{4,6},{5,7},{6,4},{7,5},{8,10},{9,11},{10,... | collective-permute-start | bytes 393224 | tf_op jit(solution)/shard_map/ppermute | solution.py:158
  53.9 5.5 %collective-permute-done.6 = f32[128,256]{1,0:T(8,128)S(1)} collective-permute-done((f32[128,256]{1,0:T(8,128)}, f32[128,256]{1,0:T(8,128)S(1)}, u32[]{:S(2)}, u32[]{:S(2)}) %collective-permute-start.6) | collective-permute-done | bytes 131104 | tf_op jit(solution)/shard_map/ppermute | solution.py:158
  59.4 0.9 add_add_fusion.refs_4_
  60.4 3.3 %collective-permute-start.11 = (f32[128,256]{1,0:T(8,128)S(1)}, f32[128,256]{1,0:T(8,128)S(1)}, u32[]{:S(2)}, u32[]{:S(2)}) collective-permute-start(f32[128,256]{1,0:T(8,128)S(1)} %add_add_fusion.refs_4_), channel_id=1, source_target_pairs={{0,3},{1,0},{2,1},{3,2},{4,7},{5,4},{6,5},{7,6},{8,11},{9,8},{10,9... | collective-permute-start | bytes 393224 | tf_op jit(solution)/shard_map/ppermute | solution.py:158
  63.7 0.9 collective-permute-start.9
  64.6 3.1 %collective-permute-done.3.refs_1_ = f32[128,256]{1,0:T(8,128)S(1)} collective-permute-done((f32[128,256]{1,0:T(8,128)S(1)}, f32[128,256]{1,0:T(8,128)S(1)}, u32[]{:S(2)}, u32[]{:S(2)}) %collective-permute-start.3) | collective-permute-done | bytes 131104 | tf_op jit(solution)/shard_map/ppermute | solution.py:158
  67.8 0.6 copy-done.5
  68.4 5.7 %join_a.1.refs_10_.a_ref = bf16[4096,256]{1,0:T(8,128)(2,1)} custom-call(s32[1]{0:T(128)} %bitcast.view_ref, f32[128,256]{1,0:T(8,128)} %copy-done.2, f32[128,256]{1,0:T(8,128)} %copy-done.5, f32[128,256]{1,0:T(8,128)} %copy-done.4, f32[128,256]{1,0:T(8,128)} %copy-done.3, s32[32,128]{1,0:T(8,128)} %bitcast.28, s32[32,128]{1,0:T(8,128)} %bitcast.29, ...), custom_call_target="tpu_custom_call" | custom-call | tf_op jit(solution)/shard_map/join_a/pallas_call | solution.py:240
  74.2 0.6 copy-done.7
  74.8 0.1 copy-done.9
  74.9 0.0 copy-done.10
  74.9 0.4 copy-done
  75.3 13.0 %join_d.1 = (f32[2048,256]{1,0:T(8,128)}, bf16[2048,256]{1,0:T(8,128)(2,1)}, s32[1,4096]{1,0:T(1,128)}, s32[1,2048]{1,0:T(1,128)}) custom-call(s32[1]{0:T(128)} %bitcast.view_ref, s32[1]{0:T(128)} %bitcast.1.core_ref, f32[128,256]{1,0:T(8,128)} %copy-done.2, f32[128,256]{1,0:T(8,128)} %copy-done.5, f32[128,256]{1,0:T(8,128)} %copy-done.4, ...), custom_call_target="tpu_custom_call" | custom-call | tf_op jit(solution)/shard_map/join_d/pallas_call | solution.py:248
  88.4 11.1 %join_own.1 = f32[2048,256]{1,0:T(8,128)} custom-call(s32[1,4096]{1,0:T(1,128)} %get-tuple-element.25.own_a_ref, bf16[4096,256]{1,0:T(8,128)(2,1)} %join_a.1.refs_10_.a_ref, s32[1,2048]{1,0:T(1,128)} %get-tuple-element.26.own_d_ref, bf16[2048,256]{1,0:T(8,128)(2,1)} %get-tuple-element.27.d_ref), custom_call_target="tpu_custom_call" | custom-call | tf_op jit(solution)/shard_map/join_own/pallas_call | solution.py:262
  99.4 1.8 %add_convert_fusion = bf16[2048,256]{1,0:T(8,128)(2,1)S(1)} fusion(f32[2048,256]{1,0:T(8,128)} %join_own.1, f32[2048,256]{1,0:T(8,128)S(1)} %collective-permute-done.12), kind=kLoop, calls=%fused_computation.1 | loop fusion | flops 1048576 | bytes 5242880 | tf_op jit(solution)/shard_map/convert_element_type | solution.py:265
  101.2 27.3 %all_to_all.15 = bf16[64,32,256]{2,1,0:T(8,128)(2,1)S(1)} all-to-all(bf16[64,32,256]{2,1,0:T(8,128)(2,1)S(1)} %bitcast.23), channel_id=1, replica_groups=mesh['keys_0'=4,'keys_1'=4,'keys_2'=2,'view'=4] {'keys_0','keys_1','view'}, dimensions={0} | all-to-all | bytes 2097152 | tf_op jit(solution)/shard_map/all_to_all | solution.py:307
  128.6 0.8 convert_reduce_fusion
  (32 shorter events, 0.1 us)
Async XLA Ops:
  4.7 26.7 %all-to-all-start = ((bf16[32,72,256]{2,1,0:T(8,128)(2,1)}), bf16[32,72,256]{2,1,0:T(8,128)(2,1)S(1)}, u32[]{:S(2)}, u32[]{:S(2)}) async-start(bf16[32,72,256]{2,1,0:T(8,128)(2,1)} %bitcast.22), calls=%async_computation | async-start | bytes 2359296 | tf_op jit(solution)/shard_map/all_to_all | solution.py:270
  31.4 4.0 %copy-start.1 = (bf16[32,72,256]{2,1,0:T(8,128)(2,1)}, bf16[32,72,256]{2,1,0:T(8,128)(2,1)S(1)}, u32[]{:S(2)}) copy-start(bf16[32,72,256]{2,1,0:T(8,128)(2,1)S(1)} %all-to-all-done) | copy-start | bytes 3538948
  31.4 42.8 %all-to-all-start.1 = ((bf16[32,72,256]{2,1,0:T(8,128)(2,1)}), bf16[32,72,256]{2,1,0:T(8,128)(2,1)S(1)}, u32[]{:S(2)}, u32[]{:S(2)}) async-start(bf16[32,72,256]{2,1,0:T(8,128)(2,1)} %bitcast.20), calls=%async_computation.1 | async-start | bytes 2359296 | tf_op jit(solution)/shard_map/all_to_all | solution.py:270
  38.2 12.6 %copy-start.8 = (f32[128,256]{1,0:T(8,128)S(1)}, f32[128,256]{1,0:T(8,128)}, u32[]{:S(2)}) copy-start(f32[128,256]{1,0:T(8,128)} %get-tuple-element.17) | copy-start | bytes 393220
  38.2 10.8 %collective-permute-start = (f32[128,256]{1,0:T(8,128)}, f32[128,256]{1,0:T(8,128)S(1)}, u32[]{:S(2)}, u32[]{:S(2)}) collective-permute-start(f32[128,256]{1,0:T(8,128)} %get-tuple-element.18), channel_id=1, source_target_pairs={{0,1},{1,2},{2,3},{3,0},{4,5},{5,6},{6,7},{7,4},{8,9},{9,10},{10,1... | collective-permute-start | bytes 393224 | tf_op jit(solution)/shard_map/ppermute | solution.py:158
  39.7 11.1 %collective-permute-start.1 = (f32[128,256]{1,0:T(8,128)}, f32[128,256]{1,0:T(8,128)S(1)}, u32[]{:S(2)}, u32[]{:S(2)}) collective-permute-start(f32[128,256]{1,0:T(8,128)} %get-tuple-element.19), channel_id=1, source_target_pairs={{0,2},{1,3},{2,0},{3,1},{4,6},{5,7},{6,4},{7,5},{8,10},{9,11},{10,... | collective-permute-start | bytes 393224 | tf_op jit(solution)/shard_map/ppermute | solution.py:158
  42.4 8.4 %collective-permute-start.2 = (f32[128,256]{1,0:T(8,128)}, f32[128,256]{1,0:T(8,128)S(1)}, u32[]{:S(2)}, u32[]{:S(2)}) collective-permute-start(f32[128,256]{1,0:T(8,128)} %get-tuple-element.20), channel_id=1, source_target_pairs={{0,3},{1,0},{2,1},{3,2},{4,7},{5,4},{6,5},{7,6},{8,11},{9,8},{10,9... | collective-permute-start | bytes 393224 | tf_op jit(solution)/shard_map/ppermute | solution.py:158
  47.5 11.9 %collective-permute-start.6 = (f32[128,256]{1,0:T(8,128)}, f32[128,256]{1,0:T(8,128)S(1)}, u32[]{:S(2)}, u32[]{:S(2)}) collective-permute-start(f32[128,256]{1,0:T(8,128)} %get-tuple-element.22), channel_id=1, source_target_pairs={{0,1},{1,2},{2,3},{3,0},{4,5},{5,6},{6,7},{7,4},{8,9},{9,10},{10,1... | collective-permute-start | bytes 393224 | tf_op jit(solution)/shard_map/ppermute | solution.py:158
  48.1 11.3 %collective-permute-start.7 = (f32[128,256]{1,0:T(8,128)}, f32[128,256]{1,0:T(8,128)S(1)}, u32[]{:S(2)}, u32[]{:S(2)}) collective-permute-start(f32[128,256]{1,0:T(8,128)} %get-tuple-element.23), channel_id=1, source_target_pairs={{0,2},{1,3},{2,0},{3,1},{4,6},{5,7},{6,4},{7,5},{8,10},{9,11},{10,... | collective-permute-start | bytes 393224 | tf_op jit(solution)/shard_map/ppermute | solution.py:158
  49.0 10.4 %collective-permute-start.8 = (f32[128,256]{1,0:T(8,128)}, f32[128,256]{1,0:T(8,128)S(1)}, u32[]{:S(2)}, u32[]{:S(2)}) collective-permute-start(f32[128,256]{1,0:T(8,128)} %get-tuple-element.24), channel_id=1, source_target_pairs={{0,3},{1,0},{2,1},{3,2},{4,7},{5,4},{6,5},{7,6},{8,11},{9,8},{10,9... | collective-permute-start | bytes 393224 | tf_op jit(solution)/shard_map/ppermute | solution.py:158
  50.9 16.9 %copy-start.2 = (f32[128,256]{1,0:T(8,128)}, f32[128,256]{1,0:T(8,128)S(1)}, u32[]{:S(2)}) copy-start(f32[128,256]{1,0:T(8,128)S(1)} %add_add_fusion.1.refs_0_) | copy-start | bytes 393220
  50.9 12.8 %collective-permute-start.5 = (f32[128,256]{1,0:T(8,128)S(1)}, f32[128,256]{1,0:T(8,128)S(1)}, u32[]{:S(2)}, u32[]{:S(2)}) collective-permute-start(f32[128,256]{1,0:T(8,128)S(1)} %add_add_fusion.1.refs_0_), channel_id=1, source_target_pairs={{0,3},{1,0},{2,1},{3,2},{4,7},{5,4},{6,5},{7,6},{8,11},{9,8},{10,9... | collective-permute-start | bytes 393224 | tf_op jit(solution)/shard_map/ppermute | solution.py:158
  52.4 12.3 %collective-permute-start.4 = (f32[128,256]{1,0:T(8,128)S(1)}, f32[128,256]{1,0:T(8,128)S(1)}, u32[]{:S(2)}, u32[]{:S(2)}) collective-permute-start(f32[128,256]{1,0:T(8,128)S(1)} %add_add_fusion.1.refs_0_), channel_id=1, source_target_pairs={{0,2},{1,3},{2,0},{3,1},{4,6},{5,7},{6,4},{7,5},{8,10},{9,11},{10,... | collective-permute-start | bytes 393224 | tf_op jit(solution)/shard_map/ppermute | solution.py:158
  59.4 8.4 %collective-permute-start.3 = (f32[128,256]{1,0:T(8,128)S(1)}, f32[128,256]{1,0:T(8,128)S(1)}, u32[]{:S(2)}, u32[]{:S(2)}) collective-permute-start(f32[128,256]{1,0:T(8,128)S(1)} %add_add_fusion.1.refs_0_), channel_id=1, source_target_pairs={{0,1},{1,2},{2,3},{3,0},{4,5},{5,6},{6,7},{7,4},{8,9},{9,10},{10,1... | collective-permute-start | bytes 393224 | tf_op jit(solution)/shard_map/ppermute | solution.py:158
  60.4 13.8 %copy-start.6 = (f32[128,256]{1,0:T(8,128)}, f32[128,256]{1,0:T(8,128)S(1)}, u32[]{:S(2)}) copy-start(f32[128,256]{1,0:T(8,128)S(1)} %add_add_fusion.refs_4_) | copy-start | bytes 393220
  60.4 13.7 %collective-permute-start.11 = (f32[128,256]{1,0:T(8,128)S(1)}, f32[128,256]{1,0:T(8,128)S(1)}, u32[]{:S(2)}, u32[]{:S(2)}) collective-permute-start(f32[128,256]{1,0:T(8,128)S(1)} %add_add_fusion.refs_4_), channel_id=1, source_target_pairs={{0,3},{1,0},{2,1},{3,2},{4,7},{5,4},{6,5},{7,6},{8,11},{9,8},{10,9... | collective-permute-start | bytes 393224 | tf_op jit(solution)/shard_map/ppermute | solution.py:158
  63.7 10.4 %collective-permute-start.10 = (f32[128,256]{1,0:T(8,128)S(1)}, f32[128,256]{1,0:T(8,128)S(1)}, u32[]{:S(2)}, u32[]{:S(2)}) collective-permute-start(f32[128,256]{1,0:T(8,128)S(1)} %add_add_fusion.refs_4_), channel_id=1, source_target_pairs={{0,2},{1,3},{2,0},{3,1},{4,6},{5,7},{6,4},{7,5},{8,10},{9,11},{10,... | collective-permute-start | bytes 393224 | tf_op jit(solution)/shard_map/ppermute | solution.py:158
  63.7 4.1 %copy-start.3 = (f32[128,256]{1,0:T(8,128)}, f32[128,256]{1,0:T(8,128)S(1)}, u32[]{:S(2)}) copy-start(f32[128,256]{1,0:T(8,128)S(1)} %collective-permute-done.5.refs_3_) | copy-start | bytes 393220
  63.7 10.4 %collective-permute-start.9 = (f32[128,256]{1,0:T(8,128)S(1)}, f32[128,256]{1,0:T(8,128)S(1)}, u32[]{:S(2)}, u32[]{:S(2)}) collective-permute-start(f32[128,256]{1,0:T(8,128)S(1)} %add_add_fusion.refs_4_), channel_id=1, source_target_pairs={{0,1},{1,2},{2,3},{3,0},{4,5},{5,6},{6,7},{7,4},{8,9},{9,10},{10,1... | collective-permute-start | bytes 393224 | tf_op jit(solution)/shard_map/ppermute | solution.py:158
  64.6 3.1 %copy-start.4 = (f32[128,256]{1,0:T(8,128)}, f32[128,256]{1,0:T(8,128)S(1)}, u32[]{:S(2)}) copy-start(f32[128,256]{1,0:T(8,128)S(1)} %collective-permute-done.4.refs_2_) | copy-start | bytes 393220
  67.8 0.7 copy-start.5
  74.1 0.7 copy-start.7
  74.1 0.7 copy-start.9
  74.2 0.7 copy-start.10
  74.2 1.2 copy-start
  88.3 11.1 %collective-permute-start.12 = (f32[2048,256]{1,0:T(8,128)}, f32[2048,256]{1,0:T(8,128)S(1)}, u32[]{:S(2)}, u32[]{:S(2)}) collective-permute-start(f32[2048,256]{1,0:T(8,128)} %get-tuple-element.28), channel_id=1, source_target_pairs={{0,4},{4,0},{1,5},{5,1},{2,6},{6,2},{3,7},{7,3},{8,12},{12,8},{9,1... | collective-permute-start | bytes 6291464 | tf_op jit(solution)/shard_map/ppermute | solution.py:261

commit v3 on v2

v3 whole, which is shorter than its diff:
```python
import jax
import jax.numpy as jnp
from jax import lax
from jax.experimental import pallas as pl
from jax.experimental.pallas import tpu as pltpu
from jax.sharding import Mesh
from jax.sharding import PartitionSpec as P


KEYS_DEV = 512
GROUPS_DEV = 32
GROUPS = 4096
DELTA_DEV = 1024
A_DEV = 4096
D = 256
OWNERS = 32
CAP = 64
BLOCK = CAP + 8
SORT, SORT_RUNS = 1024, 2
WINDOW = 1408
LIMIT = pltpu.CompilerParams(vmem_limit_bytes=16 * 2**20)
KEYS = ("keys_0", "keys_1", "keys_2")
KEYS_VIEW = ("keys_0", "keys_1", "keys_2", "view")
F32, BF16, I32, I16 = jnp.float32, jnp.bfloat16, jnp.int32, jnp.int16
NN = (((1,), (0,)), ((), ()))
NT = (((1,), (1,)), ((), ()))
TN = (((0,), (0,)), ((), ()))
VMEM = pl.BlockSpec(memory_space=pltpu.VMEM)
SMEM = pl.BlockSpec(memory_space=pltpu.SMEM)


def dot(x, y, dims=NN):
    return lax.dot_general(x, y, dims, preferred_element_type=F32)


def rows_of(shape):
    return lax.broadcasted_iota(I32, shape, 0)


def lanes_of(shape):
    return lax.broadcasted_iota(I32, shape, 1)


def flat(x):
    return jnp.concatenate([x[j : j + 1, :] for j in range(x.shape[0])], axis=1)


def pick(condition, value):
    return jnp.where(condition, value, 0.0).astype(BF16)


def onehot(rows, index, value=None):
    hit = lax.broadcasted_iota(I16, (rows, index.shape[1]), 0) == index.astype(I16)
    one = jnp.ones((), BF16) if value is None else value.astype(BF16)
    return jnp.where(hit, one, jnp.zeros((), BF16))


def counted_before(marks):
    step = jnp.where(
        (rows_of((128, 256)) < lanes_of((128, 256))) | (lanes_of((128, 256)) >= 128), 1.0, 0.0
    ).astype(BF16)
    before, carry = [], jnp.zeros((marks.shape[0], 128), F32)
    for j in range(marks.shape[1] // 128):
        counted = dot(marks[:, 128 * j : 128 * (j + 1)].astype(BF16), step)
        before.append(counted[:, :128] + carry)
        carry = carry + counted[:, 128:]
    return jnp.concatenate(before, axis=1)


def pack_kernel(with_group, me_ref, count_ref, table_ref, key_ref, mult_ref, *rest):
    group_ref = rest[0] if with_group else None
    payload_ref, out_ref = rest[-2:]
    rows = DELTA_DEV
    key = flat(key_ref[...])
    key_hi, key_lo = key >> 7, key & 127
    low = onehot(128, key_lo)
    table = table_ref[...]
    found = dot((table >> 7).astype(F32).astype(BF16), low) * 128.0 + dot(
        (table & 127).astype(F32).astype(BF16), low
    )
    slot = jnp.sum(jnp.where(rows_of((128, rows)) == key_hi, found, 0.0), axis=0, keepdims=True)
    slot = slot.astype(I32)
    owner, local = slot >> 9, slot & 511
    live = lanes_of((1, rows)) < count_ref[0]
    owner = jnp.where(live, owner, -1)
    marks = jnp.where(rows_of((OWNERS, rows)) == owner, 1.0, 0.0)
    rank = jnp.sum(marks * counted_before(marks), axis=0, keepdims=True).astype(I32)
    position = jnp.where(live, owner * CAP + rank, -1)
    sign = flat(mult_ref[...]).astype(F32)
    payload = payload_ref[...]
    for c in range(OWNERS // 4):
        chosen = onehot(4 * CAP, position - 4 * CAP * c, sign)
        packed = dot(chosen, payload).astype(BF16)
        for j in range(4):
            out_ref[pl.ds((4 * c + j) * BLOCK, CAP), :] = packed[CAP * j : CAP * (j + 1)]
    field = rows_of((8, rows))
    value = jnp.where(field == 0, local & 255, jnp.where(field == 1, local >> 8, 0))
    if with_group:
        group = flat(group_ref[...])
        value = jnp.where(field == 2, group & 255, jnp.where(field == 3, group >> 8, value))
    value = jnp.broadcast_to(value.astype(F32)[None], (OWNERS, 8, rows)).reshape(8 * OWNERS, rows)
    sent = pick((rows_of((8 * OWNERS, rows)) >> 3) == owner, value)
    place = onehot(4 * CAP, rank + CAP * (me_ref[0] % 4))
    fields = dot(sent, place, NT).astype(BF16)
    for k in range(OWNERS):
        out_ref[pl.ds(k * BLOCK + CAP, 8), :] = fields[8 * k : 8 * k + 8]


def pack(me, count, table, key, mult, group, payload):
    extra = [] if group is None else [group.reshape(8, 128)]
    return pl.pallas_call(
        lambda *refs: pack_kernel(group is not None, *refs),
        out_shape=jax.ShapeDtypeStruct((OWNERS * BLOCK, D), BF16),
        in_specs=[SMEM, SMEM] + [VMEM] * (4 + len(extra)),
        out_specs=VMEM,
        compiler_params=LIMIT,
        name="pack_a" if extra else "pack_b",
    )(me, count, table, key.reshape(8, 128), mult.reshape(8, 128), *extra, payload)


def fields_of(ref, c):
    total = ref[pl.ds(4 * c * BLOCK + CAP, 8), :].astype(F32)
    for j in range(1, 4):
        total = total + ref[pl.ds((4 * c + j) * BLOCK + CAP, 8), :].astype(F32)
    total = total.astype(I32)
    return total[0:1] + 256 * total[1:2], total[2:3] + 256 * total[3:4]


def payload_of(ref, c):
    return jnp.concatenate(
        [ref[pl.ds((4 * c + j) * BLOCK, CAP), :] for j in range(4)], axis=0
    )


def spread(total_ref, view, outs):
    for s in range(4):
        outs[s][...] = total_ref[pl.ds(((view + s) % 4) * 128, 128), :]


def sum_b_kernel(view_ref, slot_ref, weight_ref, payload_ref, *rest):
    outs, total_ref = rest[:4], rest[4]
    total_ref[...] = jnp.zeros_like(total_ref)
    for c in range(4):
        slot = flat(slot_ref[8 * c : 8 * c + 8, :])
        weight = flat(weight_ref[8 * c : 8 * c + 8, :]).astype(F32)
        chosen = onehot(KEYS_DEV, slot, weight)
        total_ref[...] += dot(chosen, payload_ref[1024 * c : 1024 * (c + 1), :])
    spread(total_ref, view_ref[0], outs)


def sum_db_kernel(view_ref, in_ref, *rest):
    outs, total_ref = rest[:4], rest[4]
    total_ref[...] = jnp.zeros_like(total_ref)
    for c in range(8):
        slot, _ = fields_of(in_ref, c)
        chosen = onehot(KEYS_DEV, slot)
        total_ref[...] += dot(chosen, payload_of(in_ref, c))
    spread(total_ref, view_ref[0], outs)


def slices(kernel, view, *args):
    return pl.pallas_call(
        kernel,
        out_shape=[jax.ShapeDtypeStruct((128, D), F32)] * 4,
        in_specs=[SMEM] + [VMEM] * len(args),
        out_specs=[VMEM] * 4,
        scratch_shapes=[pltpu.VMEM((KEYS_DEV, D), F32)],
        compiler_params=LIMIT,
    )(view, *args)


def shift(x, s):
    return lax.ppermute(x, "view", [(j, (j + s) % 4) for j in range(4)])


def own_total(parts):
    got = [parts[0]] + [shift(parts[s], s) for s in (1, 2, 3)]
    return (got[0] + got[1]) + (got[2] + got[3])


def everyone(x):
    return [x] + [shift(x, s) for s in (1, 2, 3)]


def fill(ref, view, pieces):
    for s in range(4):
        at = pl.ds(((view + 4 - s) % 4) * 128, 128)
        value = pieces(s)
        high = value.astype(BF16)
        ref[at, :D] = high
        ref[at, D:] = (value - high.astype(F32)).astype(BF16)


def terms_of(ref, slot, weight, payload):
    got = dot(onehot(KEYS_DEV, slot, weight), ref[...], TN)
    return (payload.astype(F32) * (got[:, :D] + got[:, D:])).astype(BF16)


def place_of(group, core):
    own = jnp.where(((group >> 7) & 1) == core, GROUPS // 2, 0)
    return own + ((group >> 8) << 7) + (group & 127)


def sort_kernel(core_ref, slot_ref, group_ref, weight_ref, payload_ref, out_ref, slots_ref, places_ref, weights_ref):
    for s in range(SORT_RUNS):
        rows = slice(8 * s, 8 * s + 8)
        slot, weight = flat(slot_ref[rows, :]), flat(weight_ref[rows, :])
        place = place_of(flat(group_ref[rows, :]), core_ref[0])
        bucket = place >> 6
        shape = (GROUPS // 64, SORT)
        marks = jnp.where(rows_of(shape) == bucket, 1.0, 0.0)
        first = jnp.sum(jnp.where(bucket < rows_of(shape), 1.0, 0.0), axis=1, keepdims=True)
        position = jnp.sum(marks * (counted_before(marks) + first), axis=0, keepdims=True)
        order = onehot(SORT, position.astype(I32))
        moved = dot(order, payload_ref[SORT * s : SORT * (s + 1), :]).astype(BF16)
        value, field = jnp.zeros((8, SORT), I32), rows_of((8, SORT))
        for q, part in enumerate((slot & 255, slot >> 8, weight, place & 255, place >> 8)):
            value = jnp.where(field == q, part, value)
        fields = dot(value.astype(F32).astype(BF16), order, NT).astype(I32)
        for j in range(4):
            at = slice(512 * j + 256 * s, 512 * j + 256 * (s + 1))
            part = slice(256 * j, 256 * (j + 1))
            out_ref[at, :] = moved[part]
            slots_ref[:, at] = fields[0:1, part] + 256 * fields[1:2, part]
            weights_ref[:, at] = fields[2:3, part]
            places_ref[:, at] = fields[3:4, part] + 256 * fields[4:5, part]


def sort(h, core, slot, group, weight, payload):
    rows = SORT_RUNS * SORT
    line = jax.ShapeDtypeStruct((1, rows), I32)
    return pl.pallas_call(
        sort_kernel,
        out_shape=[jax.ShapeDtypeStruct((rows, D), BF16), line, line, line],
        grid=(1,),
        in_specs=[SMEM] + [pl.BlockSpec((rows // 128, 128), lambda i: (h, 0))] * 3 + [pl.BlockSpec((rows, D), lambda i: (h, 0))],
        out_specs=[VMEM] * 4,
        compiler_params=LIMIT,
    )(core, slot.reshape(32, 128), group.reshape(32, 128), weight.reshape(32, 128), payload)


def join_kernel(view_ref, core_ref, *refs):
    db, b, sorted_rows, in_ref = refs[:4], refs[4:8], (refs[8:12], refs[12:16]), refs[16]
    peer_ref, own_ref, delta_ref, place_ref = refs[17:21]
    table_ref, whole_ref, term_ref, line_ref, total_ref = refs[21:]
    view, core = view_ref[0], core_ref[0]
    fill(table_ref, view, lambda s: db[s][...])
    fill(whole_ref, view, lambda s: b[s][...] + db[s][...])
    total_ref[...] = jnp.zeros_like(total_ref)
    starts, ends = [], []
    for j in range(4):
        for h, (payload_ref, slots_ref, places_ref, weights_ref) in enumerate(sorted_rows):
            part, at = slice(512 * j, 512 * (j + 1)), slice(1024 * j + 512 * h, 1024 * j + 512 * (h + 1))
            term_ref[at, :] = terms_of(table_ref, slots_ref[:, part], weights_ref[:, part].astype(F32), payload_ref[part, :])
            line_ref[:, at] = places_ref[:, part]
        line = line_ref[:, 1024 * j : 1024 * (j + 1)]
        starts.append(pl.multiple_of((jnp.min(line) >> 6) << 6, 64))
        ends.append(jnp.max(line))

    def window(j, start):
        rows = slice(1024 * j, 1024 * (j + 1))
        chosen = onehot(WINDOW, line_ref[:, rows] - start)
        total_ref[pl.ds(start, WINDOW), :] += dot(chosen, term_ref[rows, :])

    for j in range(4):
        window(j, starts[j])
    for j in range(4):
        def more(i, carry, j=j):
            window(j, pl.multiple_of(starts[j] + i * WINDOW, 64))
            return carry

        lax.fori_loop(1, (ends[j] - starts[j]) // WINDOW + 1, more, 0)
    for c in range(8):
        slot, group = fields_of(in_ref, c)
        at = slice(256 * c, 256 * (c + 1))
        place_ref[:, at] = place_of(group, core)
        delta_ref[at, :] = terms_of(whole_ref, slot, None, payload_of(in_ref, c))
    for g in range(GROUPS // 2 // 512):
        at = slice(512 * g, 512 * (g + 1))
        chosen = onehot(512, place_ref[...] - 512 * g)
        peer_ref[at, :] = total_ref[at, :] + dot(chosen, delta_ref[...])
    own_ref[...] = total_ref[GROUPS // 2 : GROUPS, :]


def own_kernel(own_ref, delta_ref, place_ref, out_ref):
    for g in range(GROUPS // 2 // 512):
        at = slice(512 * g, 512 * (g + 1))
        chosen = onehot(512, place_ref[...] - GROUPS // 2 - 512 * g)
        out_ref[at, :] = own_ref[at, :] + dot(chosen, delta_ref[...])


def join(view, core, db, b, halves, received):
    rows = OWNERS * CAP
    table = pltpu.VMEM((KEYS_DEV, 2 * D), BF16)
    half = jax.ShapeDtypeStruct((GROUPS // 2, D), F32)
    peer, own, delta, place = pl.pallas_call(
        join_kernel,
        out_shape=[
            half,
            half,
            jax.ShapeDtypeStruct((rows, D), BF16),
            jax.ShapeDtypeStruct((1, rows), I32),
        ],
        in_specs=[SMEM] * 2 + [VMEM] * 17,
        out_specs=[VMEM] * 4,
        scratch_shapes=[
            table,
            table,
            pltpu.VMEM((A_DEV, D), BF16),
            pltpu.VMEM((1, A_DEV), I32),
            pltpu.VMEM((GROUPS + WINDOW, D), F32),
        ],
        compiler_params=pltpu.CompilerParams(vmem_limit_bytes=36 * 2**20),
        name="join",
    )(view, core, *db, *b, *halves[0], *halves[1], received)
    other = lax.ppermute(peer, "keys_2", [(0, 1), (1, 0)])
    own = pl.pallas_call(
        own_kernel, out_shape=half, in_specs=[VMEM] * 3, out_specs=VMEM, name="join_own", compiler_params=LIMIT
    )(own, delta, place)
    return (own + other).astype(BF16)


def exchange(packed):
    blocks = packed.reshape(OWNERS, BLOCK, D)
    return lax.all_to_all(blocks, KEYS, 0, 0, tiled=True).reshape(OWNERS * BLOCK, D)


def shards(
    key_slot,
    a_slot,
    a_group,
    a_weight,
    a_payload,
    b_slot,
    b_weight,
    b_payload,
    da_key,
    da_group,
    da_mult,
    da_payload,
    da_count,
    db_key,
    db_mult,
    db_payload,
    db_count,
):
    me = lax.axis_index(KEYS).astype(I32).reshape(1)
    view = lax.axis_index("view").astype(I32).reshape(1)
    table = key_slot.reshape(128, 128)
    core = lax.axis_index("keys_2").astype(I32).reshape(1)
    db_out = pack(me, db_count, table, db_key, db_mult, None, db_payload)
    da_out = pack(me, da_count, table, da_key, da_mult, da_group, da_payload)
    db_in = exchange(db_out)
    da_in = exchange(da_out)
    b_parts = slices(
        sum_b_kernel, view, b_slot.reshape(32, 128), b_weight.reshape(32, 128), b_payload
    )
    b = everyone(own_total(b_parts))
    db = everyone(own_total(slices(sum_db_kernel, view, db_in)))
    halves = [sort(h, core, a_slot, a_group, a_weight, a_payload) for h in (0, 1)]
    partial = join(view, core, db, b, halves, da_in)
    blocks = partial.reshape(GROUPS // 2 // GROUPS_DEV, GROUPS_DEV, D)
    blocks = lax.all_to_all(blocks, ("keys_0", "keys_1", "view"), 0, 0, tiled=True)
    return jnp.sum(blocks.astype(F32), axis=0)


def solution(mesh):
    split = Mesh(
        mesh.devices.reshape(4, 4, 2, mesh.shape["view"]), ("keys_0", "keys_1", "keys_2", "view")
    )
    one, two = P(KEYS_VIEW), P(KEYS_VIEW, None)
    placed = (
        P(), one, one, one, two, one, one, two, one, one, one, two, one, one, one, two, one,
    )
    return jax.shard_map(shards, mesh=split, in_specs=placed, out_specs=two, check_vma=False)
```

time: 130 us -> 124 us (0.954)
  Pallas kernels: 44.3 us -> 26.5 us
  local copies, waits for them, and re-layouts: 1.81 us -> 14.1 us
  other arithmetic: 3.57 us -> 1.24 us
  waiting for transfers between devices: 22.2 us -> 19.9 us
  starting transfers between devices: 28.7 us -> 30.6 us
  blocking collectives: 27.3 us -> 28.9 us
    unnamed x22 -> x60, local copies, waits for them, and re-layouts: 1.81 us -> 14.1 us
    pallas_call x3 -> x4, Pallas kernels: 29.8 us -> 18.7 us  [the longest x1 11 us: join(): pl.pallas_call(join_kernel, out_shape=[half, half, jax.ShapeDtypeStruct((...]
    ppermute x12, waiting for transfers between devices: 8.63 us -> 3.44 us  [shift(): return lax.ppermute(x, 'view', [(j, (j + s) % 4) for j in range(4)])]
    pallas_call x2, Pallas kernels: 6.48 us -> 2.02 us  [slices(): pl.pallas_call(kernel, out_shape=[jax.ShapeDtypeStruct((128, D), F32)] *...]
    pallas_call x2, Pallas kernels: 8.06 us -> 5.77 us  [pack(): pl.pallas_call(lambda *refs: pack_kernel(group is not None, *refs), out_s...]
    ppermute x1, waiting for transfers between devices: 0.01 us -> 1.81 us  [join(): other = lax.ppermute(peer, 'keys_2', [(0, 1), (1, 0)])]
    ppermute x12, starting transfers between devices: 16.2 us -> 18 us  [shift(): return lax.ppermute(x, 'view', [(j, (j + s) % 4) for j in range(4)])]
    all_to_all x1, blocking collectives: 27.3 us -> 28.9 us  [shards(): lax.all_to_all(blocks, ('keys_0', 'keys_1', 'view'), 0, 0, tiled=True)]
  transfers between devices with their start and end apart: 15 -> 15, of which waited for: 3 -> 5; matrix products, arithmetic and copies ran while one was open for 1% -> 0% of each run, Pallas kernels for 21% -> 10%
where the time goes in v3:
time: 124 us; the launch traced here: 123 us
  starting transfers between devices  30.6 us (25%)
  blocking collectives  28.9 us (23%)
  Pallas kernels  26.5 us (21%)
  waiting for transfers between devices  19.9 us (16%)
  local copies, waits for them, and re-layouts  14.1 us (11%)
  between operations  1.6 us (1%)
  other arithmetic  1.24 us (1%)
    all_to_all x1, blocking collectives, shards(): lax.all_to_all(blocks, ('keys_0', 'keys_1', 'view'), 0, 0, tiled=True)  28.9 us
    ppermute x12, starting transfers between devices, shift(): return lax.ppermute(x, 'view', [(j, (j + s) % 4) for j in range(4)])  18 us
    all_to_all x2, waiting for transfers between devices, exchange(): lax.all_to_all(blocks, KEYS, 0, 0, tiled=True).reshape(OWNERS * BLOCK, D)  14.6 us
    unnamed x60, local copies, waits for them, and re-layouts  14.1 us
    all_to_all x2, starting transfers between devices, exchange(): lax.all_to_all(blocks, KEYS, 0, 0, tiled=True).reshape(OWNERS * BLOCK, D)  12.5 us
    pallas_call x1, Pallas kernels, join(): pl.pallas_call(join_kernel, out_shape=[half, half, jax.ShapeDtypeStruct((...  11 us
    pallas_call x2, Pallas kernels, pack(): pl.pallas_call(lambda *refs: pack_kernel(group is not None, *refs), out_s...  5.77 us
    pallas_call x2, Pallas kernels, sort(): pl.pallas_call(sort_kernel, out_shape=[jax.ShapeDtypeStruct((rows, D), BF...  5.32 us
  transfers between devices with their start and end apart: 15, of which 5 were waited for; matrix products, arithmetic and copies ran while one was open for 0% of the time, Pallas kernels for 10%

profile of v3, /device:TPU:0, one launch (start us, length us, event | category | flops | bytes accessed | tf_op | source)
XLA Modules:
  0.0 122.7 jit_solution(10771167018019271629)
XLA Ops:
  0.7 1.0 copy-done.2
  1.7 0.8 copy-done.4
  4.0 2.9 %pack_b.1 = bf16[2304,256]{1,0:T(8,128)(2,1)} custom-call(s32[1]{0:T(128)} %bitcast.2.refs_0_, s32[1]{0:T(128)S(6)} %copy.19.refs_1_, s32[128,128]{1,0:T(8,128)S(1)} %bitcast.21, s32[8,128]{1,0:T(8,128)S(1)} %bitcast.31, s32[8,128]{1,0:T(8,128)S(1)} %bitcast.32, bf16[1024,256]{1,0:T(8,128)(2,1)S(1)} %copy-done.2), custom_call_target="tpu_custom_call" | custom-call | tf_op jit(solution)/shard_map/pack_b/pallas_call | solution.py:111
  6.8 8.4 %all-to-all-start = ((bf16[32,72,256]{2,1,0:T(8,128)(2,1)}), bf16[32,72,256]{2,1,0:T(8,128)(2,1)S(1)}, u32[]{:S(2)}, u32[]{:S(2)}) async-start(bf16[32,72,256]{2,1,0:T(8,128)(2,1)} %bitcast.6), calls=%async_computation | async-start | bytes 2359296 | tf_op jit(solution)/shard_map/all_to_all | solution.py:325
  16.0 2.9 %pack_a.1 = bf16[2304,256]{1,0:T(8,128)(2,1)} custom-call(s32[1]{0:T(128)} %bitcast.2.refs_0_, s32[1]{0:T(128)S(6)} %copy.18.refs_1_, s32[128,128]{1,0:T(8,128)S(1)} %bitcast.22, s32[8,128]{1,0:T(8,128)S(1)} %bitcast.33, s32[8,128]{1,0:T(8,128)S(1)} %bitcast.34, s32[8,128]{1,0:T(8,128)S(1)} %bitcast.35, bf16[1024,256]{1,0:T(8,128)(2,1)S(1)} %copy-done.3), custom_call_target="tpu_custom_call" | custom-call | tf_op jit(solution)/shard_map/pack_a/pallas_call | solution.py:111
  18.9 14.6 %all-to-all-done = bf16[32,72,256]{2,1,0:T(8,128)(2,1)S(1)} async-done(((bf16[32,72,256]{2,1,0:T(8,128)(2,1)}), bf16[32,72,256]{2,1,0:T(8,128)(2,1)S(1)}, u32[]{:S(2)}, u32[]{:S(2)}) %all-to-all-start) | async-done | bytes 1179680 | tf_op jit(solution)/shard_map/all_to_all | solution.py:325
  33.5 4.0 %all-to-all-start.1 = ((bf16[32,72,256]{2,1,0:T(8,128)(2,1)}), bf16[32,72,256]{2,1,0:T(8,128)(2,1)S(1)}, u32[]{:S(2)}, u32[]{:S(2)}) async-start(bf16[32,72,256]{2,1,0:T(8,128)(2,1)} %bitcast.16), calls=%async_computation.1 | async-start | bytes 2359296 | tf_op jit(solution)/shard_map/all_to_all | solution.py:325
  37.6 1.6 %copy-done.1 = bf16[4096,256]{1,0:T(8,128)(2,1)S(1)} copy-done((bf16[4096,256]{1,0:T(8,128)(2,1)S(1)}, bf16[4096,256]{1,0:T(8,128)(2,1)}, u32[]{:S(2)}) %copy-start.1) | copy-done | bytes 2097176
  39.2 1.3 %shard_map.164 = (f32[128,256]{1,0:T(8,128)S(1)}, f32[128,256]{1,0:T(8,128)S(1)}, f32[128,256]{1,0:T(8,128)S(1)}, f32[128,256]{1,0:T(8,128)S(1)}) custom-call(s32[1]{0:T(128)} %bitcast.view_ref, s32[32,128]{1,0:T(8,128)S(1)} %bitcast.29, s32[32,128]{1,0:T(8,128)S(1)} %bitcast.30, bf16[4096,256]{1,0:T(8,128)(2,1)S(1)} %copy-done.1), custom_call_target="tpu_custom_call" | custom-call | tf_op jit(solution)/shard_map/pallas_call | solution.py:162
  40.5 1.6 %collective-permute-start.6 = (f32[128,256]{1,0:T(8,128)S(1)}, f32[128,256]{1,0:T(8,128)S(1)}, u32[]{:S(2)}, u32[]{:S(2)}) collective-permute-start(f32[128,256]{1,0:T(8,128)S(1)} %get-tuple-element.30), channel_id=1, source_target_pairs={{0,1},{1,2},{2,3},{3,0},{4,5},{5,6},{6,7},{7,4},{8,9},{9,10},{10,1... | collective-permute-start | bytes 393224 | tf_op jit(solution)/shard_map/ppermute | solution.py:173
  42.0 2.7 %collective-permute-start.7 = (f32[128,256]{1,0:T(8,128)S(1)}, f32[128,256]{1,0:T(8,128)S(1)}, u32[]{:S(2)}, u32[]{:S(2)}) collective-permute-start(f32[128,256]{1,0:T(8,128)S(1)} %get-tuple-element.31), channel_id=1, source_target_pairs={{0,2},{1,3},{2,0},{3,1},{4,6},{5,7},{6,4},{7,5},{8,10},{9,11},{10,... | collective-permute-start | bytes 393224 | tf_op jit(solution)/shard_map/ppermute | solution.py:173
  44.8 1.4 %collective-permute-start.8 = (f32[128,256]{1,0:T(8,128)S(1)}, f32[128,256]{1,0:T(8,128)S(1)}, u32[]{:S(2)}, u32[]{:S(2)}) collective-permute-start(f32[128,256]{1,0:T(8,128)S(1)} %get-tuple-element.32), channel_id=1, source_target_pairs={{0,3},{1,0},{2,1},{3,2},{4,7},{5,4},{6,5},{7,6},{8,11},{9,8},{10,9... | collective-permute-start | bytes 393224 | tf_op jit(solution)/shard_map/ppermute | solution.py:173
  46.2 0.7 shard_map.163
  47.6 0.9 collective-permute-start.1
  48.5 1.9 %collective-permute-start.2 = (f32[128,256]{1,0:T(8,128)S(1)}, f32[128,256]{1,0:T(8,128)S(1)}, u32[]{:S(2)}, u32[]{:S(2)}) collective-permute-start(f32[128,256]{1,0:T(8,128)S(1)} %get-tuple-element.28), channel_id=1, source_target_pairs={{0,3},{1,0},{2,1},{3,2},{4,7},{5,4},{6,5},{7,6},{8,11},{9,8},{10,9... | collective-permute-start | bytes 393224 | tf_op jit(solution)/shard_map/ppermute | solution.py:173
  50.4 1.5 %collective-permute-done.7 = f32[128,256]{1,0:T(8,128)S(1)} collective-permute-done((f32[128,256]{1,0:T(8,128)S(1)}, f32[128,256]{1,0:T(8,128)S(1)}, u32[]{:S(2)}, u32[]{:S(2)}) %collective-permute-start.7) | collective-permute-done | bytes 131104 | tf_op jit(solution)/shard_map/ppermute | solution.py:173
  51.9 3.2 %collective-permute-start.11 = (f32[128,256]{1,0:T(8,128)S(1)}, f32[128,256]{1,0:T(8,128)S(1)}, u32[]{:S(2)}, u32[]{:S(2)}) collective-permute-start(f32[128,256]{1,0:T(8,128)S(1)} %add_add_fusion.refs_4_), channel_id=1, source_target_pairs={{0,3},{1,0},{2,1},{3,2},{4,7},{5,4},{6,5},{7,6},{8,11},{9,8},{10,9... | collective-permute-start | bytes 393224 | tf_op jit(solution)/shard_map/ppermute | solution.py:173
  55.2 1.2 collective-permute-start.9
  56.8 1.4 %collective-permute-done.2 = f32[128,256]{1,0:T(8,128)S(1)} collective-permute-done((f32[128,256]{1,0:T(8,128)S(1)}, f32[128,256]{1,0:T(8,128)S(1)}, u32[]{:S(2)}, u32[]{:S(2)}) %collective-permute-start.2) | collective-permute-done | bytes 131104 | tf_op jit(solution)/shard_map/ppermute | solution.py:173
  58.3 1.2 collective-permute-start.5
  59.5 1.7 %collective-permute-start.4 = (f32[128,256]{1,0:T(8,128)S(1)}, f32[128,256]{1,0:T(8,128)}, u32[]{:S(2)}, u32[]{:S(2)}) collective-permute-start(f32[128,256]{1,0:T(8,128)S(1)} %add_add_fusion.1.refs_0_), channel_id=1, source_target_pairs={{0,2},{1,3},{2,0},{3,1},{4,6},{5,7},{6,4},{7,5},{8,10},{9,11},{10,... | collective-permute-start | bytes 393224 | tf_op jit(solution)/shard_map/ppermute | solution.py:173
  61.8 1.6 %collective-permute-start.3 = (f32[128,256]{1,0:T(8,128)S(1)}, f32[128,256]{1,0:T(8,128)}, u32[]{:S(2)}, u32[]{:S(2)}) collective-permute-start(f32[128,256]{1,0:T(8,128)S(1)} %add_add_fusion.1.refs_0_), channel_id=1, source_target_pairs={{0,1},{1,2},{2,3},{3,0},{4,5},{5,6},{6,7},{7,4},{8,9},{9,10},{10,1... | collective-permute-start | bytes 393224 | tf_op jit(solution)/shard_map/ppermute | solution.py:173
  63.4 2.7 %shard_map.166 = (bf16[2048,256]{1,0:T(8,128)(2,1)S(1)}, s32[1,2048]{1,0:T(1,128)S(1)}, s32[1,2048]{1,0:T(1,128)S(1)}, s32[1,2048]{1,0:T(1,128)S(1)}) custom-call(s32[1]{0:T(128)} %bitcast.1.core_ref, s32[32,128]{1,0:T(8,128)S(1)} %bitcast.23, s32[32,128]{1,0:T(8,128)S(1)} %bitcast.25, s32[32,128]{1,0:T(8,128)S(1)} %bitcast.27, bf16[4096,256]{1,0:T(8,128)(2,1)S(1)} %copy-done), custom_call_target="tpu_custom_call" | custom-call | tf_op jit(solution)/shard_map/pallas_call | solution.py:232
  66.1 2.7 %shard_map.165 = (bf16[2048,256]{1,0:T(8,128)(2,1)S(1)}, s32[1,2048]{1,0:T(1,128)S(1)}, s32[1,2048]{1,0:T(1,128)S(1)}, s32[1,2048]{1,0:T(1,128)S(1)}) custom-call(s32[1]{0:T(128)} %bitcast.1.core_ref, s32[32,128]{1,0:T(8,128)S(1)} %bitcast.24, s32[32,128]{1,0:T(8,128)S(1)} %bitcast.26, s32[32,128]{1,0:T(8,128)S(1)} %bitcast.28, bf16[4096,256]{1,0:T(8,128)(2,1)S(1)} %copy-done), custom_call_target="tpu_custom_call" | custom-call | tf_op jit(solution)/shard_map/pallas_call | solution.py:232
  71.9 0.9 copy-done.7
  72.8 0.9 copy-done.9
  73.7 0.9 copy-done.11
  77.4 11.0 %join.1 = (f32[2048,256]{1,0:T(8,128)S(1)}, f32[2048,256]{1,0:T(8,128)S(1)}, bf16[2048,256]{1,0:T(8,128)(2,1)S(1)}, s32[1,2048]{1,0:T(1,128)S(1)}) custom-call(s32[1]{0:T(128)} %bitcast.view_ref, s32[1]{0:T(128)} %bitcast.1.core_ref, f32[128,256]{1,0:T(8,128)S(1)} %add_add_fusion.1.refs_0_, f32[128,256]{1,0:T(8,128)} %collective-permute-done.3.refs_1_, ...), custom_call_target="tpu_custom_call" | custom-call | tf_op jit(solution)/shard_map/join/pallas_call | solution.py:296
  88.5 2.3 %join_own.1 = f32[2048,256]{1,0:T(8,128)S(1)} custom-call(f32[2048,256]{1,0:T(8,128)S(1)} %get-tuple-element.41.own_ref, bf16[2048,256]{1,0:T(8,128)(2,1)S(1)} %get-tuple-element.42.delta_ref, s32[1,2048]{1,0:T(1,128)S(1)} %get-tuple-element.43.place_ref), custom_call_target="tpu_custom_call" | custom-call | tf_op jit(solution)/shard_map/join_own/pallas_call | solution.py:317
  90.8 1.8 %collective-permute-done.12 = f32[2048,256]{1,0:T(8,128)S(1)} collective-permute-done((f32[2048,256]{1,0:T(8,128)S(1)}, f32[2048,256]{1,0:T(8,128)S(1)}, u32[]{:S(2)}, u32[]{:S(2)}) %collective-permute-start.12) | collective-permute-done | bytes 2097184 | tf_op jit(solution)/shard_map/ppermute | solution.py:316
  93.0 28.9 %all_to_all.15 = bf16[64,32,256]{2,1,0:T(8,128)(2,1)S(1)} all-to-all(bf16[64,32,256]{2,1,0:T(8,128)(2,1)S(1)} %bitcast.36), channel_id=1, replica_groups=mesh['keys_0'=4,'keys_1'=4,'keys_2'=2,'view'=4] {'keys_0','keys_1','view'}, dimensions={0} | all-to-all | bytes 2097152 | tf_op jit(solution)/shard_map/all_to_all | solution.py:363
  121.9 0.8 convert_reduce_fusion
  (71 shorter events, 9.7 us)
Async XLA Ops:
  0.0 16.0 %copy-start.28 = (s32[1024]{0:T(1024)S(1)}, s32[1024]{0:T(1024)}, u32[]{:S(2)}) copy-start(s32[1024]{0:T(1024)} %param.27) | copy-start | bytes 12292
  0.0 16.0 %copy-start.29 = (s32[1024]{0:T(1024)S(1)}, s32[1024]{0:T(1024)}, u32[]{:S(2)}) copy-start(s32[1024]{0:T(1024)} %param.26) | copy-start | bytes 12292
  0.0 16.0 %copy-start.27 = (s32[1024]{0:T(1024)S(1)}, s32[1024]{0:T(1024)}, u32[]{:S(2)}) copy-start(s32[1024]{0:T(1024)} %param.25) | copy-start | bytes 12292
  0.7 1.0 copy-start.2
  4.0 12.1 %copy-start.3 = (bf16[1024,256]{1,0:T(8,128)(2,1)S(1)}, bf16[1024,256]{1,0:T(8,128)(2,1)}, u32[]{:S(2)}) copy-start(bf16[1024,256]{1,0:T(8,128)(2,1)} %refs_6_.1) | copy-start | bytes 1572868
  4.0 12.1 %copy-start.5 = (s32[16384]{0:T(1024)S(1)}, s32[16384]{0:T(1024)}, u32[]{:S(2)}) copy-start(s32[16384]{0:T(1024)} %param.17) | copy-start | bytes 196612
  6.8 26.7 %all-to-all-start = ((bf16[32,72,256]{2,1,0:T(8,128)(2,1)}), bf16[32,72,256]{2,1,0:T(8,128)(2,1)S(1)}, u32[]{:S(2)}, u32[]{:S(2)}) async-start(bf16[32,72,256]{2,1,0:T(8,128)(2,1)} %bitcast.6), calls=%async_computation | async-start | bytes 2359296 | tf_op jit(solution)/shard_map/all_to_all | solution.py:325
  15.3 22.3 %copy-start.15 = (s32[4096]{0:T(1024)S(1)}, s32[4096]{0:T(1024)}, u32[]{:S(2)}) copy-start(s32[4096]{0:T(1024)} %param.22) | copy-start | bytes 49156
  15.3 22.3 %copy-start.16 = (s32[4096]{0:T(1024)S(1)}, s32[4096]{0:T(1024)}, u32[]{:S(2)}) copy-start(s32[4096]{0:T(1024)} %param.23) | copy-start | bytes 49156
  33.5 38.3 %all-to-all-start.1 = ((bf16[32,72,256]{2,1,0:T(8,128)(2,1)}), bf16[32,72,256]{2,1,0:T(8,128)(2,1)S(1)}, u32[]{:S(2)}, u32[]{:S(2)}) async-start(bf16[32,72,256]{2,1,0:T(8,128)(2,1)} %bitcast.16), calls=%async_computation.1 | async-start | bytes 2359296 | tf_op jit(solution)/shard_map/all_to_all | solution.py:325
  37.6 1.6 %copy-start.1 = (bf16[4096,256]{1,0:T(8,128)(2,1)S(1)}, bf16[4096,256]{1,0:T(8,128)(2,1)}, u32[]{:S(2)}) copy-start(bf16[4096,256]{1,0:T(8,128)(2,1)} %payload_ref.3) | copy-start | bytes 6291460
  39.2 24.2 %copy-start = (bf16[4096,256]{1,0:T(8,128)(2,1)S(1)}, bf16[4096,256]{1,0:T(8,128)(2,1)}, u32[]{:S(2)}) copy-start(bf16[4096,256]{1,0:T(8,128)(2,1)} %payload_ref.5) | copy-start | bytes 6291460
  39.2 24.2 %copy-start.12 = (s32[4096]{0:T(1024)S(1)}, s32[4096]{0:T(1024)}, u32[]{:S(2)}) copy-start(s32[4096]{0:T(1024)} %param.18) | copy-start | bytes 49156
  39.2 24.2 %copy-start.13 = (s32[4096]{0:T(1024)S(1)}, s32[4096]{0:T(1024)}, u32[]{:S(2)}) copy-start(s32[4096]{0:T(1024)} %param.19) | copy-start | bytes 49156
  39.2 24.2 %copy-start.14 = (s32[4096]{0:T(1024)S(1)}, s32[4096]{0:T(1024)}, u32[]{:S(2)}) copy-start(s32[4096]{0:T(1024)} %param.20) | copy-start | bytes 49156
  40.5 8.0 %collective-permute-start.6 = (f32[128,256]{1,0:T(8,128)S(1)}, f32[128,256]{1,0:T(8,128)S(1)}, u32[]{:S(2)}, u32[]{:S(2)}) collective-permute-start(f32[128,256]{1,0:T(8,128)S(1)} %get-tuple-element.30), channel_id=1, source_target_pairs={{0,1},{1,2},{2,3},{3,0},{4,5},{5,6},{6,7},{7,4},{8,9},{9,10},{10,1... | collective-permute-start | bytes 393224 | tf_op jit(solution)/shard_map/ppermute | solution.py:173
  42.0 9.9 %collective-permute-start.7 = (f32[128,256]{1,0:T(8,128)S(1)}, f32[128,256]{1,0:T(8,128)S(1)}, u32[]{:S(2)}, u32[]{:S(2)}) collective-permute-start(f32[128,256]{1,0:T(8,128)S(1)} %get-tuple-element.31), channel_id=1, source_target_pairs={{0,2},{1,3},{2,0},{3,1},{4,6},{5,7},{6,4},{7,5},{8,10},{9,11},{10,... | collective-permute-start | bytes 393224 | tf_op jit(solution)/shard_map/ppermute | solution.py:173
  44.8 7.2 %collective-permute-start.8 = (f32[128,256]{1,0:T(8,128)S(1)}, f32[128,256]{1,0:T(8,128)S(1)}, u32[]{:S(2)}, u32[]{:S(2)}) collective-permute-start(f32[128,256]{1,0:T(8,128)S(1)} %get-tuple-element.32), channel_id=1, source_target_pairs={{0,3},{1,0},{2,1},{3,2},{4,7},{5,4},{6,5},{7,6},{8,11},{9,8},{10,9... | collective-permute-start | bytes 393224 | tf_op jit(solution)/shard_map/ppermute | solution.py:173
  46.9 8.3 %collective-permute-start = (f32[128,256]{1,0:T(8,128)S(1)}, f32[128,256]{1,0:T(8,128)S(1)}, u32[]{:S(2)}, u32[]{:S(2)}) collective-permute-start(f32[128,256]{1,0:T(8,128)S(1)} %get-tuple-element.26), channel_id=1, source_target_pairs={{0,1},{1,2},{2,3},{3,0},{4,5},{5,6},{6,7},{7,4},{8,9},{9,10},{10,1... | collective-permute-start | bytes 393224 | tf_op jit(solution)/shard_map/ppermute | solution.py:173
  47.6 9.2 %collective-permute-start.1 = (f32[128,256]{1,0:T(8,128)S(1)}, f32[128,256]{1,0:T(8,128)S(1)}, u32[]{:S(2)}, u32[]{:S(2)}) collective-permute-start(f32[128,256]{1,0:T(8,128)S(1)} %get-tuple-element.27), channel_id=1, source_target_pairs={{0,2},{1,3},{2,0},{3,1},{4,6},{5,7},{6,4},{7,5},{8,10},{9,11},{10,... | collective-permute-start | bytes 393224 | tf_op jit(solution)/shard_map/ppermute | solution.py:173
  48.5 9.8 %collective-permute-start.2 = (f32[128,256]{1,0:T(8,128)S(1)}, f32[128,256]{1,0:T(8,128)S(1)}, u32[]{:S(2)}, u32[]{:S(2)}) collective-permute-start(f32[128,256]{1,0:T(8,128)S(1)} %get-tuple-element.28), channel_id=1, source_target_pairs={{0,3},{1,0},{2,1},{3,2},{4,7},{5,4},{6,5},{7,6},{8,11},{9,8},{10,9... | collective-permute-start | bytes 393224 | tf_op jit(solution)/shard_map/ppermute | solution.py:173
  51.9 9.2 %collective-permute-start.11 = (f32[128,256]{1,0:T(8,128)S(1)}, f32[128,256]{1,0:T(8,128)S(1)}, u32[]{:S(2)}, u32[]{:S(2)}) collective-permute-start(f32[128,256]{1,0:T(8,128)S(1)} %add_add_fusion.refs_4_), channel_id=1, source_target_pairs={{0,3},{1,0},{2,1},{3,2},{4,7},{5,4},{6,5},{7,6},{8,11},{9,8},{10,9... | collective-permute-start | bytes 393224 | tf_op jit(solution)/shard_map/ppermute | solution.py:173
  55.1 15.4 %collective-permute-start.10 = (f32[128,256]{1,0:T(8,128)S(1)}, f32[128,256]{1,0:T(8,128)S(1)}, u32[]{:S(2)}, u32[]{:S(2)}) collective-permute-start(f32[128,256]{1,0:T(8,128)S(1)} %add_add_fusion.refs_4_), channel_id=1, source_target_pairs={{0,2},{1,3},{2,0},{3,1},{4,6},{5,7},{6,4},{7,5},{8,10},{9,11},{10,... | collective-permute-start | bytes 393224 | tf_op jit(solution)/shard_map/ppermute | solution.py:173
  55.2 16.0 %collective-permute-start.9 = (f32[128,256]{1,0:T(8,128)S(1)}, f32[128,256]{1,0:T(8,128)S(1)}, u32[]{:S(2)}, u32[]{:S(2)}) collective-permute-start(f32[128,256]{1,0:T(8,128)S(1)} %add_add_fusion.refs_4_), channel_id=1, source_target_pairs={{0,1},{1,2},{2,3},{3,0},{4,5},{5,6},{6,7},{7,4},{8,9},{9,10},{10,1... | collective-permute-start | bytes 393224 | tf_op jit(solution)/shard_map/ppermute | solution.py:173
  58.3 13.6 %collective-permute-start.5 = (f32[128,256]{1,0:T(8,128)S(1)}, f32[128,256]{1,0:T(8,128)}, u32[]{:S(2)}, u32[]{:S(2)}) collective-permute-start(f32[128,256]{1,0:T(8,128)S(1)} %add_add_fusion.1.refs_0_), channel_id=1, source_target_pairs={{0,3},{1,0},{2,1},{3,2},{4,7},{5,4},{6,5},{7,6},{8,11},{9,8},{10,9... | collective-permute-start | bytes 393224 | tf_op jit(solution)/shard_map/ppermute | solution.py:173
  59.5 12.4 %collective-permute-start.4 = (f32[128,256]{1,0:T(8,128)S(1)}, f32[128,256]{1,0:T(8,128)}, u32[]{:S(2)}, u32[]{:S(2)}) collective-permute-start(f32[128,256]{1,0:T(8,128)S(1)} %add_add_fusion.1.refs_0_), channel_id=1, source_target_pairs={{0,2},{1,3},{2,0},{3,1},{4,6},{5,7},{6,4},{7,5},{8,10},{9,11},{10,... | collective-permute-start | bytes 393224 | tf_op jit(solution)/shard_map/ppermute | solution.py:173
  61.8 10.1 %collective-permute-start.3 = (f32[128,256]{1,0:T(8,128)S(1)}, f32[128,256]{1,0:T(8,128)}, u32[]{:S(2)}, u32[]{:S(2)}) collective-permute-start(f32[128,256]{1,0:T(8,128)S(1)} %add_add_fusion.1.refs_0_), channel_id=1, source_target_pairs={{0,1},{1,2},{2,3},{3,0},{4,5},{5,6},{6,7},{7,4},{8,9},{9,10},{10,1... | collective-permute-start | bytes 393224 | tf_op jit(solution)/shard_map/ppermute | solution.py:173
  66.1 4.5 %copy-start.17 = (s32[1,2048]{1,0:T(1,128)}, s32[1,2048]{1,0:T(1,128)S(1)}, u32[]{:S(2)}) copy-start(s32[1,2048]{1,0:T(1,128)S(1)} %get-tuple-element.40.refs_15_) | copy-start | bytes 24580
  71.9 0.9 copy-start.7
  72.8 0.9 copy-start.9
  73.7 0.9 copy-start.11
  88.4 4.2 %collective-permute-start.12 = (f32[2048,256]{1,0:T(8,128)S(1)}, f32[2048,256]{1,0:T(8,128)S(1)}, u32[]{:S(2)}, u32[]{:S(2)}) collective-permute-start(f32[2048,256]{1,0:T(8,128)S(1)} %get-tuple-element.44), channel_id=1, source_target_pairs={{0,4},{4,0},{1,5},{5,1},{2,6},{6,2},{3,7},{7,3},{8,12},{12,8},{9,1... | collective-permute-start | bytes 6291464 | tf_op jit(solution)/shard_map/ppermute | solution.py:316
  (13 other events, 8.7 us)

commit v4 on v3

--- a/solution.py
+++ b/solution.py
@@ -27,6 +27,11 @@
 TN = (((0,), (0,)), ((), ()))
 VMEM = pl.BlockSpec(memory_space=pltpu.VMEM)
 SMEM = pl.BlockSpec(memory_space=pltpu.SMEM)
+HBM = pl.BlockSpec(memory_space=pltpu.HBM)
+
+
+def in_hbm(x):
+    return pltpu.with_memory_space_constraint(x, pltpu.HBM)
 
 
 def dot(x, y, dims=NN):
@@ -110,12 +115,12 @@
     extra = [] if group is None else [group.reshape(8, 128)]
     return pl.pallas_call(
         lambda *refs: pack_kernel(group is not None, *refs),
-        out_shape=jax.ShapeDtypeStruct((OWNERS * BLOCK, D), BF16),
+        out_shape=pltpu.HBM((OWNERS * BLOCK, D), BF16),
         in_specs=[SMEM, SMEM] + [VMEM] * (4 + len(extra)),
         out_specs=VMEM,
         compiler_params=LIMIT,
         name="pack_a" if extra else "pack_b",
-    )(me, count, table, key.reshape(8, 128), mult.reshape(8, 128), *extra, payload)
+    )(me, count, *map(in_hbm, (table, key.reshape(8, 128), mult.reshape(8, 128), *extra, payload)))
 
 
 def fields_of(ref, c):
@@ -201,7 +206,7 @@
     return own + ((group >> 8) << 7) + (group & 127)
 
 
-def sort_kernel(core_ref, slot_ref, group_ref, weight_ref, payload_ref, out_ref, slots_ref, places_ref, weights_ref):
+def sort_kernel(core_ref, slot_ref, group_ref, weight_ref, payload_ref, out_ref, field_ref):
     for s in range(SORT_RUNS):
         rows = slice(8 * s, 8 * s + 8)
         slot, weight = flat(slot_ref[rows, :]), flat(weight_ref[rows, :])
@@ -221,46 +226,68 @@
             at = slice(512 * j + 256 * s, 512 * j + 256 * (s + 1))
             part = slice(256 * j, 256 * (j + 1))
             out_ref[at, :] = moved[part]
-            slots_ref[:, at] = fields[0:1, part] + 256 * fields[1:2, part]
-            weights_ref[:, at] = fields[2:3, part]
-            places_ref[:, at] = fields[3:4, part] + 256 * fields[4:5, part]
+            field_ref[:, at] = fields[:, part]
 
 
 def sort(h, core, slot, group, weight, payload):
     rows = SORT_RUNS * SORT
-    line = jax.ShapeDtypeStruct((1, rows), I32)
     return pl.pallas_call(
         sort_kernel,
-        out_shape=[jax.ShapeDtypeStruct((rows, D), BF16), line, line, line],
+        out_shape=[pltpu.HBM((rows, D), BF16), pltpu.HBM((8, rows), I32)],
         grid=(1,),
         in_specs=[SMEM] + [pl.BlockSpec((rows // 128, 128), lambda i: (h, 0))] * 3 + [pl.BlockSpec((rows, D), lambda i: (h, 0))],
-        out_specs=[VMEM] * 4,
+        out_specs=[VMEM] * 2,
         compiler_params=LIMIT,
     )(core, slot.reshape(32, 128), group.reshape(32, 128), weight.reshape(32, 128), payload)
 
 
 def join_kernel(view_ref, core_ref, *refs):
-    db, b, sorted_rows, in_ref = refs[:4], refs[4:8], (refs[8:12], refs[12:16]), refs[16]
-    peer_ref, own_ref, delta_ref, place_ref = refs[17:21]
-    table_ref, whole_ref, term_ref, line_ref, total_ref = refs[21:]
+    db, b, (first, second, fields0, fields1, in_ref) = refs[:4], refs[4:8], refs[8:13]
+    peer_ref, own_ref, delta_ref, place_ref = refs[13:17]
+    table_ref, whole_ref, sorted_ref, field_ref, line_ref, total_ref, sems = refs[17:]
+    copies = [
+        pltpu.make_async_copy(source, target, sems.at[n])
+        for n, (source, target) in enumerate(
+            (
+                (fields0, field_ref.at[0]),
+                (fields1, field_ref.at[1]),
+                (first, sorted_ref.at[0]),
+                (second, sorted_ref.at[1]),
+            )
+        )
+    ]
+    for copy in copies:
+        copy.start()
     view, core = view_ref[0], core_ref[0]
     fill(table_ref, view, lambda s: db[s][...])
     fill(whole_ref, view, lambda s: b[s][...] + db[s][...])
-    total_ref[...] = jnp.zeros_like(total_ref)
+    for c in range(8):
+        slot, group = fields_of(in_ref, c)
+        at = slice(256 * c, 256 * (c + 1))
+        place_ref[:, at] = place_of(group, core)
+        delta_ref[at, :] = terms_of(whole_ref, slot, None, payload_of(in_ref, c))
+    for g in range(GROUPS // 2 // 512):
+        chosen = onehot(512, place_ref[...] - 512 * g)
+        total_ref[512 * g : 512 * (g + 1), :] = dot(chosen, delta_ref[...])
+    total_ref[GROUPS // 2 :, :] = jnp.zeros((GROUPS // 2 + WINDOW, D), F32)
+    for copy in copies:
+        copy.wait()
     starts, ends = [], []
     for j in range(4):
-        for h, (payload_ref, slots_ref, places_ref, weights_ref) in enumerate(sorted_rows):
-            part, at = slice(512 * j, 512 * (j + 1)), slice(1024 * j + 512 * h, 1024 * j + 512 * (h + 1))
-            term_ref[at, :] = terms_of(table_ref, slots_ref[:, part], weights_ref[:, part].astype(F32), payload_ref[part, :])
-            line_ref[:, at] = places_ref[:, part]
-        line = line_ref[:, 1024 * j : 1024 * (j + 1)]
+        for h in range(2):
+            part, at = slice(512 * j, 512 * (j + 1)), slice(512 * h, 512 * (h + 1))
+            fields = field_ref[h, :, part]
+            slot = fields[0:1] + 256 * fields[1:2]
+            sorted_ref[h, part, :] = terms_of(table_ref, slot, fields[2:3].astype(F32), sorted_ref[h, part, :])
+            line_ref[j : j + 1, at] = fields[3:4] + 256 * fields[4:5]
+        line = line_ref[j : j + 1, :]
         starts.append(pl.multiple_of((jnp.min(line) >> 6) << 6, 64))
         ends.append(jnp.max(line))
 
     def window(j, start):
-        rows = slice(1024 * j, 1024 * (j + 1))
-        chosen = onehot(WINDOW, line_ref[:, rows] - start)
-        total_ref[pl.ds(start, WINDOW), :] += dot(chosen, term_ref[rows, :])
+        chosen = onehot(WINDOW, line_ref[j : j + 1, :] - start)
+        rows = sorted_ref[:, 512 * j : 512 * (j + 1), :].reshape(1024, D)
+        total_ref[pl.ds(start, WINDOW), :] += dot(chosen, rows)
 
     for j in range(4):
         window(j, starts[j])
@@ -270,15 +297,7 @@
             return carry
 
         lax.fori_loop(1, (ends[j] - starts[j]) // WINDOW + 1, more, 0)
-    for c in range(8):
-        slot, group = fields_of(in_ref, c)
-        at = slice(256 * c, 256 * (c + 1))
-        place_ref[:, at] = place_of(group, core)
-        delta_ref[at, :] = terms_of(whole_ref, slot, None, payload_of(in_ref, c))
-    for g in range(GROUPS // 2 // 512):
-        at = slice(512 * g, 512 * (g + 1))
-        chosen = onehot(512, place_ref[...] - 512 * g)
-        peer_ref[at, :] = total_ref[at, :] + dot(chosen, delta_ref[...])
+    peer_ref[...] = total_ref[: GROUPS // 2, :]
     own_ref[...] = total_ref[GROUPS // 2 : GROUPS, :]
 
 
@@ -301,18 +320,20 @@
             jax.ShapeDtypeStruct((rows, D), BF16),
             jax.ShapeDtypeStruct((1, rows), I32),
         ],
-        in_specs=[SMEM] * 2 + [VMEM] * 17,
+        in_specs=[SMEM] * 2 + [VMEM] * 8 + [HBM] * 4 + [VMEM],
         out_specs=[VMEM] * 4,
         scratch_shapes=[
             table,
             table,
-            pltpu.VMEM((A_DEV, D), BF16),
-            pltpu.VMEM((1, A_DEV), I32),
+            pltpu.VMEM((2, A_DEV // 2, D), BF16),
+            pltpu.VMEM((2, 8, A_DEV // 2), I32),
+            pltpu.VMEM((4, 1024), I32),
             pltpu.VMEM((GROUPS + WINDOW, D), F32),
+            pltpu.SemaphoreType.DMA((4,)),
         ],
-        compiler_params=pltpu.CompilerParams(vmem_limit_bytes=36 * 2**20),
+        compiler_params=pltpu.CompilerParams(vmem_limit_bytes=32 * 2**20),
         name="join",
-    )(view, core, *db, *b, *halves[0], *halves[1], received)
+    )(view, core, *db, *b, *(in_hbm(half[i]) for i in (0, 1) for half in halves), received)
     other = lax.ppermute(peer, "keys_2", [(0, 1), (1, 0)])
     own = pl.pallas_call(
         own_kernel, out_shape=half, in_specs=[VMEM] * 3, out_specs=VMEM, name="join_own", compiler_params=LIMIT
@@ -350,7 +371,7 @@
     core = lax.axis_index("keys_2").astype(I32).reshape(1)
     db_out = pack(me, db_count, table, db_key, db_mult, None, db_payload)
     da_out = pack(me, da_count, table, da_key, da_mult, da_group, da_payload)
-    db_in = exchange(db_out)
+    db_in = in_hbm(exchange(db_out))
     da_in = exchange(da_out)
     b_parts = slices(
         sum_b_kernel, view, b_slot.reshape(32, 128), b_weight.reshape(32, 128), b_payload

time: 124 us -> 115 us (0.927)
  local copies, waits for them, and re-layouts: 14.1 us -> 1.06 us
  Pallas kernels: 26.5 us -> 32 us
  starting transfers between devices: 30.6 us -> 29.2 us
    unnamed x60 -> x16, local copies, waits for them, and re-layouts: 14.1 us -> 1.06 us
    pallas_call x2, Pallas kernels: 5.77 us -> 8 us  [pack(): pl.pallas_call(lambda *refs: pack_kernel(group is not None, *refs), out_s...]
    pallas_call x2, Pallas kernels: 5.32 us -> 7.3 us  [sort(): pl.pallas_call(sort_kernel, out_shape=[pltpu.HBM((rows, D), BF16), pltpu....]
    ppermute x12, waiting for transfers between devices: 3.44 us -> 5.06 us  [shift(): return lax.ppermute(x, 'view', [(j, (j + s) % 4) for j in range(4)])]
    ppermute x12, starting transfers between devices: 18 us -> 16.7 us  [shift(): return lax.ppermute(x, 'view', [(j, (j + s) % 4) for j in range(4)])]
    pallas_call x2, Pallas kernels: 2.02 us -> 3.29 us  [slices(): pl.pallas_call(kernel, out_shape=[jax.ShapeDtypeStruct((128, D), F32)] *...]
  transfers between devices with their start and end apart: 15 -> 15, of which waited for: 5 -> 4; matrix products, arithmetic and copies ran while one was open for 0% -> 0% of each run, Pallas kernels for 10% -> 15%
where the time goes in v4:
time: 115 us; the launch traced here: 114 us
  Pallas kernels  32 us (28%)
  starting transfers between devices  29.2 us (25%)
  blocking collectives  28.8 us (25%)
  waiting for transfers between devices  20.3 us (18%)
  between operations  1.65 us (1%)
  other arithmetic  1.24 us (1%)
    all_to_all x1, blocking collectives, shards(): lax.all_to_all(blocks, ('keys_0', 'keys_1', 'view'), 0, 0, tiled=True)  28.8 us
    ppermute x12, starting transfers between devices, shift(): return lax.ppermute(x, 'view', [(j, (j + s) % 4) for j in range(4)])  16.7 us
    all_to_all x2, waiting for transfers between devices, exchange(): lax.all_to_all(blocks, KEYS, 0, 0, tiled=True).reshape(OWNERS * BLOCK, D)  13.4 us
    all_to_all x2, starting transfers between devices, exchange(): lax.all_to_all(blocks, KEYS, 0, 0, tiled=True).reshape(OWNERS * BLOCK, D)  12.4 us
    pallas_call x1, Pallas kernels, join(): pl.pallas_call(join_kernel, out_shape=[half, half, jax.ShapeDtypeStruct((...  11.1 us
    pallas_call x2, Pallas kernels, pack(): pl.pallas_call(lambda *refs: pack_kernel(group is not None, *refs), out_s...  8 us
    pallas_call x2, Pallas kernels, sort(): pl.pallas_call(sort_kernel, out_shape=[pltpu.HBM((rows, D), BF16), pltpu....  7.3 us
    ppermute x12, waiting for transfers between devices, shift(): return lax.ppermute(x, 'view', [(j, (j + s) % 4) for j in range(4)])  5.06 us
  transfers between devices with their start and end apart: 15, of which 4 were waited for; matrix products, arithmetic and copies ran while one was open for 0% of the time, Pallas kernels for 15%

profile of v4, /device:TPU:0, one launch (start us, length us, event | category | flops | bytes accessed | tf_op | source)
XLA Modules:
  0.0 114.2 jit_solution(3248456314313716088)
XLA Ops:
  0.7 4.0 %pack_b.1 = bf16[2304,256]{1,0:T(8,128)(2,1)} custom-call(s32[1]{0:T(128)} %bitcast.2.refs_0_, s32[1]{0:T(128)S(6)} %copy.19.refs_1_, s32[128,128]{1,0:T(8,128)} %bitcast.32, s32[8,128]{1,0:T(8,128)} %bitcast.34, s32[8,128]{1,0:T(8,128)} %bitcast.35, bf16[1024,256]{1,0:T(8,128)(2,1)} %refs_5_.1), custom_call_target="tpu_custom_call" | custom-call | tf_op jit(solution)/shard_map/pack_b/pallas_call | solution.py:116
  4.6 8.4 %all-to-all-start = ((bf16[32,72,256]{2,1,0:T(8,128)(2,1)}), bf16[32,72,256]{2,1,0:T(8,128)(2,1)S(1)}, u32[]{:S(2)}, u32[]{:S(2)}) async-start(bf16[32,72,256]{2,1,0:T(8,128)(2,1)} %bitcast.30), calls=%async_computation | async-start | bytes 2359296 | tf_op jit(solution)/shard_map/all_to_all | solution.py:346
  13.1 0.0 copy-start.1
  13.9 4.0 %pack_a.1 = bf16[2304,256]{1,0:T(8,128)(2,1)} custom-call(s32[1]{0:T(128)} %bitcast.2.refs_0_, s32[1]{0:T(128)S(6)} %copy.18.refs_1_, s32[128,128]{1,0:T(8,128)} %bitcast.33, s32[8,128]{1,0:T(8,128)} %bitcast.36, s32[8,128]{1,0:T(8,128)} %bitcast.37, s32[8,128]{1,0:T(8,128)} %bitcast.38, bf16[1024,256]{1,0:T(8,128)(2,1)} %refs_6_.1), custom_call_target="tpu_custom_call" | custom-call | tf_op jit(solution)/shard_map/pack_a/pallas_call | solution.py:116
  17.9 13.4 %all-to-all-done = bf16[32,72,256]{2,1,0:T(8,128)(2,1)S(1)} async-done(((bf16[32,72,256]{2,1,0:T(8,128)(2,1)}), bf16[32,72,256]{2,1,0:T(8,128)(2,1)S(1)}, u32[]{:S(2)}, u32[]{:S(2)}) %all-to-all-start) | async-done | bytes 1179680 | tf_op jit(solution)/shard_map/all_to_all | solution.py:346
  31.3 1.0 copy-done.7
  32.3 4.0 %all-to-all-start.1 = ((bf16[32,72,256]{2,1,0:T(8,128)(2,1)}), bf16[32,72,256]{2,1,0:T(8,128)(2,1)S(1)}, u32[]{:S(2)}, u32[]{:S(2)}) async-start(bf16[32,72,256]{2,1,0:T(8,128)(2,1)} %bitcast.28), calls=%async_computation.1 | async-start | bytes 2359296 | tf_op jit(solution)/shard_map/all_to_all | solution.py:346
  36.4 0.0 copy-start.3
  36.4 0.0 copy-start.4
  36.4 1.3 %shard_map.164 = (f32[128,256]{1,0:T(8,128)S(1)}, f32[128,256]{1,0:T(8,128)S(1)}, f32[128,256]{1,0:T(8,128)S(1)}, f32[128,256]{1,0:T(8,128)S(1)}) custom-call(s32[1]{0:T(128)} %bitcast.view_ref, s32[32,128]{1,0:T(8,128)S(1)} %bitcast.26, s32[32,128]{1,0:T(8,128)S(1)} %bitcast.27, bf16[4096,256]{1,0:T(8,128)(2,1)S(1)} %copy-done.1), custom_call_target="tpu_custom_call" | custom-call | tf_op jit(solution)/shard_map/pallas_call | solution.py:167
  37.7 1.6 %collective-permute-start.6 = (f32[128,256]{1,0:T(8,128)S(1)}, f32[128,256]{1,0:T(8,128)S(1)}, u32[]{:S(2)}, u32[]{:S(2)}) collective-permute-start(f32[128,256]{1,0:T(8,128)S(1)} %get-tuple-element.26), channel_id=1, source_target_pairs={{0,1},{1,2},{2,3},{3,0},{4,5},{5,6},{6,7},{7,4},{8,9},{9,10},{10,1... | collective-permute-start | bytes 393224 | tf_op jit(solution)/shard_map/ppermute | solution.py:178
  39.3 2.7 %collective-permute-start.7 = (f32[128,256]{1,0:T(8,128)S(1)}, f32[128,256]{1,0:T(8,128)S(1)}, u32[]{:S(2)}, u32[]{:S(2)}) collective-permute-start(f32[128,256]{1,0:T(8,128)S(1)} %get-tuple-element.27), channel_id=1, source_target_pairs={{0,2},{1,3},{2,0},{3,1},{4,6},{5,7},{6,4},{7,5},{8,10},{9,11},{10,... | collective-permute-start | bytes 393224 | tf_op jit(solution)/shard_map/ppermute | solution.py:178
  42.0 1.4 %collective-permute-start.8 = (f32[128,256]{1,0:T(8,128)S(1)}, f32[128,256]{1,0:T(8,128)S(1)}, u32[]{:S(2)}, u32[]{:S(2)}) collective-permute-start(f32[128,256]{1,0:T(8,128)S(1)} %get-tuple-element.28), channel_id=1, source_target_pairs={{0,3},{1,0},{2,1},{3,2},{4,7},{5,4},{6,5},{7,6},{8,11},{9,8},{10,9... | collective-permute-start | bytes 393224 | tf_op jit(solution)/shard_map/ppermute | solution.py:178
  43.5 2.0 %shard_map.163 = (f32[128,256]{1,0:T(8,128)S(1)}, f32[128,256]{1,0:T(8,128)S(1)}, f32[128,256]{1,0:T(8,128)S(1)}, f32[128,256]{1,0:T(8,128)S(1)}) custom-call(s32[1]{0:T(128)} %bitcast.view_ref, bf16[2304,256]{1,0:T(8,128)(2,1)} %bitcast.29), custom_call_target="tpu_custom_call" | custom-call | tf_op jit(solution)/shard_map/pallas_call | solution.py:167
  45.5 0.7 collective-permute-start
  46.1 0.9 collective-permute-start.1
  47.0 1.9 %collective-permute-start.2 = (f32[128,256]{1,0:T(8,128)S(1)}, f32[128,256]{1,0:T(8,128)S(1)}, u32[]{:S(2)}, u32[]{:S(2)}) collective-permute-start(f32[128,256]{1,0:T(8,128)S(1)} %get-tuple-element.24), channel_id=1, source_target_pairs={{0,3},{1,0},{2,1},{3,2},{4,7},{5,4},{6,5},{7,6},{8,11},{9,8},{10,9... | collective-permute-start | bytes 393224 | tf_op jit(solution)/shard_map/ppermute | solution.py:178
  48.9 0.3 collective-permute-done.7
  49.2 1.6 %collective-permute-start.11 = (f32[128,256]{1,0:T(8,128)S(1)}, f32[128,256]{1,0:T(8,128)S(1)}, u32[]{:S(2)}, u32[]{:S(2)}) collective-permute-start(f32[128,256]{1,0:T(8,128)S(1)} %add_add_fusion.refs_4_), channel_id=1, source_target_pairs={{0,3},{1,0},{2,1},{3,2},{4,7},{5,4},{6,5},{7,6},{8,11},{9,8},{10,9... | collective-permute-start | bytes 393224 | tf_op jit(solution)/shard_map/ppermute | solution.py:178
  50.8 1.3 %collective-permute-start.10 = (f32[128,256]{1,0:T(8,128)S(1)}, f32[128,256]{1,0:T(8,128)S(1)}, u32[]{:S(2)}, u32[]{:S(2)}) collective-permute-start(f32[128,256]{1,0:T(8,128)S(1)} %add_add_fusion.refs_4_), channel_id=1, source_target_pairs={{0,2},{1,3},{2,0},{3,1},{4,6},{5,7},{6,4},{7,5},{8,10},{9,11},{10,... | collective-permute-start | bytes 393224 | tf_op jit(solution)/shard_map/ppermute | solution.py:178
  52.1 4.8 %collective-permute-done = f32[128,256]{1,0:T(8,128)S(1)} collective-permute-done((f32[128,256]{1,0:T(8,128)S(1)}, f32[128,256]{1,0:T(8,128)S(1)}, u32[]{:S(2)}, u32[]{:S(2)}) %collective-permute-start) | collective-permute-done | bytes 131104 | tf_op jit(solution)/shard_map/ppermute | solution.py:178
  56.9 3.3 %collective-permute-start.5 = (f32[128,256]{1,0:T(8,128)S(1)}, f32[128,256]{1,0:T(8,128)S(1)}, u32[]{:S(2)}, u32[]{:S(2)}) collective-permute-start(f32[128,256]{1,0:T(8,128)S(1)} %add_add_fusion.1.refs_0_), channel_id=1, source_target_pairs={{0,3},{1,0},{2,1},{3,2},{4,7},{5,4},{6,5},{7,6},{8,11},{9,8},{10,9... | collective-permute-start | bytes 393224 | tf_op jit(solution)/shard_map/ppermute | solution.py:178
  60.2 1.3 %collective-permute-start.3 = (f32[128,256]{1,0:T(8,128)S(1)}, f32[128,256]{1,0:T(8,128)S(1)}, u32[]{:S(2)}, u32[]{:S(2)}) collective-permute-start(f32[128,256]{1,0:T(8,128)S(1)} %add_add_fusion.1.refs_0_), channel_id=1, source_target_pairs={{0,1},{1,2},{2,3},{3,0},{4,5},{5,6},{6,7},{7,4},{8,9},{9,10},{10,1... | collective-permute-start | bytes 393224 | tf_op jit(solution)/shard_map/ppermute | solution.py:178
  61.6 3.7 %shard_map.166 = (bf16[2048,256]{1,0:T(8,128)(2,1)}, s32[8,2048]{1,0:T(8,128)}) custom-call(s32[1]{0:T(128)} %bitcast.1.core_ref, s32[32,128]{1,0:T(8,128)S(1)} %bitcast.20, s32[32,128]{1,0:T(8,128)S(1)} %bitcast.22, s32[32,128]{1,0:T(8,128)S(1)} %bitcast.24, bf16[4096,256]{1,0:T(8,128)(2,1)S(1)} %copy-done), custom_call_target="tpu_custom_call" | custom-call | tf_op jit(solution)/shard_map/pallas_call | solution.py:234
  65.3 3.6 %shard_map.165 = (bf16[2048,256]{1,0:T(8,128)(2,1)}, s32[8,2048]{1,0:T(8,128)}) custom-call(s32[1]{0:T(128)} %bitcast.1.core_ref, s32[32,128]{1,0:T(8,128)S(1)} %bitcast.21, s32[32,128]{1,0:T(8,128)S(1)} %bitcast.23, s32[32,128]{1,0:T(8,128)S(1)} %bitcast.25, bf16[4096,256]{1,0:T(8,128)(2,1)S(1)} %copy-done), custom_call_target="tpu_custom_call" | custom-call | tf_op jit(solution)/shard_map/pallas_call | solution.py:234
  68.9 11.1 %join.1 = (f32[2048,256]{1,0:T(8,128)S(1)}, f32[2048,256]{1,0:T(8,128)S(1)}, bf16[2048,256]{1,0:T(8,128)(2,1)S(1)}, s32[1,2048]{1,0:T(1,128)S(1)}) custom-call(s32[1]{0:T(128)} %bitcast.view_ref, s32[1]{0:T(128)} %bitcast.1.core_ref, f32[128,256]{1,0:T(8,128)S(1)} %add_add_fusion.1.refs_0_, f32[128,256]{1,0:T(8,128)S(1)} %collective-permute-done.3.refs_1_, ...), custom_call_target="tpu_custom_call" | custom-call | tf_op jit(solution)/shard_map/join/pallas_call | solution.py:315
  80.0 0.1 collective-permute-start.12
  80.1 2.3 %join_own.1 = f32[2048,256]{1,0:T(8,128)S(1)} custom-call(f32[2048,256]{1,0:T(8,128)S(1)} %get-tuple-element.33.own_ref, bf16[2048,256]{1,0:T(8,128)(2,1)S(1)} %get-tuple-element.34.delta_ref, s32[1,2048]{1,0:T(1,128)S(1)} %get-tuple-element.35.place_ref), custom_call_target="tpu_custom_call" | custom-call | tf_op jit(solution)/shard_map/join_own/pallas_call | solution.py:338
  82.4 1.8 %collective-permute-done.12 = f32[2048,256]{1,0:T(8,128)S(1)} collective-permute-done((f32[2048,256]{1,0:T(8,128)S(1)}, f32[2048,256]{1,0:T(8,128)S(1)}, u32[]{:S(2)}, u32[]{:S(2)}) %collective-permute-start.12) | collective-permute-done | bytes 2097184 | tf_op jit(solution)/shard_map/ppermute | solution.py:337
  84.2 0.4 add_convert_fusion
  84.6 28.8 %all_to_all.15 = bf16[64,32,256]{2,1,0:T(8,128)(2,1)S(1)} all-to-all(bf16[64,32,256]{2,1,0:T(8,128)(2,1)S(1)} %bitcast.31), channel_id=1, replica_groups=mesh['keys_0'=4,'keys_1'=4,'keys_2'=2,'view'=4] {'keys_0','keys_1','view'}, dimensions={0} | all-to-all | bytes 2097152 | tf_op jit(solution)/shard_map/all_to_all | solution.py:384
  113.5 0.8 convert_reduce_fusion
  (27 shorter events, 0.1 us)
Async XLA Ops:
  4.6 26.7 %all-to-all-start = ((bf16[32,72,256]{2,1,0:T(8,128)(2,1)}), bf16[32,72,256]{2,1,0:T(8,128)(2,1)S(1)}, u32[]{:S(2)}, u32[]{:S(2)}) async-start(bf16[32,72,256]{2,1,0:T(8,128)(2,1)} %bitcast.30), calls=%async_computation | async-start | bytes 2359296 | tf_op jit(solution)/shard_map/all_to_all | solution.py:346
  13.1 23.3 %copy-start.1 = (bf16[4096,256]{1,0:T(8,128)(2,1)S(1)}, bf16[4096,256]{1,0:T(8,128)(2,1)}, u32[]{:S(2)}) copy-start(bf16[4096,256]{1,0:T(8,128)(2,1)} %payload_ref.3) | copy-start | bytes 6291460
  13.1 23.3 %copy-start.5 = (s32[4096]{0:T(1024)S(1)}, s32[4096]{0:T(1024)}, u32[]{:S(2)}) copy-start(s32[4096]{0:T(1024)} %param.22) | copy-start | bytes 49156
  13.1 23.3 %copy-start.6 = (s32[4096]{0:T(1024)S(1)}, s32[4096]{0:T(1024)}, u32[]{:S(2)}) copy-start(s32[4096]{0:T(1024)} %param.23) | copy-start | bytes 49156
  31.3 1.0 copy-start.7
  32.3 36.6 %all-to-all-start.1 = ((bf16[32,72,256]{2,1,0:T(8,128)(2,1)}), bf16[32,72,256]{2,1,0:T(8,128)(2,1)S(1)}, u32[]{:S(2)}, u32[]{:S(2)}) async-start(bf16[32,72,256]{2,1,0:T(8,128)(2,1)} %bitcast.28), calls=%async_computation.1 | async-start | bytes 2359296 | tf_op jit(solution)/shard_map/all_to_all | solution.py:346
  36.4 25.2 %copy-start = (bf16[4096,256]{1,0:T(8,128)(2,1)S(1)}, bf16[4096,256]{1,0:T(8,128)(2,1)}, u32[]{:S(2)}) copy-start(bf16[4096,256]{1,0:T(8,128)(2,1)} %payload_ref.5) | copy-start | bytes 6291460
  36.4 25.2 %copy-start.2 = (s32[4096]{0:T(1024)S(1)}, s32[4096]{0:T(1024)}, u32[]{:S(2)}) copy-start(s32[4096]{0:T(1024)} %param.18) | copy-start | bytes 49156
  36.4 25.2 %copy-start.3 = (s32[4096]{0:T(1024)S(1)}, s32[4096]{0:T(1024)}, u32[]{:S(2)}) copy-start(s32[4096]{0:T(1024)} %param.19) | copy-start | bytes 49156
  36.4 25.2 %copy-start.4 = (s32[4096]{0:T(1024)S(1)}, s32[4096]{0:T(1024)}, u32[]{:S(2)}) copy-start(s32[4096]{0:T(1024)} %param.20) | copy-start | bytes 49156
  37.7 9.3 %collective-permute-start.6 = (f32[128,256]{1,0:T(8,128)S(1)}, f32[128,256]{1,0:T(8,128)S(1)}, u32[]{:S(2)}, u32[]{:S(2)}) collective-permute-start(f32[128,256]{1,0:T(8,128)S(1)} %get-tuple-element.26), channel_id=1, source_target_pairs={{0,1},{1,2},{2,3},{3,0},{4,5},{5,6},{6,7},{7,4},{8,9},{9,10},{10,1... | collective-permute-start | bytes 393224 | tf_op jit(solution)/shard_map/ppermute | solution.py:178
  39.3 9.9 %collective-permute-start.7 = (f32[128,256]{1,0:T(8,128)S(1)}, f32[128,256]{1,0:T(8,128)S(1)}, u32[]{:S(2)}, u32[]{:S(2)}) collective-permute-start(f32[128,256]{1,0:T(8,128)S(1)} %get-tuple-element.27), channel_id=1, source_target_pairs={{0,2},{1,3},{2,0},{3,1},{4,6},{5,7},{6,4},{7,5},{8,10},{9,11},{10,... | collective-permute-start | bytes 393224 | tf_op jit(solution)/shard_map/ppermute | solution.py:178
  42.0 7.2 %collective-permute-start.8 = (f32[128,256]{1,0:T(8,128)S(1)}, f32[128,256]{1,0:T(8,128)S(1)}, u32[]{:S(2)}, u32[]{:S(2)}) collective-permute-start(f32[128,256]{1,0:T(8,128)S(1)} %get-tuple-element.28), channel_id=1, source_target_pairs={{0,3},{1,0},{2,1},{3,2},{4,7},{5,4},{6,5},{7,6},{8,11},{9,8},{10,9... | collective-permute-start | bytes 393224 | tf_op jit(solution)/shard_map/ppermute | solution.py:178
  45.5 11.4 %collective-permute-start = (f32[128,256]{1,0:T(8,128)S(1)}, f32[128,256]{1,0:T(8,128)S(1)}, u32[]{:S(2)}, u32[]{:S(2)}) collective-permute-start(f32[128,256]{1,0:T(8,128)S(1)} %get-tuple-element.22), channel_id=1, source_target_pairs={{0,1},{1,2},{2,3},{3,0},{4,5},{5,6},{6,7},{7,4},{8,9},{9,10},{10,1... | collective-permute-start | bytes 393224 | tf_op jit(solution)/shard_map/ppermute | solution.py:178
  46.1 10.8 %collective-permute-start.1 = (f32[128,256]{1,0:T(8,128)S(1)}, f32[128,256]{1,0:T(8,128)S(1)}, u32[]{:S(2)}, u32[]{:S(2)}) collective-permute-start(f32[128,256]{1,0:T(8,128)S(1)} %get-tuple-element.23), channel_id=1, source_target_pairs={{0,2},{1,3},{2,0},{3,1},{4,6},{5,7},{6,4},{7,5},{8,10},{9,11},{10,... | collective-permute-start | bytes 393224 | tf_op jit(solution)/shard_map/ppermute | solution.py:178
  47.0 9.9 %collective-permute-start.2 = (f32[128,256]{1,0:T(8,128)S(1)}, f32[128,256]{1,0:T(8,128)S(1)}, u32[]{:S(2)}, u32[]{:S(2)}) collective-permute-start(f32[128,256]{1,0:T(8,128)S(1)} %get-tuple-element.24), channel_id=1, source_target_pairs={{0,3},{1,0},{2,1},{3,2},{4,7},{5,4},{6,5},{7,6},{8,11},{9,8},{10,9... | collective-permute-start | bytes 393224 | tf_op jit(solution)/shard_map/ppermute | solution.py:178
  49.2 11.0 %collective-permute-start.11 = (f32[128,256]{1,0:T(8,128)S(1)}, f32[128,256]{1,0:T(8,128)S(1)}, u32[]{:S(2)}, u32[]{:S(2)}) collective-permute-start(f32[128,256]{1,0:T(8,128)S(1)} %add_add_fusion.refs_4_), channel_id=1, source_target_pairs={{0,3},{1,0},{2,1},{3,2},{4,7},{5,4},{6,5},{7,6},{8,11},{9,8},{10,9... | collective-permute-start | bytes 393224 | tf_op jit(solution)/shard_map/ppermute | solution.py:178
  50.8 18.0 %collective-permute-start.10 = (f32[128,256]{1,0:T(8,128)S(1)}, f32[128,256]{1,0:T(8,128)S(1)}, u32[]{:S(2)}, u32[]{:S(2)}) collective-permute-start(f32[128,256]{1,0:T(8,128)S(1)} %add_add_fusion.refs_4_), channel_id=1, source_target_pairs={{0,2},{1,3},{2,0},{3,1},{4,6},{5,7},{6,4},{7,5},{8,10},{9,11},{10,... | collective-permute-start | bytes 393224 | tf_op jit(solution)/shard_map/ppermute | solution.py:178
  56.9 12.0 %collective-permute-start.9 = (f32[128,256]{1,0:T(8,128)S(1)}, f32[128,256]{1,0:T(8,128)S(1)}, u32[]{:S(2)}, u32[]{:S(2)}) collective-permute-start(f32[128,256]{1,0:T(8,128)S(1)} %add_add_fusion.refs_4_), channel_id=1, source_target_pairs={{0,1},{1,2},{2,3},{3,0},{4,5},{5,6},{6,7},{7,4},{8,9},{9,10},{10,1... | collective-permute-start | bytes 393224 | tf_op jit(solution)/shard_map/ppermute | solution.py:178
  56.9 12.0 %collective-permute-start.5 = (f32[128,256]{1,0:T(8,128)S(1)}, f32[128,256]{1,0:T(8,128)S(1)}, u32[]{:S(2)}, u32[]{:S(2)}) collective-permute-start(f32[128,256]{1,0:T(8,128)S(1)} %add_add_fusion.1.refs_0_), channel_id=1, source_target_pairs={{0,3},{1,0},{2,1},{3,2},{4,7},{5,4},{6,5},{7,6},{8,11},{9,8},{10,9... | collective-permute-start | bytes 393224 | tf_op jit(solution)/shard_map/ppermute | solution.py:178
  60.2 8.7 %collective-permute-start.4 = (f32[128,256]{1,0:T(8,128)S(1)}, f32[128,256]{1,0:T(8,128)S(1)}, u32[]{:S(2)}, u32[]{:S(2)}) collective-permute-start(f32[128,256]{1,0:T(8,128)S(1)} %add_add_fusion.1.refs_0_), channel_id=1, source_target_pairs={{0,2},{1,3},{2,0},{3,1},{4,6},{5,7},{6,4},{7,5},{8,10},{9,11},{10,... | collective-permute-start | bytes 393224 | tf_op jit(solution)/shard_map/ppermute | solution.py:178
  60.2 8.7 %collective-permute-start.3 = (f32[128,256]{1,0:T(8,128)S(1)}, f32[128,256]{1,0:T(8,128)S(1)}, u32[]{:S(2)}, u32[]{:S(2)}) collective-permute-start(f32[128,256]{1,0:T(8,128)S(1)} %add_add_fusion.1.refs_0_), channel_id=1, source_target_pairs={{0,1},{1,2},{2,3},{3,0},{4,5},{5,6},{6,7},{7,4},{8,9},{9,10},{10,1... | collective-permute-start | bytes 393224 | tf_op jit(solution)/shard_map/ppermute | solution.py:178
  80.0 4.2 %collective-permute-start.12 = (f32[2048,256]{1,0:T(8,128)S(1)}, f32[2048,256]{1,0:T(8,128)S(1)}, u32[]{:S(2)}, u32[]{:S(2)}) collective-permute-start(f32[2048,256]{1,0:T(8,128)S(1)} %get-tuple-element.36), channel_id=1, source_target_pairs={{0,4},{4,0},{1,5},{5,1},{2,6},{6,2},{3,7},{7,3},{8,12},{12,8},{9,1... | collective-permute-start | bytes 6291464 | tf_op jit(solution)/shard_map/ppermute | solution.py:337

commit v5 on v4

--- a/solution.py
+++ b/solution.py
@@ -1,3 +1,5 @@
+import functools
+
 import jax
 import jax.numpy as jnp
 from jax import lax
@@ -18,6 +20,7 @@
 BLOCK = CAP + 8
 SORT, SORT_RUNS = 1024, 2
 WINDOW = 1408
+STEP = 256
 LIMIT = pltpu.CompilerParams(vmem_limit_bytes=16 * 2**20)
 KEYS = ("keys_0", "keys_1", "keys_2")
 KEYS_VIEW = ("keys_0", "keys_1", "keys_2", "view")
@@ -74,8 +77,10 @@
 
 def pack_kernel(with_group, me_ref, count_ref, table_ref, key_ref, mult_ref, *rest):
     group_ref = rest[0] if with_group else None
-    payload_ref, out_ref = rest[-2:]
+    payload_hbm, out_hbm, payload_ref, out_ref, in_sem, out_sems = rest[-6:]
     rows = DELTA_DEV
+    fetch = pltpu.make_async_copy(payload_hbm, payload_ref, in_sem)
+    fetch.start()
     key = flat(key_ref[...])
     key_hi, key_lo = key >> 7, key & 127
     low = onehot(128, key_lo)
@@ -92,23 +97,29 @@
     rank = jnp.sum(marks * counted_before(marks), axis=0, keepdims=True).astype(I32)
     position = jnp.where(live, owner * CAP + rank, -1)
     sign = flat(mult_ref[...]).astype(F32)
-    payload = payload_ref[...]
-    for c in range(OWNERS // 4):
-        chosen = onehot(4 * CAP, position - 4 * CAP * c, sign)
-        packed = dot(chosen, payload).astype(BF16)
-        for j in range(4):
-            out_ref[pl.ds((4 * c + j) * BLOCK, CAP), :] = packed[CAP * j : CAP * (j + 1)]
     field = rows_of((8, rows))
     value = jnp.where(field == 0, local & 255, jnp.where(field == 1, local >> 8, 0))
     if with_group:
         group = flat(group_ref[...])
         value = jnp.where(field == 2, group & 255, jnp.where(field == 3, group >> 8, value))
     value = jnp.broadcast_to(value.astype(F32)[None], (OWNERS, 8, rows)).reshape(8 * OWNERS, rows)
-    sent = pick((rows_of((8 * OWNERS, rows)) >> 3) == owner, value)
+    held = pick((rows_of((8 * OWNERS, rows)) >> 3) == owner, value)
     place = onehot(4 * CAP, rank + CAP * (me_ref[0] % 4))
-    fields = dot(sent, place, NT).astype(BF16)
+    fields = dot(held, place, NT).astype(BF16)
     for k in range(OWNERS):
         out_ref[pl.ds(k * BLOCK + CAP, 8), :] = fields[8 * k : 8 * k + 8]
+    fetch.wait()
+    payload, sent = payload_ref[...], []
+    for c in range(OWNERS // 4):
+        chosen = onehot(4 * CAP, position - 4 * CAP * c, sign)
+        packed = dot(chosen, payload).astype(BF16)
+        for j in range(4):
+            out_ref[pl.ds((4 * c + j) * BLOCK, CAP), :] = packed[CAP * j : CAP * (j + 1)]
+        part = pl.ds(4 * c * BLOCK, 4 * BLOCK)
+        sent.append(pltpu.make_async_copy(out_ref.at[part], out_hbm.at[part], out_sems.at[c]))
+        sent[-1].start()
+    for copy in sent:
+        copy.wait()
 
 
 def pack(me, count, table, key, mult, group, payload):
@@ -116,8 +127,14 @@
     return pl.pallas_call(
         lambda *refs: pack_kernel(group is not None, *refs),
         out_shape=pltpu.HBM((OWNERS * BLOCK, D), BF16),
-        in_specs=[SMEM, SMEM] + [VMEM] * (4 + len(extra)),
-        out_specs=VMEM,
+        in_specs=[SMEM, SMEM] + [VMEM] * (3 + len(extra)) + [HBM],
+        out_specs=HBM,
+        scratch_shapes=[
+            pltpu.VMEM((DELTA_DEV, D), BF16),
+            pltpu.VMEM((OWNERS * BLOCK, D), BF16),
+            pltpu.SemaphoreType.DMA,
+            pltpu.SemaphoreType.DMA((OWNERS // 4,)),
+        ],
         compiler_params=LIMIT,
         name="pack_a" if extra else "pack_b",
     )(me, count, *map(in_hbm, (table, key.reshape(8, 128), mult.reshape(8, 128), *extra, payload)))
@@ -158,15 +175,14 @@
     total_ref[...] = jnp.zeros_like(total_ref)
     for c in range(8):
         slot, _ = fields_of(in_ref, c)
-        chosen = onehot(KEYS_DEV, slot)
-        total_ref[...] += dot(chosen, payload_of(in_ref, c))
+        total_ref[...] += dot(onehot(KEYS_DEV, slot), payload_of(in_ref, c))
     spread(total_ref, view_ref[0], outs)
 
 
 def slices(kernel, view, *args):
     return pl.pallas_call(
         kernel,
-        out_shape=[jax.ShapeDtypeStruct((128, D), F32)] * 4,
+        out_shape=[pltpu.HBM((128, D), F32)] + [jax.ShapeDtypeStruct((128, D), F32)] * 3,
         in_specs=[SMEM] + [VMEM] * len(args),
         out_specs=[VMEM] * 4,
         scratch_shapes=[pltpu.VMEM((KEYS_DEV, D), F32)],
@@ -206,9 +222,13 @@
     return own + ((group >> 8) << 7) + (group & 127)
 
 
-def sort_kernel(core_ref, slot_ref, group_ref, weight_ref, payload_ref, out_ref, field_ref):
+def sort_kernel(h, core_ref, slot_ref, group_ref, weight_ref, payload_hbm, out_ref, field_ref, payload_ref, sem):
+    source = payload_hbm.at[pl.ds(h * SORT_RUNS * SORT, SORT_RUNS * SORT)]
+    fetch = pltpu.make_async_copy(source, payload_ref, sem)
+    fetch.start()
     for s in range(SORT_RUNS):
-        rows = slice(8 * s, 8 * s + 8)
+        first_row = 8 * (h * SORT_RUNS + s)
+        rows = slice(first_row, first_row + 8)
         slot, weight = flat(slot_ref[rows, :]), flat(weight_ref[rows, :])
         place = place_of(flat(group_ref[rows, :]), core_ref[0])
         bucket = place >> 6
@@ -217,6 +237,8 @@
         first = jnp.sum(jnp.where(bucket < rows_of(shape), 1.0, 0.0), axis=1, keepdims=True)
         position = jnp.sum(marks * (counted_before(marks) + first), axis=0, keepdims=True)
         order = onehot(SORT, position.astype(I32))
+        if s == 0:
+            fetch.wait()
         moved = dot(order, payload_ref[SORT * s : SORT * (s + 1), :]).astype(BF16)
         value, field = jnp.zeros((8, SORT), I32), rows_of((8, SORT))
         for q, part in enumerate((slot & 255, slot >> 8, weight, place & 255, place >> 8)):
@@ -232,112 +254,181 @@
 def sort(h, core, slot, group, weight, payload):
     rows = SORT_RUNS * SORT
     return pl.pallas_call(
-        sort_kernel,
+        functools.partial(sort_kernel, h),
         out_shape=[pltpu.HBM((rows, D), BF16), pltpu.HBM((8, rows), I32)],
-        grid=(1,),
-        in_specs=[SMEM] + [pl.BlockSpec((rows // 128, 128), lambda i: (h, 0))] * 3 + [pl.BlockSpec((rows, D), lambda i: (h, 0))],
+        in_specs=[SMEM] + [VMEM] * 3 + [HBM],
         out_specs=[VMEM] * 2,
+        scratch_shapes=[pltpu.VMEM((rows, D), BF16), pltpu.SemaphoreType.DMA],
         compiler_params=LIMIT,
-    )(core, slot.reshape(32, 128), group.reshape(32, 128), weight.reshape(32, 128), payload)
-
-
-def join_kernel(view_ref, core_ref, *refs):
-    db, b, (first, second, fields0, fields1, in_ref) = refs[:4], refs[4:8], refs[8:13]
-    peer_ref, own_ref, delta_ref, place_ref = refs[13:17]
-    table_ref, whole_ref, sorted_ref, field_ref, line_ref, total_ref, sems = refs[17:]
+    )(core, *(in_hbm(x.reshape(32, 128)) for x in (slot, group, weight)), in_hbm(payload))
+
+
+def join_a_kernel(view_ref, *refs):
+    db, sources, outs, table_hbm = refs[:4], refs[4:8], refs[8:10], refs[10]
+    table_ref, rows_ref, field_ref, in_sems, out_sems = refs[11:]
+    fetched = []
+    for h in range(2):
+        for n, (source, target) in enumerate(((sources[h + 2], field_ref), (sources[h], rows_ref))):
+            fetched.append(pltpu.make_async_copy(source, target.at[h], in_sems.at[2 * h + n]))
+            fetched[-1].start()
+    sent = []
+    for s in range(4):
+        at = pl.ds(((view_ref[0] + 4 - s) % 4) * 128, 128)
+        sent.append(pltpu.make_async_copy(db[s], table_hbm.at[at], out_sems.at[8 + s]))
+        sent[-1].start()
+    fill(table_ref, view_ref[0], lambda s: db[s][...])
+    for h in range(2):
+        fetched[2 * h].wait()
+        fetched[2 * h + 1].wait()
+        for j in range(4):
+            part = pl.ds(512 * j, 512)
+            fields = field_ref[h, :, part]
+            slot = fields[0:1] + 256 * fields[1:2]
+            rows_ref[h, part, :] = terms_of(
+                table_ref, slot, fields[2:3].astype(F32), rows_ref[h, part, :]
+            )
+            sent.append(
+                pltpu.make_async_copy(
+                    rows_ref.at[h, part], outs[h].at[part], out_sems.at[4 * h + j]
+                )
+            )
+            sent[-1].start()
+    for copy in sent:
+        copy.wait()
+
+
+def add_windows(half, total_ref, rows_ref, line_ref, starts, ends):
+    base = half * (GROUPS // 2)
+
+    def window(j, at, size):
+        chosen = onehot(size, line_ref[j : j + 1, :] - at)
+        rows = rows_ref[:, 512 * j : 512 * (j + 1), :].reshape(1024, D)
+        total_ref[pl.ds(pl.multiple_of(at - base, 64), size), :] += dot(chosen, rows)
+
+    near = (2 * half, 2 * half + 1)
+    first = [jnp.clip(start, base, base + GROUPS // 2) for start in starts]
+    for j in near:
+        window(j, first[j], WINDOW)
+    for j in range(4):
+        begin = first[j] + (WINDOW if j in near else 0)
+        last = jnp.minimum(ends[j], base + GROUPS // 2 - 1)
+
+        def more(i, carry, j=j, begin=begin):
+            window(j, begin + i * STEP, STEP)
+            return carry
+
+        lax.fori_loop(0, (last - begin + STEP) // STEP, more, 0)
+
+
+def join_d_kernel(view_ref, core_ref, *refs):
+    db_ref, b, (first, second, fields0, fields1, in_ref) = refs[0], refs[1:5], refs[5:10]
+    peer_ref, delta_ref, place_ref, rows_ref, line_ref, bound_ref = refs[10:16]
+    whole_ref, field_ref, total_ref, sems = refs[16:]
     copies = [
         pltpu.make_async_copy(source, target, sems.at[n])
         for n, (source, target) in enumerate(
             (
                 (fields0, field_ref.at[0]),
                 (fields1, field_ref.at[1]),
-                (first, sorted_ref.at[0]),
-                (second, sorted_ref.at[1]),
+                (first, rows_ref.at[0]),
+                (second, rows_ref.at[1]),
             )
         )
     ]
     for copy in copies:
         copy.start()
     view, core = view_ref[0], core_ref[0]
-    fill(table_ref, view, lambda s: db[s][...])
-    fill(whole_ref, view, lambda s: b[s][...] + db[s][...])
+    fill(
+        whole_ref, view, lambda s: b[s][...] + db_ref[pl.ds(((view + 4 - s) % 4) * 128, 128), :]
+    )
     for c in range(8):
         slot, group = fields_of(in_ref, c)
         at = slice(256 * c, 256 * (c + 1))
         place_ref[:, at] = place_of(group, core)
         delta_ref[at, :] = terms_of(whole_ref, slot, None, payload_of(in_ref, c))
+    copies[0].wait()
+    copies[1].wait()
+    starts, ends = [], []
+    for j in range(4):
+        for h in range(2):
+            fields = field_ref[h, :, 512 * j : 512 * (j + 1)]
+            line_ref[j : j + 1, 512 * h : 512 * (h + 1)] = fields[3:4] + 256 * fields[4:5]
+        line = line_ref[j : j + 1, :]
+        starts.append((jnp.min(line) >> 6) << 6)
+        ends.append(jnp.max(line))
+        bound_ref[j], bound_ref[4 + j] = starts[j], ends[j]
     for g in range(GROUPS // 2 // 512):
         chosen = onehot(512, place_ref[...] - 512 * g)
         total_ref[512 * g : 512 * (g + 1), :] = dot(chosen, delta_ref[...])
-    total_ref[GROUPS // 2 :, :] = jnp.zeros((GROUPS // 2 + WINDOW, D), F32)
-    for copy in copies:
-        copy.wait()
-    starts, ends = [], []
-    for j in range(4):
-        for h in range(2):
-            part, at = slice(512 * j, 512 * (j + 1)), slice(512 * h, 512 * (h + 1))
-            fields = field_ref[h, :, part]
-            slot = fields[0:1] + 256 * fields[1:2]
-            sorted_ref[h, part, :] = terms_of(table_ref, slot, fields[2:3].astype(F32), sorted_ref[h, part, :])
-            line_ref[j : j + 1, at] = fields[3:4] + 256 * fields[4:5]
-        line = line_ref[j : j + 1, :]
-        starts.append(pl.multiple_of((jnp.min(line) >> 6) << 6, 64))
-        ends.append(jnp.max(line))
-
-    def window(j, start):
-        chosen = onehot(WINDOW, line_ref[j : j + 1, :] - start)
-        rows = sorted_ref[:, 512 * j : 512 * (j + 1), :].reshape(1024, D)
-        total_ref[pl.ds(start, WINDOW), :] += dot(chosen, rows)
-
-    for j in range(4):
-        window(j, starts[j])
-    for j in range(4):
-        def more(i, carry, j=j):
-            window(j, pl.multiple_of(starts[j] + i * WINDOW, 64))
-            return carry
-
-        lax.fori_loop(1, (ends[j] - starts[j]) // WINDOW + 1, more, 0)
+    total_ref[GROUPS // 2 :, :] = jnp.zeros((WINDOW, D), F32)
+    copies[2].wait()
+    copies[3].wait()
+    add_windows(0, total_ref, rows_ref, line_ref, starts, ends)
     peer_ref[...] = total_ref[: GROUPS // 2, :]
-    own_ref[...] = total_ref[GROUPS // 2 : GROUPS, :]
-
-
-def own_kernel(own_ref, delta_ref, place_ref, out_ref):
+
+
+def own_kernel(bound_ref, delta_ref, place_ref, rows_ref, line_ref, out_ref, total_ref):
     for g in range(GROUPS // 2 // 512):
-        at = slice(512 * g, 512 * (g + 1))
         chosen = onehot(512, place_ref[...] - GROUPS // 2 - 512 * g)
-        out_ref[at, :] = own_ref[at, :] + dot(chosen, delta_ref[...])
+        total_ref[512 * g : 512 * (g + 1), :] = dot(chosen, delta_ref[...])
+    total_ref[GROUPS // 2 :, :] = jnp.zeros((WINDOW, D), F32)
+    starts, ends = [bound_ref[j] for j in range(4)], [bound_ref[4 + j] for j in range(4)]
+    add_windows(1, total_ref, rows_ref, line_ref, starts, ends)
+    out_ref[...] = total_ref[: GROUPS // 2, :]
 
 
 def join(view, core, db, b, halves, received):
     rows = OWNERS * CAP
     table = pltpu.VMEM((KEYS_DEV, 2 * D), BF16)
+    total = pltpu.VMEM((GROUPS // 2 + WINDOW, D), F32)
     half = jax.ShapeDtypeStruct((GROUPS // 2, D), F32)
-    peer, own, delta, place = pl.pallas_call(
-        join_kernel,
+    fields = [in_hbm(halves[h][1]) for h in (0, 1)]
+    *terms, db_table = pl.pallas_call(
+        join_a_kernel,
+        out_shape=[pltpu.HBM((A_DEV // 2, D), BF16)] * 2 + [pltpu.HBM((KEYS_DEV, D), F32)],
+        in_specs=[SMEM] + [VMEM] * 4 + [HBM] * 4,
+        out_specs=[HBM] * 3,
+        scratch_shapes=[
+            table,
+            pltpu.VMEM((2, A_DEV // 2, D), BF16),
+            pltpu.VMEM((2, 8, A_DEV // 2), I32),
+            pltpu.SemaphoreType.DMA((4,)),
+            pltpu.SemaphoreType.DMA((12,)),
+        ],
+        compiler_params=LIMIT,
+        name="join_a",
+    )(view, *db, in_hbm(halves[0][0]), in_hbm(halves[1][0]), *fields)
+    peer, delta, place, sorted_rows, line, bound = pl.pallas_call(
+        join_d_kernel,
         out_shape=[
-            half,
             half,
             jax.ShapeDtypeStruct((rows, D), BF16),
             jax.ShapeDtypeStruct((1, rows), I32),
+            jax.ShapeDtypeStruct((2, A_DEV // 2, D), BF16),
+            jax.ShapeDtypeStruct((4, 1024), I32),
+            jax.ShapeDtypeStruct((8,), I32),
         ],
-        in_specs=[SMEM] * 2 + [VMEM] * 8 + [HBM] * 4 + [VMEM],
-        out_specs=[VMEM] * 4,
+        in_specs=[SMEM] * 2 + [VMEM] * 5 + [HBM] * 4 + [VMEM],
+        out_specs=[VMEM] * 5 + [SMEM],
         scratch_shapes=[
             table,
-            table,
-            pltpu.VMEM((2, A_DEV // 2, D), BF16),
             pltpu.VMEM((2, 8, A_DEV // 2), I32),
-            pltpu.VMEM((4, 1024), I32),
-            pltpu.VMEM((GROUPS + WINDOW, D), F32),
+            total,
             pltpu.SemaphoreType.DMA((4,)),
         ],
-        compiler_params=pltpu.CompilerParams(vmem_limit_bytes=32 * 2**20),
-        name="join",
-    )(view, core, *db, *b, *(in_hbm(half[i]) for i in (0, 1) for half in halves), received)
+        compiler_params=pltpu.CompilerParams(vmem_limit_bytes=28 * 2**20),
+        name="join_d",
+    )(view, core, in_hbm(db_table), *b, *map(in_hbm, terms), *fields, received)
     other = lax.ppermute(peer, "keys_2", [(0, 1), (1, 0)])
     own = pl.pallas_call(
-        own_kernel, out_shape=half, in_specs=[VMEM] * 3, out_specs=VMEM, name="join_own", compiler_params=LIMIT
-    )(own, delta, place)
+        own_kernel,
+        out_shape=half,
+        in_specs=[SMEM] + [VMEM] * 4,
+        out_specs=VMEM,
+        scratch_shapes=[total],
+        compiler_params=LIMIT,
+        name="join_own",
+    )(bound, delta, place, sorted_rows, line)
     return (own + other).astype(BF16)
 
 
@@ -371,7 +462,7 @@
     core = lax.axis_index("keys_2").astype(I32).reshape(1)
     db_out = pack(me, db_count, table, db_key, db_mult, None, db_payload)
     da_out = pack(me, da_count, table, da_key, da_mult, da_group, da_payload)
-    db_in = in_hbm(exchange(db_out))
+    db_in = exchange(db_out)
     da_in = exchange(da_out)
     b_parts = slices(
         sum_b_kernel, view, b_slot.reshape(32, 128), b_weight.reshape(32, 128), b_payload

time: 115 us -> 122 us (1.061)
  Pallas kernels: 32 us -> 39.7 us
  waiting for transfers between devices: 20.3 us -> 18.8 us
    pallas_call x6 -> x7, Pallas kernels: 24 us -> 31.6 us  [the longest x2 11 us: sort(): pl.pallas_call(functools.partial(sort_kernel, h), out_shape=[pltpu.HBM((r...]
    ppermute x1, waiting for transfers between devices: 1.81 us -> 0.01 us  [join(): other = lax.ppermute(peer, 'keys_2', [(0, 1), (1, 0)])]
  transfers between devices with their start and end apart: 15 -> 15, of which waited for: 4 -> 2; matrix products, arithmetic and copies ran while one was open for 0% -> 1% of each run, Pallas kernels for 15% -> 23%
where the time goes in v5:
time: 122 us; the launch traced here: 121 us
  Pallas kernels  39.7 us (33%)
  starting transfers between devices  29 us (24%)
  blocking collectives  28.7 us (24%)
  waiting for transfers between devices  18.8 us (15%)
  other arithmetic  2.15 us (2%)
  local copies, waits for them, and re-layouts  1.61 us (1%)
  between operations  1.49 us (1%)
    all_to_all x1, blocking collectives, shards(): lax.all_to_all(blocks, ('keys_0', 'keys_1', 'view'), 0, 0, tiled=True)  28.7 us
    ppermute x12, starting transfers between devices, shift(): return lax.ppermute(x, 'view', [(j, (j + s) % 4) for j in range(4)])  16.2 us
    all_to_all x2, waiting for transfers between devices, exchange(): lax.all_to_all(blocks, KEYS, 0, 0, tiled=True).reshape(OWNERS * BLOCK, D)  13.5 us
    all_to_all x2, starting transfers between devices, exchange(): lax.all_to_all(blocks, KEYS, 0, 0, tiled=True).reshape(OWNERS * BLOCK, D)  12.5 us
    pallas_call x2, Pallas kernels, sort(): pl.pallas_call(functools.partial(sort_kernel, h), out_shape=[pltpu.HBM((r...  11 us
    pallas_call x2, Pallas kernels, pack(): pl.pallas_call(lambda *refs: pack_kernel(group is not None, *refs), out_s...  8.12 us
    pallas_call x1, Pallas kernels, join(): pl.pallas_call(join_d_kernel, out_shape=[half, jax.ShapeDtypeStruct((rows...  7.26 us
    ppermute x12, waiting for transfers between devices, shift(): return lax.ppermute(x, 'view', [(j, (j + s) % 4) for j in range(4)])  5.31 us
  transfers between devices with their start and end apart: 15, of which 2 were waited for; matrix products, arithmetic and copies ran while one was open for 1% of the time, Pallas kernels for 23%

profile of v5, /device:TPU:0, one launch (start us, length us, event | category | flops | bytes accessed | tf_op | source)
XLA Modules:
  0.0 121.4 jit_solution(12700053159422917484)
XLA Ops:
  0.7 4.0 %pack_b.1 = bf16[2304,256]{1,0:T(8,128)(2,1)} custom-call(s32[1]{0:T(128)} %bitcast.2.refs_0_, s32[1]{0:T(128)S(6)} %copy.19.refs_1_, s32[128,128]{1,0:T(8,128)} %bitcast.26, s32[8,128]{1,0:T(8,128)} %bitcast.34, s32[8,128]{1,0:T(8,128)} %bitcast.35, bf16[1024,256]{1,0:T(8,128)(2,1)} %refs_5_.1), custom_call_target="tpu_custom_call" | custom-call | tf_op jit(solution)/shard_map/pack_b/pallas_call | solution.py:127
  4.7 8.5 %all-to-all-start = ((bf16[32,72,256]{2,1,0:T(8,128)(2,1)}), bf16[32,72,256]{2,1,0:T(8,128)(2,1)S(1)}, u32[]{:S(2)}, u32[]{:S(2)}) async-start(bf16[32,72,256]{2,1,0:T(8,128)(2,1)} %bitcast.24), calls=%async_computation | async-start | bytes 2359296 | tf_op jit(solution)/shard_map/all_to_all | solution.py:437
  13.8 4.1 %pack_a.1 = bf16[2304,256]{1,0:T(8,128)(2,1)} custom-call(s32[1]{0:T(128)} %bitcast.2.refs_0_, s32[1]{0:T(128)S(6)} %copy.18.refs_1_, s32[128,128]{1,0:T(8,128)} %bitcast.27, s32[8,128]{1,0:T(8,128)} %bitcast.36, s32[8,128]{1,0:T(8,128)} %bitcast.37, s32[8,128]{1,0:T(8,128)} %bitcast.38, bf16[1024,256]{1,0:T(8,128)(2,1)} %refs_6_.1), custom_call_target="tpu_custom_call" | custom-call | tf_op jit(solution)/shard_map/pack_a/pallas_call | solution.py:127
  17.9 0.0 copy-start.1
  17.9 0.0 copy-start.2
  17.9 13.5 %all-to-all-done = bf16[32,72,256]{2,1,0:T(8,128)(2,1)S(1)} async-done(((bf16[32,72,256]{2,1,0:T(8,128)(2,1)}), bf16[32,72,256]{2,1,0:T(8,128)(2,1)S(1)}, u32[]{:S(2)}, u32[]{:S(2)}) %all-to-all-start) | async-done | bytes 1179680 | tf_op jit(solution)/shard_map/all_to_all | solution.py:437
  31.4 4.0 %all-to-all-start.1 = ((bf16[32,72,256]{2,1,0:T(8,128)(2,1)}), bf16[32,72,256]{2,1,0:T(8,128)(2,1)S(1)}, u32[]{:S(2)}, u32[]{:S(2)}) async-start(bf16[32,72,256]{2,1,0:T(8,128)(2,1)} %bitcast.23), calls=%async_computation.1 | async-start | bytes 2359296 | tf_op jit(solution)/shard_map/all_to_all | solution.py:437
  35.4 1.4 %shard_map.163 = (f32[128,256]{1,0:T(8,128)}, f32[128,256]{1,0:T(8,128)S(1)}, f32[128,256]{1,0:T(8,128)S(1)}, f32[128,256]{1,0:T(8,128)S(1)}) custom-call(s32[1]{0:T(128)} %bitcast.view_ref, bf16[2304,256]{1,0:T(8,128)(2,1)S(1)} %bitcast.20), custom_call_target="tpu_custom_call" | custom-call | tf_op jit(solution)/shard_map/pallas_call | solution.py:183
  36.8 1.5 %collective-permute-start = (f32[128,256]{1,0:T(8,128)S(1)}, f32[128,256]{1,0:T(8,128)S(1)}, u32[]{:S(2)}, u32[]{:S(2)}) collective-permute-start(f32[128,256]{1,0:T(8,128)S(1)} %get-tuple-element.27), channel_id=1, source_target_pairs={{0,1},{1,2},{2,3},{3,0},{4,5},{5,6},{6,7},{7,4},{8,9},{9,10},{10,1... | collective-permute-start | bytes 393224 | tf_op jit(solution)/shard_map/ppermute | solution.py:194
  38.3 2.7 %collective-permute-start.1 = (f32[128,256]{1,0:T(8,128)S(1)}, f32[128,256]{1,0:T(8,128)S(1)}, u32[]{:S(2)}, u32[]{:S(2)}) collective-permute-start(f32[128,256]{1,0:T(8,128)S(1)} %get-tuple-element.28), channel_id=1, source_target_pairs={{0,2},{1,3},{2,0},{3,1},{4,6},{5,7},{6,4},{7,5},{8,10},{9,11},{10,... | collective-permute-start | bytes 393224 | tf_op jit(solution)/shard_map/ppermute | solution.py:194
  41.0 1.4 %collective-permute-start.2 = (f32[128,256]{1,0:T(8,128)S(1)}, f32[128,256]{1,0:T(8,128)S(1)}, u32[]{:S(2)}, u32[]{:S(2)}) collective-permute-start(f32[128,256]{1,0:T(8,128)S(1)} %get-tuple-element.29), channel_id=1, source_target_pairs={{0,3},{1,0},{2,1},{3,2},{4,7},{5,4},{6,5},{7,6},{8,11},{9,8},{10,9... | collective-permute-start | bytes 393224 | tf_op jit(solution)/shard_map/ppermute | solution.py:194
  42.5 1.6 %copy-done = bf16[4096,256]{1,0:T(8,128)(2,1)S(1)} copy-done((bf16[4096,256]{1,0:T(8,128)(2,1)S(1)}, bf16[4096,256]{1,0:T(8,128)(2,1)}, u32[]{:S(2)}) %copy-start) | copy-done | bytes 2097176
  44.1 1.9 %shard_map.166 = (f32[128,256]{1,0:T(8,128)}, f32[128,256]{1,0:T(8,128)S(1)}, f32[128,256]{1,0:T(8,128)S(1)}, f32[128,256]{1,0:T(8,128)S(1)}) custom-call(s32[1]{0:T(128)} %bitcast.view_ref, s32[32,128]{1,0:T(8,128)S(1)} %bitcast.21, s32[32,128]{1,0:T(8,128)S(1)} %bitcast.22, bf16[4096,256]{1,0:T(8,128)(2,1)S(1)} %copy-done), custom_call_target="tpu_custom_call" | custom-call | tf_op jit(solution)/shard_map/pallas_call | solution.py:183
  46.0 0.6 collective-permute-start.6
  46.6 0.9 collective-permute-start.7
  47.5 0.0 collective-permute-done
  47.5 1.8 %collective-permute-start.8 = (f32[128,256]{1,0:T(8,128)S(1)}, f32[128,256]{1,0:T(8,128)S(1)}, u32[]{:S(2)}, u32[]{:S(2)}) collective-permute-start(f32[128,256]{1,0:T(8,128)S(1)} %get-tuple-element.38), channel_id=1, source_target_pairs={{0,3},{1,0},{2,1},{3,2},{4,7},{5,4},{6,5},{7,6},{8,11},{9,8},{10,9... | collective-permute-start | bytes 393224 | tf_op jit(solution)/shard_map/ppermute | solution.py:194
  49.3 1.5 %collective-permute-start.5 = (f32[128,256]{1,0:T(8,128)S(1)}, f32[128,256]{1,0:T(8,128)S(1)}, u32[]{:S(2)}, u32[]{:S(2)}) collective-permute-start(f32[128,256]{1,0:T(8,128)S(1)} %add_add_fusion.1.refs_0_), channel_id=1, source_target_pairs={{0,3},{1,0},{2,1},{3,2},{4,7},{5,4},{6,5},{7,6},{8,11},{9,8},{10,9... | collective-permute-start | bytes 393224 | tf_op jit(solution)/shard_map/ppermute | solution.py:194
  50.8 1.6 %collective-permute-start.4 = (f32[128,256]{1,0:T(8,128)S(1)}, f32[128,256]{1,0:T(8,128)S(1)}, u32[]{:S(2)}, u32[]{:S(2)}) collective-permute-start(f32[128,256]{1,0:T(8,128)S(1)} %add_add_fusion.1.refs_0_), channel_id=1, source_target_pairs={{0,2},{1,3},{2,0},{3,1},{4,6},{5,7},{6,4},{7,5},{8,10},{9,11},{10,... | collective-permute-start | bytes 393224 | tf_op jit(solution)/shard_map/ppermute | solution.py:194
  52.4 5.3 %collective-permute-done.6 = f32[128,256]{1,0:T(8,128)S(1)} collective-permute-done((f32[128,256]{1,0:T(8,128)S(1)}, f32[128,256]{1,0:T(8,128)S(1)}, u32[]{:S(2)}, u32[]{:S(2)}) %collective-permute-start.6) | collective-permute-done | bytes 131104 | tf_op jit(solution)/shard_map/ppermute | solution.py:194
  57.7 0.9 add_add_fusion.refs_1_
  58.6 3.3 %collective-permute-start.11 = (f32[128,256]{1,0:T(8,128)S(1)}, f32[128,256]{1,0:T(8,128)S(1)}, u32[]{:S(2)}, u32[]{:S(2)}) collective-permute-start(f32[128,256]{1,0:T(8,128)S(1)} %add_add_fusion.refs_1_), channel_id=1, source_target_pairs={{0,3},{1,0},{2,1},{3,2},{4,7},{5,4},{6,5},{7,6},{8,11},{9,8},{10,9... | collective-permute-start | bytes 393224 | tf_op jit(solution)/shard_map/ppermute | solution.py:194
  62.0 0.9 collective-permute-start.9
  62.9 5.5 %shard_map.165 = (bf16[2048,256]{1,0:T(8,128)(2,1)}, s32[8,2048]{1,0:T(8,128)}) custom-call(s32[1]{0:T(128)} %bitcast.1.core_ref, s32[32,128]{1,0:T(8,128)} %bitcast.28, s32[32,128]{1,0:T(8,128)} %bitcast.30, s32[32,128]{1,0:T(8,128)} %bitcast.32, bf16[4096,256]{1,0:T(8,128)(2,1)} %payload_hbm.3), custom_call_target="tpu_custom_call" | custom-call | tf_op jit(solution)/shard_map/pallas_call | solution.py:256
  68.4 5.5 %shard_map.164 = (bf16[2048,256]{1,0:T(8,128)(2,1)}, s32[8,2048]{1,0:T(8,128)}) custom-call(s32[1]{0:T(128)} %bitcast.1.core_ref, s32[32,128]{1,0:T(8,128)} %bitcast.29, s32[32,128]{1,0:T(8,128)} %bitcast.31, s32[32,128]{1,0:T(8,128)} %bitcast.33, bf16[4096,256]{1,0:T(8,128)(2,1)} %payload_hbm.3), custom_call_target="tpu_custom_call" | custom-call | tf_op jit(solution)/shard_map/pallas_call | solution.py:256
  73.9 5.0 %join_a.1 = (bf16[2048,256]{1,0:T(8,128)(2,1)}, bf16[2048,256]{1,0:T(8,128)(2,1)}, f32[512,256]{1,0:T(8,128)}) custom-call(s32[1]{0:T(128)} %bitcast.view_ref, f32[128,256]{1,0:T(8,128)S(1)} %add_add_fusion.1.refs_0_, f32[128,256]{1,0:T(8,128)S(1)} %collective-permute-done.3.refs_1_, f32[128,256]{1,0:T(8,128)S(1)} %collective-permute-done.4.refs_2_, ...), custom_call_target="tpu_custom_call" | custom-call | tf_op jit(solution)/shard_map/join_a/pallas_call | solution.py:386
  79.0 7.3 %join_d.1 = (f32[2048,256]{1,0:T(8,128)S(1)}, bf16[2048,256]{1,0:T(8,128)(2,1)S(1)}, s32[1,2048]{1,0:T(1,128)S(1)}, bf16[2,2048,256]{2,1,0:T(8,128)(2,1)S(1)}, s32[4,1024]{1,0:T(4,128)S(1)}, /*index=5*/s32[8]{0:T(128)S(1)}) custom-call(s32[1]{0:T(128)} %bitcast.view_ref, s32[1]{0:T(128)} %bitcast.1.core_ref, f32[512,256]{1,0:T(8,128)} %get-tuple-element.34.refs_0_, ...), custom_call_target="tpu_custom_call" | custom-call | tf_op jit(solution)/shard_map/join_d/pallas_call | solution.py:401
  86.3 0.3 collective-permute-start.12
  86.6 5.0 %join_own.1 = f32[2048,256]{1,0:T(8,128)S(1)} custom-call(s32[8]{0:T(128)S(1)} %get-tuple-element.41.bound_ref, bf16[2048,256]{1,0:T(8,128)(2,1)S(1)} %get-tuple-element.42.delta_ref, s32[1,2048]{1,0:T(1,128)S(1)} %get-tuple-element.43.place_ref, bf16[2,2048,256]{2,1,0:T(8,128)(2,1)S(1)} %get-tuple-element.44.rows_ref, s32[4,1024]{1,0:T(4,128)S(1)} %get-tuple-element.45.line_ref), custom_call_target="tpu_custom_call" | custom-call | tf_op jit(solution)/shard_map/join_own/pallas_call | solution.py:423
  91.6 0.4 add_convert_fusion
  91.9 28.7 %all_to_all.15 = bf16[64,32,256]{2,1,0:T(8,128)(2,1)S(1)} all-to-all(bf16[64,32,256]{2,1,0:T(8,128)(2,1)S(1)} %bitcast.25), channel_id=1, replica_groups=mesh['keys_0'=4,'keys_1'=4,'keys_2'=2,'view'=4] {'keys_0','keys_1','view'}, dimensions={0} | all-to-all | bytes 2097152 | tf_op jit(solution)/shard_map/all_to_all | solution.py:475
  120.6 0.8 convert_reduce_fusion
  (20 shorter events, 0.1 us)
Async XLA Ops:
  4.7 26.7 %all-to-all-start = ((bf16[32,72,256]{2,1,0:T(8,128)(2,1)}), bf16[32,72,256]{2,1,0:T(8,128)(2,1)S(1)}, u32[]{:S(2)}, u32[]{:S(2)}) async-start(bf16[32,72,256]{2,1,0:T(8,128)(2,1)} %bitcast.24), calls=%async_computation | async-start | bytes 2359296 | tf_op jit(solution)/shard_map/all_to_all | solution.py:437
  17.9 24.6 %copy-start.1 = (s32[4096]{0:T(1024)S(1)}, s32[4096]{0:T(1024)}, u32[]{:S(2)}) copy-start(s32[4096]{0:T(1024)} %param.22) | copy-start | bytes 49156
  17.9 24.6 %copy-start.2 = (s32[4096]{0:T(1024)S(1)}, s32[4096]{0:T(1024)}, u32[]{:S(2)}) copy-start(s32[4096]{0:T(1024)} %param.23) | copy-start | bytes 49156
  31.4 47.6 %all-to-all-start.1 = ((bf16[32,72,256]{2,1,0:T(8,128)(2,1)}), bf16[32,72,256]{2,1,0:T(8,128)(2,1)S(1)}, u32[]{:S(2)}, u32[]{:S(2)}) async-start(bf16[32,72,256]{2,1,0:T(8,128)(2,1)} %bitcast.23), calls=%async_computation.1 | async-start | bytes 2359296 | tf_op jit(solution)/shard_map/all_to_all | solution.py:437
  36.8 10.7 %collective-permute-start = (f32[128,256]{1,0:T(8,128)S(1)}, f32[128,256]{1,0:T(8,128)S(1)}, u32[]{:S(2)}, u32[]{:S(2)}) collective-permute-start(f32[128,256]{1,0:T(8,128)S(1)} %get-tuple-element.27), channel_id=1, source_target_pairs={{0,1},{1,2},{2,3},{3,0},{4,5},{5,6},{6,7},{7,4},{8,9},{9,10},{10,1... | collective-permute-start | bytes 393224 | tf_op jit(solution)/shard_map/ppermute | solution.py:194
  38.3 11.0 %collective-permute-start.1 = (f32[128,256]{1,0:T(8,128)S(1)}, f32[128,256]{1,0:T(8,128)S(1)}, u32[]{:S(2)}, u32[]{:S(2)}) collective-permute-start(f32[128,256]{1,0:T(8,128)S(1)} %get-tuple-element.28), channel_id=1, source_target_pairs={{0,2},{1,3},{2,0},{3,1},{4,6},{5,7},{6,4},{7,5},{8,10},{9,11},{10,... | collective-permute-start | bytes 393224 | tf_op jit(solution)/shard_map/ppermute | solution.py:194
  41.0 8.3 %collective-permute-start.2 = (f32[128,256]{1,0:T(8,128)S(1)}, f32[128,256]{1,0:T(8,128)S(1)}, u32[]{:S(2)}, u32[]{:S(2)}) collective-permute-start(f32[128,256]{1,0:T(8,128)S(1)} %get-tuple-element.29), channel_id=1, source_target_pairs={{0,3},{1,0},{2,1},{3,2},{4,7},{5,4},{6,5},{7,6},{8,11},{9,8},{10,9... | collective-permute-start | bytes 393224 | tf_op jit(solution)/shard_map/ppermute | solution.py:194
  42.5 1.6 %copy-start = (bf16[4096,256]{1,0:T(8,128)(2,1)S(1)}, bf16[4096,256]{1,0:T(8,128)(2,1)}, u32[]{:S(2)}) copy-start(bf16[4096,256]{1,0:T(8,128)(2,1)} %payload_ref.1) | copy-start | bytes 6291460
  44.1 5.2 %copy-start.3 = (f32[128,256]{1,0:T(8,128)S(1)}, f32[128,256]{1,0:T(8,128)}, u32[]{:S(2)}) copy-start(f32[128,256]{1,0:T(8,128)} %get-tuple-element.26) | copy-start | bytes 393220
  46.0 11.7 %collective-permute-start.6 = (f32[128,256]{1,0:T(8,128)S(1)}, f32[128,256]{1,0:T(8,128)S(1)}, u32[]{:S(2)}, u32[]{:S(2)}) collective-permute-start(f32[128,256]{1,0:T(8,128)S(1)} %get-tuple-element.36), channel_id=1, source_target_pairs={{0,1},{1,2},{2,3},{3,0},{4,5},{5,6},{6,7},{7,4},{8,9},{9,10},{10,1... | collective-permute-start | bytes 393224 | tf_op jit(solution)/shard_map/ppermute | solution.py:194
  46.6 11.1 %collective-permute-start.7 = (f32[128,256]{1,0:T(8,128)S(1)}, f32[128,256]{1,0:T(8,128)S(1)}, u32[]{:S(2)}, u32[]{:S(2)}) collective-permute-start(f32[128,256]{1,0:T(8,128)S(1)} %get-tuple-element.37), channel_id=1, source_target_pairs={{0,2},{1,3},{2,0},{3,1},{4,6},{5,7},{6,4},{7,5},{8,10},{9,11},{10,... | collective-permute-start | bytes 393224 | tf_op jit(solution)/shard_map/ppermute | solution.py:194
  47.5 10.2 %collective-permute-start.8 = (f32[128,256]{1,0:T(8,128)S(1)}, f32[128,256]{1,0:T(8,128)S(1)}, u32[]{:S(2)}, u32[]{:S(2)}) collective-permute-start(f32[128,256]{1,0:T(8,128)S(1)} %get-tuple-element.38), channel_id=1, source_target_pairs={{0,3},{1,0},{2,1},{3,2},{4,7},{5,4},{6,5},{7,6},{8,11},{9,8},{10,9... | collective-permute-start | bytes 393224 | tf_op jit(solution)/shard_map/ppermute | solution.py:194
  49.3 12.6 %collective-permute-start.5 = (f32[128,256]{1,0:T(8,128)S(1)}, f32[128,256]{1,0:T(8,128)S(1)}, u32[]{:S(2)}, u32[]{:S(2)}) collective-permute-start(f32[128,256]{1,0:T(8,128)S(1)} %add_add_fusion.1.refs_0_), channel_id=1, source_target_pairs={{0,3},{1,0},{2,1},{3,2},{4,7},{5,4},{6,5},{7,6},{8,11},{9,8},{10,9... | collective-permute-start | bytes 393224 | tf_op jit(solution)/shard_map/ppermute | solution.py:194
  50.8 23.1 %collective-permute-start.4 = (f32[128,256]{1,0:T(8,128)S(1)}, f32[128,256]{1,0:T(8,128)S(1)}, u32[]{:S(2)}, u32[]{:S(2)}) collective-permute-start(f32[128,256]{1,0:T(8,128)S(1)} %add_add_fusion.1.refs_0_), channel_id=1, source_target_pairs={{0,2},{1,3},{2,0},{3,1},{4,6},{5,7},{6,4},{7,5},{8,10},{9,11},{10,... | collective-permute-start | bytes 393224 | tf_op jit(solution)/shard_map/ppermute | solution.py:194
  57.7 16.2 %collective-permute-start.3 = (f32[128,256]{1,0:T(8,128)S(1)}, f32[128,256]{1,0:T(8,128)S(1)}, u32[]{:S(2)}, u32[]{:S(2)}) collective-permute-start(f32[128,256]{1,0:T(8,128)S(1)} %add_add_fusion.1.refs_0_), channel_id=1, source_target_pairs={{0,1},{1,2},{2,3},{3,0},{4,5},{5,6},{6,7},{7,4},{8,9},{9,10},{10,1... | collective-permute-start | bytes 393224 | tf_op jit(solution)/shard_map/ppermute | solution.py:194
  58.6 20.3 %collective-permute-start.11 = (f32[128,256]{1,0:T(8,128)S(1)}, f32[128,256]{1,0:T(8,128)S(1)}, u32[]{:S(2)}, u32[]{:S(2)}) collective-permute-start(f32[128,256]{1,0:T(8,128)S(1)} %add_add_fusion.refs_1_), channel_id=1, source_target_pairs={{0,3},{1,0},{2,1},{3,2},{4,7},{5,4},{6,5},{7,6},{8,11},{9,8},{10,9... | collective-permute-start | bytes 393224 | tf_op jit(solution)/shard_map/ppermute | solution.py:194
  61.9 17.0 %collective-permute-start.10 = (f32[128,256]{1,0:T(8,128)S(1)}, f32[128,256]{1,0:T(8,128)S(1)}, u32[]{:S(2)}, u32[]{:S(2)}) collective-permute-start(f32[128,256]{1,0:T(8,128)S(1)} %add_add_fusion.refs_1_), channel_id=1, source_target_pairs={{0,2},{1,3},{2,0},{3,1},{4,6},{5,7},{6,4},{7,5},{8,10},{9,11},{10,... | collective-permute-start | bytes 393224 | tf_op jit(solution)/shard_map/ppermute | solution.py:194
  62.0 17.0 %collective-permute-start.9 = (f32[128,256]{1,0:T(8,128)S(1)}, f32[128,256]{1,0:T(8,128)S(1)}, u32[]{:S(2)}, u32[]{:S(2)}) collective-permute-start(f32[128,256]{1,0:T(8,128)S(1)} %add_add_fusion.refs_1_), channel_id=1, source_target_pairs={{0,1},{1,2},{2,3},{3,0},{4,5},{5,6},{6,7},{7,4},{8,9},{9,10},{10,1... | collective-permute-start | bytes 393224 | tf_op jit(solution)/shard_map/ppermute | solution.py:194
  86.3 5.3 %collective-permute-start.12 = (f32[2048,256]{1,0:T(8,128)S(1)}, f32[2048,256]{1,0:T(8,128)S(1)}, u32[]{:S(2)}, u32[]{:S(2)}) collective-permute-start(f32[2048,256]{1,0:T(8,128)S(1)} %get-tuple-element.46), channel_id=1, source_target_pairs={{0,4},{4,0},{1,5},{5,1},{2,6},{6,2},{3,7},{7,3},{8,12},{12,8},{9,1... | collective-permute-start | bytes 6291464 | tf_op jit(solution)/shard_map/ppermute | solution.py:422

commit v6 on v5

--- a/solution.py
+++ b/solution.py
@@ -1,5 +1,3 @@
-import functools
-
 import jax
 import jax.numpy as jnp
 from jax import lax
@@ -18,8 +16,8 @@
 OWNERS = 32
 CAP = 64
 BLOCK = CAP + 8
-SORT, SORT_RUNS = 1024, 2
-WINDOW = 1408
+SORT, RUNS = 512, 8
+WINDOW = 1472
 STEP = 256
 LIMIT = pltpu.CompilerParams(vmem_limit_bytes=16 * 2**20)
 KEYS = ("keys_0", "keys_1", "keys_2")
@@ -77,7 +75,7 @@
 
 def pack_kernel(with_group, me_ref, count_ref, table_ref, key_ref, mult_ref, *rest):
     group_ref = rest[0] if with_group else None
-    payload_hbm, out_hbm, payload_ref, out_ref, in_sem, out_sems = rest[-6:]
+    payload_hbm, out_ref, payload_ref, in_sem = rest[-4:]
     rows = DELTA_DEV
     fetch = pltpu.make_async_copy(payload_hbm, payload_ref, in_sem)
     fetch.start()
@@ -109,32 +107,22 @@
     for k in range(OWNERS):
         out_ref[pl.ds(k * BLOCK + CAP, 8), :] = fields[8 * k : 8 * k + 8]
     fetch.wait()
-    payload, sent = payload_ref[...], []
+    payload = payload_ref[...]
     for c in range(OWNERS // 4):
         chosen = onehot(4 * CAP, position - 4 * CAP * c, sign)
         packed = dot(chosen, payload).astype(BF16)
         for j in range(4):
             out_ref[pl.ds((4 * c + j) * BLOCK, CAP), :] = packed[CAP * j : CAP * (j + 1)]
-        part = pl.ds(4 * c * BLOCK, 4 * BLOCK)
-        sent.append(pltpu.make_async_copy(out_ref.at[part], out_hbm.at[part], out_sems.at[c]))
-        sent[-1].start()
-    for copy in sent:
-        copy.wait()
 
 
 def pack(me, count, table, key, mult, group, payload):
     extra = [] if group is None else [group.reshape(8, 128)]
     return pl.pallas_call(
         lambda *refs: pack_kernel(group is not None, *refs),
-        out_shape=pltpu.HBM((OWNERS * BLOCK, D), BF16),
+        out_shape=jax.ShapeDtypeStruct((OWNERS * BLOCK, D), BF16),
         in_specs=[SMEM, SMEM] + [VMEM] * (3 + len(extra)) + [HBM],
-        out_specs=HBM,
-        scratch_shapes=[
-            pltpu.VMEM((DELTA_DEV, D), BF16),
-            pltpu.VMEM((OWNERS * BLOCK, D), BF16),
-            pltpu.SemaphoreType.DMA,
-            pltpu.SemaphoreType.DMA((OWNERS // 4,)),
-        ],
+        out_specs=VMEM,
+        scratch_shapes=[pltpu.VMEM((DELTA_DEV, D), BF16), pltpu.SemaphoreType.DMA],
         compiler_params=LIMIT,
         name="pack_a" if extra else "pack_b",
     )(me, count, *map(in_hbm, (table, key.reshape(8, 128), mult.reshape(8, 128), *extra, payload)))
@@ -222,77 +210,85 @@
     return own + ((group >> 8) << 7) + (group & 127)
 
 
-def sort_kernel(h, core_ref, slot_ref, group_ref, weight_ref, payload_hbm, out_ref, field_ref, payload_ref, sem):
-    source = payload_hbm.at[pl.ds(h * SORT_RUNS * SORT, SORT_RUNS * SORT)]
-    fetch = pltpu.make_async_copy(source, payload_ref, sem)
-    fetch.start()
-    for s in range(SORT_RUNS):
-        first_row = 8 * (h * SORT_RUNS + s)
-        rows = slice(first_row, first_row + 8)
-        slot, weight = flat(slot_ref[rows, :]), flat(weight_ref[rows, :])
-        place = place_of(flat(group_ref[rows, :]), core_ref[0])
-        bucket = place >> 6
-        shape = (GROUPS // 64, SORT)
-        marks = jnp.where(rows_of(shape) == bucket, 1.0, 0.0)
-        first = jnp.sum(jnp.where(bucket < rows_of(shape), 1.0, 0.0), axis=1, keepdims=True)
-        position = jnp.sum(marks * (counted_before(marks) + first), axis=0, keepdims=True)
-        order = onehot(SORT, position.astype(I32))
-        if s == 0:
-            fetch.wait()
-        moved = dot(order, payload_ref[SORT * s : SORT * (s + 1), :]).astype(BF16)
-        value, field = jnp.zeros((8, SORT), I32), rows_of((8, SORT))
+def sort_kernel(
+    core_ref, slot_ref, group_ref, weight_ref, payload_hbm, out_ref, field_ref, payload_ref, sems
+):
+    fetched = []
+    for s in range(RUNS):
+        part = pl.ds(SORT * s, SORT)
+        fetched.append(
+            pltpu.make_async_copy(payload_hbm.at[part], payload_ref.at[part], sems.at[s])
+        )
+        fetched[-1].start()
+    buckets, quarter = GROUPS // 64, SORT // 4
+    places = place_of(group_ref[...], core_ref[0])
+
+    def run_of(x, s):
+        return flat(x[SORT // 128 * s : SORT // 128 * (s + 1), :])
+
+    bucket = [run_of(places, s) >> 6 for s in range(RUNS)]
+    number = rows_of((buckets, SORT))
+    marks = [jnp.where(number == k, 1.0, 0.0) for k in bucket]
+    first = [jnp.sum(jnp.where(k < number, 1.0, 0.0), axis=1, keepdims=True) for k in bucket]
+    before = counted_before(jnp.concatenate(marks, axis=0)) + jnp.concatenate(first, axis=0)
+    position = [
+        jnp.sum(marks[s] * before[buckets * s : buckets * (s + 1)], axis=0, keepdims=True)
+        for s in range(RUNS)
+    ]
+    position = [p.astype(I32) for p in position]
+    row, found = rows_of((24, SORT)), []
+    for s in range(RUNS):
+        slot, weight, place = (run_of(x, s) for x in (slot_ref[...], weight_ref[...], places))
+        value = jnp.zeros((24, SORT), I32)
         for q, part in enumerate((slot & 255, slot >> 8, weight, place & 255, place >> 8)):
-            value = jnp.where(field == q, part, value)
-        fields = dot(value.astype(F32).astype(BF16), order, NT).astype(I32)
+            value = jnp.where((row >> 2) == q, part, value)
+        held = pick((row & 3) == position[s] // quarter, value.astype(F32))
+        found.append(dot(held, onehot(quarter, position[s] % quarter), NT).astype(I32))
+    for s in range(RUNS):
+        at, f = slice(quarter * s, quarter * (s + 1)), found[s]
+        field_ref[0:4, at] = f[0:4] + 256 * f[4:8]
+        field_ref[4:8, at] = f[8:12]
+        field_ref[8:12, at] = f[12:16] + 256 * f[16:20]
+        field_ref[12:16, at] = jnp.zeros((4, quarter), I32)
+    for s in range(RUNS):
+        fetched[s].wait()
+        moved = dot(onehot(SORT, position[s]), payload_ref[SORT * s : SORT * (s + 1), :])
         for j in range(4):
-            at = slice(512 * j + 256 * s, 512 * j + 256 * (s + 1))
-            part = slice(256 * j, 256 * (j + 1))
-            out_ref[at, :] = moved[part]
-            field_ref[:, at] = fields[:, part]
-
-
-def sort(h, core, slot, group, weight, payload):
-    rows = SORT_RUNS * SORT
+            out_ref[j, quarter * s : quarter * (s + 1), :] = moved[
+                quarter * j : quarter * (j + 1)
+            ].astype(BF16)
+
+
+def sort(core, slot, group, weight, payload):
     return pl.pallas_call(
-        functools.partial(sort_kernel, h),
-        out_shape=[pltpu.HBM((rows, D), BF16), pltpu.HBM((8, rows), I32)],
+        sort_kernel,
+        out_shape=[
+            jax.ShapeDtypeStruct((4, A_DEV // 4, D), BF16),
+            jax.ShapeDtypeStruct((16, A_DEV // 4), I32),
+        ],
         in_specs=[SMEM] + [VMEM] * 3 + [HBM],
         out_specs=[VMEM] * 2,
-        scratch_shapes=[pltpu.VMEM((rows, D), BF16), pltpu.SemaphoreType.DMA],
+        scratch_shapes=[pltpu.VMEM((A_DEV, D), BF16), pltpu.SemaphoreType.DMA((RUNS,))],
         compiler_params=LIMIT,
+        name="sort",
     )(core, *(in_hbm(x.reshape(32, 128)) for x in (slot, group, weight)), in_hbm(payload))
 
 
 def join_a_kernel(view_ref, *refs):
-    db, sources, outs, table_hbm = refs[:4], refs[4:8], refs[8:10], refs[10]
-    table_ref, rows_ref, field_ref, in_sems, out_sems = refs[11:]
-    fetched = []
-    for h in range(2):
-        for n, (source, target) in enumerate(((sources[h + 2], field_ref), (sources[h], rows_ref))):
-            fetched.append(pltpu.make_async_copy(source, target.at[h], in_sems.at[2 * h + n]))
-            fetched[-1].start()
-    sent = []
+    db, (sorted_ref, field_ref), (terms_hbm, field_hbm, table_hbm) = refs[:4], refs[4:6], refs[6:9]
+    table_ref, rows_ref, sems = refs[9:]
+    sent = [pltpu.make_async_copy(field_ref, field_hbm, sems.at[8])]
     for s in range(4):
         at = pl.ds(((view_ref[0] + 4 - s) % 4) * 128, 128)
-        sent.append(pltpu.make_async_copy(db[s], table_hbm.at[at], out_sems.at[8 + s]))
+        sent.append(pltpu.make_async_copy(db[s], table_hbm.at[at], sems.at[4 + s]))
+    for copy in sent:
+        copy.start()
+    fill(table_ref, view_ref[0], lambda s: db[s][...])
+    for j in range(4):
+        weight = field_ref[4 + j : 5 + j, :].astype(F32)
+        rows_ref[j] = terms_of(table_ref, field_ref[j : j + 1, :], weight, sorted_ref[j])
+        sent.append(pltpu.make_async_copy(rows_ref.at[j], terms_hbm.at[j], sems.at[j]))
         sent[-1].start()
-    fill(table_ref, view_ref[0], lambda s: db[s][...])
-    for h in range(2):
-        fetched[2 * h].wait()
-        fetched[2 * h + 1].wait()
-        for j in range(4):
-            part = pl.ds(512 * j, 512)
-            fields = field_ref[h, :, part]
-            slot = fields[0:1] + 256 * fields[1:2]
-            rows_ref[h, part, :] = terms_of(
-                table_ref, slot, fields[2:3].astype(F32), rows_ref[h, part, :]
-            )
-            sent.append(
-                pltpu.make_async_copy(
-                    rows_ref.at[h, part], outs[h].at[part], out_sems.at[4 * h + j]
-                )
-            )
-            sent[-1].start()
     for copy in sent:
         copy.wait()
 
@@ -302,8 +298,7 @@
 
     def window(j, at, size):
         chosen = onehot(size, line_ref[j : j + 1, :] - at)
-        rows = rows_ref[:, 512 * j : 512 * (j + 1), :].reshape(1024, D)
-        total_ref[pl.ds(pl.multiple_of(at - base, 64), size), :] += dot(chosen, rows)
+        total_ref[pl.ds(pl.multiple_of(at - base, 64), size), :] += dot(chosen, rows_ref[j])
 
     near = (2 * half, 2 * half + 1)
     first = [jnp.clip(start, base, base + GROUPS // 2) for start in starts]
@@ -320,105 +315,106 @@
         lax.fori_loop(0, (last - begin + STEP) // STEP, more, 0)
 
 
+def add_deltas(half, total_ref, place_ref, delta_ref):
+    for g in range(2):
+        chosen = onehot(1024, place_ref[...] - (half * (GROUPS // 2) + 1024 * g))
+        total_ref[1024 * g : 1024 * (g + 1), :] = dot(chosen, delta_ref[...])
+    total_ref[GROUPS // 2 :, :] = jnp.zeros((WINDOW, D), F32)
+
+
 def join_d_kernel(view_ref, core_ref, *refs):
-    db_ref, b, (first, second, fields0, fields1, in_ref) = refs[0], refs[1:5], refs[5:10]
-    peer_ref, delta_ref, place_ref, rows_ref, line_ref, bound_ref = refs[10:16]
-    whole_ref, field_ref, total_ref, sems = refs[16:]
-    copies = [
-        pltpu.make_async_copy(source, target, sems.at[n])
-        for n, (source, target) in enumerate(
-            (
-                (fields0, field_ref.at[0]),
-                (fields1, field_ref.at[1]),
-                (first, rows_ref.at[0]),
-                (second, rows_ref.at[1]),
-            )
-        )
-    ]
-    for copy in copies:
+    db_hbm, b, (field_hbm, terms_hbm, in_ref) = refs[0], refs[1:5], refs[5:8]
+    peer_ref, delta_ref, place_ref, rows_ref, line_ref, bound_ref = refs[8:14]
+    whole_ref, total_ref, db_ref, b_ref, field_ref, sems = refs[14:]
+    view, core = view_ref[0], core_ref[0]
+    tables = [pltpu.make_async_copy(db_hbm, db_ref, sems.at[0])]
+    for s in range(4):
+        at = pl.ds(((view + 4 - s) % 4) * 128, 128)
+        tables.append(pltpu.make_async_copy(b[s], b_ref.at[at], sems.at[1 + s]))
+    fields = pltpu.make_async_copy(field_hbm, field_ref, sems.at[5])
+    terms = pltpu.make_async_copy(terms_hbm, rows_ref, sems.at[6])
+    for copy in (*tables, fields, terms):
         copy.start()
-    view, core = view_ref[0], core_ref[0]
-    fill(
-        whole_ref, view, lambda s: b[s][...] + db_ref[pl.ds(((view + 4 - s) % 4) * 128, 128), :]
-    )
+    slots = []
     for c in range(8):
         slot, group = fields_of(in_ref, c)
+        place_ref[:, 256 * c : 256 * (c + 1)] = place_of(group, core)
+        slots.append(slot)
+    for copy in tables:
+        copy.wait()
+    whole = b_ref[...] + db_ref[...]
+    high = whole.astype(BF16)
+    whole_ref[:, :D] = high
+    whole_ref[:, D:] = (whole - high.astype(F32)).astype(BF16)
+    for c in range(8):
         at = slice(256 * c, 256 * (c + 1))
-        place_ref[:, at] = place_of(group, core)
-        delta_ref[at, :] = terms_of(whole_ref, slot, None, payload_of(in_ref, c))
-    copies[0].wait()
-    copies[1].wait()
+        delta_ref[at, :] = terms_of(whole_ref, slots[c], None, payload_of(in_ref, c))
+    fields.wait()
     starts, ends = [], []
     for j in range(4):
-        for h in range(2):
-            fields = field_ref[h, :, 512 * j : 512 * (j + 1)]
-            line_ref[j : j + 1, 512 * h : 512 * (h + 1)] = fields[3:4] + 256 * fields[4:5]
-        line = line_ref[j : j + 1, :]
+        line = field_ref[8 + j : 9 + j, :]
+        line_ref[j : j + 1, :] = line
         starts.append((jnp.min(line) >> 6) << 6)
         ends.append(jnp.max(line))
         bound_ref[j], bound_ref[4 + j] = starts[j], ends[j]
-    for g in range(GROUPS // 2 // 512):
-        chosen = onehot(512, place_ref[...] - 512 * g)
-        total_ref[512 * g : 512 * (g + 1), :] = dot(chosen, delta_ref[...])
-    total_ref[GROUPS // 2 :, :] = jnp.zeros((WINDOW, D), F32)
-    copies[2].wait()
-    copies[3].wait()
+    add_deltas(0, total_ref, place_ref, delta_ref)
+    terms.wait()
     add_windows(0, total_ref, rows_ref, line_ref, starts, ends)
     peer_ref[...] = total_ref[: GROUPS // 2, :]
 
 
 def own_kernel(bound_ref, delta_ref, place_ref, rows_ref, line_ref, out_ref, total_ref):
-    for g in range(GROUPS // 2 // 512):
-        chosen = onehot(512, place_ref[...] - GROUPS // 2 - 512 * g)
-        total_ref[512 * g : 512 * (g + 1), :] = dot(chosen, delta_ref[...])
-    total_ref[GROUPS // 2 :, :] = jnp.zeros((WINDOW, D), F32)
+    add_deltas(1, total_ref, place_ref, delta_ref)
     starts, ends = [bound_ref[j] for j in range(4)], [bound_ref[4 + j] for j in range(4)]
     add_windows(1, total_ref, rows_ref, line_ref, starts, ends)
     out_ref[...] = total_ref[: GROUPS // 2, :]
 
 
-def join(view, core, db, b, halves, received):
+def join(view, core, db, b, sorted_rows, received):
     rows = OWNERS * CAP
     table = pltpu.VMEM((KEYS_DEV, 2 * D), BF16)
     total = pltpu.VMEM((GROUPS // 2 + WINDOW, D), F32)
     half = jax.ShapeDtypeStruct((GROUPS // 2, D), F32)
-    fields = [in_hbm(halves[h][1]) for h in (0, 1)]
-    *terms, db_table = pl.pallas_call(
+    terms, fields, db_table = pl.pallas_call(
         join_a_kernel,
-        out_shape=[pltpu.HBM((A_DEV // 2, D), BF16)] * 2 + [pltpu.HBM((KEYS_DEV, D), F32)],
-        in_specs=[SMEM] + [VMEM] * 4 + [HBM] * 4,
+        out_shape=[
+            pltpu.HBM((4, A_DEV // 4, D), BF16),
+            pltpu.HBM((16, A_DEV // 4), I32),
+            pltpu.HBM((KEYS_DEV, D), F32),
+        ],
+        in_specs=[SMEM] + [VMEM] * 6,
         out_specs=[HBM] * 3,
         scratch_shapes=[
             table,
-            pltpu.VMEM((2, A_DEV // 2, D), BF16),
-            pltpu.VMEM((2, 8, A_DEV // 2), I32),
-            pltpu.SemaphoreType.DMA((4,)),
-            pltpu.SemaphoreType.DMA((12,)),
+            pltpu.VMEM((4, A_DEV // 4, D), BF16),
+            pltpu.SemaphoreType.DMA((9,)),
         ],
         compiler_params=LIMIT,
         name="join_a",
-    )(view, *db, in_hbm(halves[0][0]), in_hbm(halves[1][0]), *fields)
-    peer, delta, place, sorted_rows, line, bound = pl.pallas_call(
+    )(view, *db, *sorted_rows)
+    peer, delta, place, term_rows, line, bound = pl.pallas_call(
         join_d_kernel,
         out_shape=[
             half,
             jax.ShapeDtypeStruct((rows, D), BF16),
             jax.ShapeDtypeStruct((1, rows), I32),
-            jax.ShapeDtypeStruct((2, A_DEV // 2, D), BF16),
-            jax.ShapeDtypeStruct((4, 1024), I32),
+            jax.ShapeDtypeStruct((4, A_DEV // 4, D), BF16),
+            jax.ShapeDtypeStruct((4, A_DEV // 4), I32),
             jax.ShapeDtypeStruct((8,), I32),
         ],
-        in_specs=[SMEM] * 2 + [VMEM] * 5 + [HBM] * 4 + [VMEM],
+        in_specs=[SMEM] * 2 + [HBM] * 7 + [VMEM],
         out_specs=[VMEM] * 5 + [SMEM],
         scratch_shapes=[
             table,
-            pltpu.VMEM((2, 8, A_DEV // 2), I32),
             total,
-            pltpu.SemaphoreType.DMA((4,)),
+            pltpu.VMEM((KEYS_DEV, D), F32),
+            pltpu.VMEM((KEYS_DEV, D), F32),
+            pltpu.VMEM((16, A_DEV // 4), I32),
+            pltpu.SemaphoreType.DMA((7,)),
         ],
         compiler_params=pltpu.CompilerParams(vmem_limit_bytes=28 * 2**20),
         name="join_d",
-    )(view, core, in_hbm(db_table), *b, *map(in_hbm, terms), *fields, received)
+    )(view, core, *map(in_hbm, (db_table, *b, fields, terms)), received)
     other = lax.ppermute(peer, "keys_2", [(0, 1), (1, 0)])
     own = pl.pallas_call(
         own_kernel,
@@ -428,7 +424,7 @@
         scratch_shapes=[total],
         compiler_params=LIMIT,
         name="join_own",
-    )(bound, delta, place, sorted_rows, line)
+    )(bound, delta, place, term_rows, line)
     return (own + other).astype(BF16)
 
 
@@ -469,8 +465,8 @@
     )
     b = everyone(own_total(b_parts))
     db = everyone(own_total(slices(sum_db_kernel, view, db_in)))
-    halves = [sort(h, core, a_slot, a_group, a_weight, a_payload) for h in (0, 1)]
-    partial = join(view, core, db, b, halves, da_in)
+    sorted_rows = sort(core, a_slot, a_group, a_weight, a_payload)
+    partial = join(view, core, db, b, sorted_rows, da_in)
     blocks = partial.reshape(GROUPS // 2 // GROUPS_DEV, GROUPS_DEV, D)
     blocks = lax.all_to_all(blocks, ("keys_0", "keys_1", "view"), 0, 0, tiled=True)
     return jnp.sum(blocks.astype(F32), axis=0)

time: 122 us -> 116 us (0.951)
  Pallas kernels: 39.7 us -> 33.6 us
    pallas_call x3 -> x2, Pallas kernels: 16 us -> 8.79 us  [the longest x1 5.24 us: sort(): pl.pallas_call(sort_kernel, out_shape=[jax.ShapeDtypeStruct((4, A_DEV //...]
  transfers between devices with their start and end apart: 15 -> 15, of which waited for: 2 -> 2; matrix products, arithmetic and copies ran while one was open for 1% -> 1% of each run, Pallas kernels for 23% -> 19%
where the time goes in v6:
time: 116 us; the launch traced here: 115 us
  Pallas kernels  33.6 us (29%)
  starting transfers between devices  29 us (25%)
  blocking collectives  28.4 us (24%)
  waiting for transfers between devices  18.5 us (16%)
  local copies, waits for them, and re-layouts  2.31 us (2%)
  other arithmetic  2.15 us (2%)
  between operations  1.52 us (1%)
    all_to_all x1, blocking collectives, shards(): lax.all_to_all(blocks, ('keys_0', 'keys_1', 'view'), 0, 0, tiled=True)  28.4 us
    ppermute x12, starting transfers between devices, shift(): return lax.ppermute(x, 'view', [(j, (j + s) % 4) for j in range(4)])  16.2 us
    all_to_all x2, waiting for transfers between devices, exchange(): lax.all_to_all(blocks, KEYS, 0, 0, tiled=True).reshape(OWNERS * BLOCK, D)  13.2 us
    all_to_all x2, starting transfers between devices, exchange(): lax.all_to_all(blocks, KEYS, 0, 0, tiled=True).reshape(OWNERS * BLOCK, D)  12.5 us
    pallas_call x2, Pallas kernels, pack(): pl.pallas_call(lambda *refs: pack_kernel(group is not None, *refs), out_s...  8.73 us
    pallas_call x1, Pallas kernels, join(): pl.pallas_call(join_d_kernel, out_shape=[half, jax.ShapeDtypeStruct((rows...  7.7 us
    ppermute x12, waiting for transfers between devices, shift(): return lax.ppermute(x, 'view', [(j, (j + s) % 4) for j in range(4)])  5.31 us
    pallas_call x1, Pallas kernels, sort(): pl.pallas_call(sort_kernel, out_shape=[jax.ShapeDtypeStruct((4, A_DEV //...  5.24 us
  transfers between devices with their start and end apart: 15, of which 2 were waited for; matrix products, arithmetic and copies ran while one was open for 1% of the time, Pallas kernels for 19%

profile of v6, /device:TPU:0, one launch (start us, length us, event | category | flops | bytes accessed | tf_op | source)
XLA Modules:
  0.0 115.5 jit_solution(8782159244868988995)
XLA Ops:
  0.7 4.4 %pack_b.1 = bf16[2304,256]{1,0:T(8,128)(2,1)} custom-call(s32[1]{0:T(128)} %bitcast.2.refs_0_, s32[1]{0:T(128)S(6)} %copy.19.refs_1_, s32[128,128]{1,0:T(8,128)} %bitcast.24, s32[8,128]{1,0:T(8,128)} %bitcast.29, s32[8,128]{1,0:T(8,128)} %bitcast.30, bf16[1024,256]{1,0:T(8,128)(2,1)} %refs_5_.1), custom_call_target="tpu_custom_call" | custom-call | tf_op jit(solution)/shard_map/pack_b/pallas_call | solution.py:120
  5.0 8.5 %all-to-all-start = ((bf16[32,72,256]{2,1,0:T(8,128)(2,1)}), bf16[32,72,256]{2,1,0:T(8,128)(2,1)S(1)}, u32[]{:S(2)}, u32[]{:S(2)}) async-start(bf16[32,72,256]{2,1,0:T(8,128)(2,1)} %bitcast.6), calls=%async_computation | async-start | bytes 2359296 | tf_op jit(solution)/shard_map/all_to_all | solution.py:433
  14.2 4.4 %pack_a.1 = bf16[2304,256]{1,0:T(8,128)(2,1)} custom-call(s32[1]{0:T(128)} %bitcast.2.refs_0_, s32[1]{0:T(128)S(6)} %copy.18.refs_1_, s32[128,128]{1,0:T(8,128)} %bitcast.25, s32[8,128]{1,0:T(8,128)} %bitcast.31, s32[8,128]{1,0:T(8,128)} %bitcast.32, s32[8,128]{1,0:T(8,128)} %bitcast.33, bf16[1024,256]{1,0:T(8,128)(2,1)} %refs_6_.1), custom_call_target="tpu_custom_call" | custom-call | tf_op jit(solution)/shard_map/pack_a/pallas_call | solution.py:120
  18.5 0.0 copy-start.1
  18.5 13.2 %all-to-all-done = bf16[32,72,256]{2,1,0:T(8,128)(2,1)S(1)} async-done(((bf16[32,72,256]{2,1,0:T(8,128)(2,1)}), bf16[32,72,256]{2,1,0:T(8,128)(2,1)S(1)}, u32[]{:S(2)}, u32[]{:S(2)}) %all-to-all-start) | async-done | bytes 1179680 | tf_op jit(solution)/shard_map/all_to_all | solution.py:433
  31.7 4.0 %all-to-all-start.1 = ((bf16[32,72,256]{2,1,0:T(8,128)(2,1)}), bf16[32,72,256]{2,1,0:T(8,128)(2,1)S(1)}, u32[]{:S(2)}, u32[]{:S(2)}) async-start(bf16[32,72,256]{2,1,0:T(8,128)(2,1)} %bitcast.16), calls=%async_computation.1 | async-start | bytes 2359296 | tf_op jit(solution)/shard_map/all_to_all | solution.py:433
  35.8 1.4 %shard_map.163 = (f32[128,256]{1,0:T(8,128)}, f32[128,256]{1,0:T(8,128)S(1)}, f32[128,256]{1,0:T(8,128)S(1)}, f32[128,256]{1,0:T(8,128)S(1)}) custom-call(s32[1]{0:T(128)} %bitcast.view_ref, bf16[2304,256]{1,0:T(8,128)(2,1)S(1)} %bitcast.20), custom_call_target="tpu_custom_call" | custom-call | tf_op jit(solution)/shard_map/pallas_call | solution.py:171
  37.2 1.5 %collective-permute-start = (f32[128,256]{1,0:T(8,128)S(1)}, f32[128,256]{1,0:T(8,128)S(1)}, u32[]{:S(2)}, u32[]{:S(2)}) collective-permute-start(f32[128,256]{1,0:T(8,128)S(1)} %get-tuple-element.25), channel_id=1, source_target_pairs={{0,1},{1,2},{2,3},{3,0},{4,5},{5,6},{6,7},{7,4},{8,9},{9,10},{10,1... | collective-permute-start | bytes 393224 | tf_op jit(solution)/shard_map/ppermute | solution.py:182
  38.6 2.7 %collective-permute-start.1 = (f32[128,256]{1,0:T(8,128)S(1)}, f32[128,256]{1,0:T(8,128)S(1)}, u32[]{:S(2)}, u32[]{:S(2)}) collective-permute-start(f32[128,256]{1,0:T(8,128)S(1)} %get-tuple-element.26), channel_id=1, source_target_pairs={{0,2},{1,3},{2,0},{3,1},{4,6},{5,7},{6,4},{7,5},{8,10},{9,11},{10,... | collective-permute-start | bytes 393224 | tf_op jit(solution)/shard_map/ppermute | solution.py:182
  41.4 1.4 %collective-permute-start.2 = (f32[128,256]{1,0:T(8,128)S(1)}, f32[128,256]{1,0:T(8,128)S(1)}, u32[]{:S(2)}, u32[]{:S(2)}) collective-permute-start(f32[128,256]{1,0:T(8,128)S(1)} %get-tuple-element.27), channel_id=1, source_target_pairs={{0,3},{1,0},{2,1},{3,2},{4,7},{5,4},{6,5},{7,6},{8,11},{9,8},{10,9... | collective-permute-start | bytes 393224 | tf_op jit(solution)/shard_map/ppermute | solution.py:182
  42.8 1.6 %copy-done = bf16[4096,256]{1,0:T(8,128)(2,1)S(1)} copy-done((bf16[4096,256]{1,0:T(8,128)(2,1)S(1)}, bf16[4096,256]{1,0:T(8,128)(2,1)}, u32[]{:S(2)}) %copy-start) | copy-done | bytes 2097176
  44.4 1.9 %shard_map.164 = (f32[128,256]{1,0:T(8,128)}, f32[128,256]{1,0:T(8,128)S(1)}, f32[128,256]{1,0:T(8,128)S(1)}, f32[128,256]{1,0:T(8,128)S(1)}) custom-call(s32[1]{0:T(128)} %bitcast.view_ref, s32[32,128]{1,0:T(8,128)S(1)} %bitcast.21, s32[32,128]{1,0:T(8,128)S(1)} %bitcast.22, bf16[4096,256]{1,0:T(8,128)(2,1)S(1)} %copy-done), custom_call_target="tpu_custom_call" | custom-call | tf_op jit(solution)/shard_map/pallas_call | solution.py:171
  46.3 0.6 collective-permute-start.6
  46.9 0.9 collective-permute-start.7
  47.8 1.8 %collective-permute-start.8 = (f32[128,256]{1,0:T(8,128)S(1)}, f32[128,256]{1,0:T(8,128)S(1)}, u32[]{:S(2)}, u32[]{:S(2)}) collective-permute-start(f32[128,256]{1,0:T(8,128)S(1)} %get-tuple-element.34), channel_id=1, source_target_pairs={{0,3},{1,0},{2,1},{3,2},{4,7},{5,4},{6,5},{7,6},{8,11},{9,8},{10,9... | collective-permute-start | bytes 393224 | tf_op jit(solution)/shard_map/ppermute | solution.py:182
  49.7 1.5 %collective-permute-start.5 = (f32[128,256]{1,0:T(8,128)S(1)}, f32[128,256]{1,0:T(8,128)S(1)}, u32[]{:S(2)}, u32[]{:S(2)}) collective-permute-start(f32[128,256]{1,0:T(8,128)S(1)} %add_add_fusion.1.refs_0_), channel_id=1, source_target_pairs={{0,3},{1,0},{2,1},{3,2},{4,7},{5,4},{6,5},{7,6},{8,11},{9,8},{10,9... | collective-permute-start | bytes 393224 | tf_op jit(solution)/shard_map/ppermute | solution.py:182
  51.1 1.6 %collective-permute-start.4 = (f32[128,256]{1,0:T(8,128)S(1)}, f32[128,256]{1,0:T(8,128)S(1)}, u32[]{:S(2)}, u32[]{:S(2)}) collective-permute-start(f32[128,256]{1,0:T(8,128)S(1)} %add_add_fusion.1.refs_0_), channel_id=1, source_target_pairs={{0,2},{1,3},{2,0},{3,1},{4,6},{5,7},{6,4},{7,5},{8,10},{9,11},{10,... | collective-permute-start | bytes 393224 | tf_op jit(solution)/shard_map/ppermute | solution.py:182
  52.7 5.3 %collective-permute-done.6 = f32[128,256]{1,0:T(8,128)S(1)} collective-permute-done((f32[128,256]{1,0:T(8,128)S(1)}, f32[128,256]{1,0:T(8,128)S(1)}, u32[]{:S(2)}, u32[]{:S(2)}) %collective-permute-start.6) | collective-permute-done | bytes 131104 | tf_op jit(solution)/shard_map/ppermute | solution.py:182
  58.0 0.9 add_add_fusion.refs_1_
  59.0 3.3 %collective-permute-start.11 = (f32[128,256]{1,0:T(8,128)S(1)}, f32[128,256]{1,0:T(8,128)S(1)}, u32[]{:S(2)}, u32[]{:S(2)}) collective-permute-start(f32[128,256]{1,0:T(8,128)S(1)} %add_add_fusion.refs_1_), channel_id=1, source_target_pairs={{0,3},{1,0},{2,1},{3,2},{4,7},{5,4},{6,5},{7,6},{8,11},{9,8},{10,9... | collective-permute-start | bytes 393224 | tf_op jit(solution)/shard_map/ppermute | solution.py:182
  62.3 0.9 collective-permute-start.9
  63.2 5.2 %sort.1 = (bf16[4,1024,256]{2,1,0:T(8,128)(2,1)S(1)}, s32[16,1024]{1,0:T(8,128)S(1)}) custom-call(s32[1]{0:T(128)} %bitcast.1.core_ref, s32[32,128]{1,0:T(8,128)} %bitcast.26, s32[32,128]{1,0:T(8,128)} %bitcast.27, s32[32,128]{1,0:T(8,128)} %bitcast.28, bf16[4096,256]{1,0:T(8,128)(2,1)} %payload_hbm.1), custom_call_target="tpu_custom_call" | custom-call | tf_op jit(solution)/shard_map/sort/pallas_call | solution.py:263
  68.5 3.5 %join_a.1 = (bf16[4,1024,256]{2,1,0:T(8,128)(2,1)}, s32[16,1024]{1,0:T(8,128)}, f32[512,256]{1,0:T(8,128)}) custom-call(s32[1]{0:T(128)} %bitcast.view_ref, f32[128,256]{1,0:T(8,128)S(1)} %add_add_fusion.1.refs_0_, f32[128,256]{1,0:T(8,128)S(1)} %collective-permute-done.3.refs_1_, f32[128,256]{1,0:T(8,128)S(1)} %collective-permute-done.4.refs_2_, ...), custom_call_target="tpu_custom_call" | custom-call | tf_op jit(solution)/shard_map/join_a/pallas_call | solution.py:378
  72.1 0.6 copy-done.4
  72.7 0.0 copy-done.5
  72.8 0.1 copy-done.6
  72.8 7.7 %join_d.1 = (f32[2048,256]{1,0:T(8,128)S(1)}, bf16[2048,256]{1,0:T(8,128)(2,1)S(1)}, s32[1,2048]{1,0:T(1,128)S(1)}, bf16[4,1024,256]{2,1,0:T(8,128)(2,1)S(1)}, s32[4,1024]{1,0:T(4,128)S(1)}, /*index=5*/s32[8]{0:T(128)S(1)}) custom-call(s32[1]{0:T(128)} %bitcast.view_ref, s32[1]{0:T(128)} %bitcast.1.core_ref, f32[512,256]{1,0:T(8,128)} %get-tuple-element.30.refs_0_, ...), custom_call_target="tpu_custom_call" | custom-call | tf_op jit(solution)/shard_map/join_d/pallas_call | solution.py:395
  80.5 0.3 collective-permute-start.12
  80.8 5.1 %join_own.1 = f32[2048,256]{1,0:T(8,128)S(1)} custom-call(s32[8]{0:T(128)S(1)} %get-tuple-element.37.bound_ref, bf16[2048,256]{1,0:T(8,128)(2,1)S(1)} %get-tuple-element.38.delta_ref, s32[1,2048]{1,0:T(1,128)S(1)} %get-tuple-element.39.place_ref, bf16[4,1024,256]{2,1,0:T(8,128)(2,1)S(1)} %get-tuple-element.40.rows_ref, s32[4,1024]{1,0:T(4,128)S(1)} %get-tuple-element.41.line_ref), custom_call_target="tpu_custom_call" | custom-call | tf_op jit(solution)/shard_map/join_own/pallas_call | solution.py:419
  85.9 0.4 add_convert_fusion
  86.3 28.4 %all_to_all.15 = bf16[64,32,256]{2,1,0:T(8,128)(2,1)S(1)} all-to-all(bf16[64,32,256]{2,1,0:T(8,128)(2,1)S(1)} %bitcast.23), channel_id=1, replica_groups=mesh['keys_0'=4,'keys_1'=4,'keys_2'=2,'view'=4] {'keys_0','keys_1','view'}, dimensions={0} | all-to-all | bytes 2097152 | tf_op jit(solution)/shard_map/all_to_all | solution.py:471
  114.7 0.8 convert_reduce_fusion
  (27 shorter events, 0.1 us)
Async XLA Ops:
  5.0 26.7 %all-to-all-start = ((bf16[32,72,256]{2,1,0:T(8,128)(2,1)}), bf16[32,72,256]{2,1,0:T(8,128)(2,1)S(1)}, u32[]{:S(2)}, u32[]{:S(2)}) async-start(bf16[32,72,256]{2,1,0:T(8,128)(2,1)} %bitcast.6), calls=%async_computation | async-start | bytes 2359296 | tf_op jit(solution)/shard_map/all_to_all | solution.py:433
  18.5 24.3 %copy-start.1 = (s32[4096]{0:T(1024)S(1)}, s32[4096]{0:T(1024)}, u32[]{:S(2)}) copy-start(s32[4096]{0:T(1024)} %param.22) | copy-start | bytes 49156
  18.5 24.3 %copy-start.2 = (s32[4096]{0:T(1024)S(1)}, s32[4096]{0:T(1024)}, u32[]{:S(2)}) copy-start(s32[4096]{0:T(1024)} %param.23) | copy-start | bytes 49156
  31.7 40.4 %all-to-all-start.1 = ((bf16[32,72,256]{2,1,0:T(8,128)(2,1)}), bf16[32,72,256]{2,1,0:T(8,128)(2,1)S(1)}, u32[]{:S(2)}, u32[]{:S(2)}) async-start(bf16[32,72,256]{2,1,0:T(8,128)(2,1)} %bitcast.16), calls=%async_computation.1 | async-start | bytes 2359296 | tf_op jit(solution)/shard_map/all_to_all | solution.py:433
  37.2 10.7 %collective-permute-start = (f32[128,256]{1,0:T(8,128)S(1)}, f32[128,256]{1,0:T(8,128)S(1)}, u32[]{:S(2)}, u32[]{:S(2)}) collective-permute-start(f32[128,256]{1,0:T(8,128)S(1)} %get-tuple-element.25), channel_id=1, source_target_pairs={{0,1},{1,2},{2,3},{3,0},{4,5},{5,6},{6,7},{7,4},{8,9},{9,10},{10,1... | collective-permute-start | bytes 393224 | tf_op jit(solution)/shard_map/ppermute | solution.py:182
  38.6 11.0 %collective-permute-start.1 = (f32[128,256]{1,0:T(8,128)S(1)}, f32[128,256]{1,0:T(8,128)S(1)}, u32[]{:S(2)}, u32[]{:S(2)}) collective-permute-start(f32[128,256]{1,0:T(8,128)S(1)} %get-tuple-element.26), channel_id=1, source_target_pairs={{0,2},{1,3},{2,0},{3,1},{4,6},{5,7},{6,4},{7,5},{8,10},{9,11},{10,... | collective-permute-start | bytes 393224 | tf_op jit(solution)/shard_map/ppermute | solution.py:182
  41.4 8.2 %collective-permute-start.2 = (f32[128,256]{1,0:T(8,128)S(1)}, f32[128,256]{1,0:T(8,128)S(1)}, u32[]{:S(2)}, u32[]{:S(2)}) collective-permute-start(f32[128,256]{1,0:T(8,128)S(1)} %get-tuple-element.27), channel_id=1, source_target_pairs={{0,3},{1,0},{2,1},{3,2},{4,7},{5,4},{6,5},{7,6},{8,11},{9,8},{10,9... | collective-permute-start | bytes 393224 | tf_op jit(solution)/shard_map/ppermute | solution.py:182
  42.8 1.6 %copy-start = (bf16[4096,256]{1,0:T(8,128)(2,1)S(1)}, bf16[4096,256]{1,0:T(8,128)(2,1)}, u32[]{:S(2)}) copy-start(bf16[4096,256]{1,0:T(8,128)(2,1)} %payload_ref.1) | copy-start | bytes 6291460
  44.4 5.2 %copy-start.7 = (f32[128,256]{1,0:T(8,128)S(1)}, f32[128,256]{1,0:T(8,128)}, u32[]{:S(2)}) copy-start(f32[128,256]{1,0:T(8,128)} %get-tuple-element.24) | copy-start | bytes 393220
  46.3 11.7 %collective-permute-start.6 = (f32[128,256]{1,0:T(8,128)S(1)}, f32[128,256]{1,0:T(8,128)S(1)}, u32[]{:S(2)}, u32[]{:S(2)}) collective-permute-start(f32[128,256]{1,0:T(8,128)S(1)} %get-tuple-element.32), channel_id=1, source_target_pairs={{0,1},{1,2},{2,3},{3,0},{4,5},{5,6},{6,7},{7,4},{8,9},{9,10},{10,1... | collective-permute-start | bytes 393224 | tf_op jit(solution)/shard_map/ppermute | solution.py:182
  46.9 11.1 %collective-permute-start.7 = (f32[128,256]{1,0:T(8,128)S(1)}, f32[128,256]{1,0:T(8,128)S(1)}, u32[]{:S(2)}, u32[]{:S(2)}) collective-permute-start(f32[128,256]{1,0:T(8,128)S(1)} %get-tuple-element.33), channel_id=1, source_target_pairs={{0,2},{1,3},{2,0},{3,1},{4,6},{5,7},{6,4},{7,5},{8,10},{9,11},{10,... | collective-permute-start | bytes 393224 | tf_op jit(solution)/shard_map/ppermute | solution.py:182
  47.8 10.2 %collective-permute-start.8 = (f32[128,256]{1,0:T(8,128)S(1)}, f32[128,256]{1,0:T(8,128)S(1)}, u32[]{:S(2)}, u32[]{:S(2)}) collective-permute-start(f32[128,256]{1,0:T(8,128)S(1)} %get-tuple-element.34), channel_id=1, source_target_pairs={{0,3},{1,0},{2,1},{3,2},{4,7},{5,4},{6,5},{7,6},{8,11},{9,8},{10,9... | collective-permute-start | bytes 393224 | tf_op jit(solution)/shard_map/ppermute | solution.py:182
  49.7 12.6 %collective-permute-start.5 = (f32[128,256]{1,0:T(8,128)S(1)}, f32[128,256]{1,0:T(8,128)S(1)}, u32[]{:S(2)}, u32[]{:S(2)}) collective-permute-start(f32[128,256]{1,0:T(8,128)S(1)} %add_add_fusion.1.refs_0_), channel_id=1, source_target_pairs={{0,3},{1,0},{2,1},{3,2},{4,7},{5,4},{6,5},{7,6},{8,11},{9,8},{10,9... | collective-permute-start | bytes 393224 | tf_op jit(solution)/shard_map/ppermute | solution.py:182
  51.1 17.3 %collective-permute-start.4 = (f32[128,256]{1,0:T(8,128)S(1)}, f32[128,256]{1,0:T(8,128)S(1)}, u32[]{:S(2)}, u32[]{:S(2)}) collective-permute-start(f32[128,256]{1,0:T(8,128)S(1)} %add_add_fusion.1.refs_0_), channel_id=1, source_target_pairs={{0,2},{1,3},{2,0},{3,1},{4,6},{5,7},{6,4},{7,5},{8,10},{9,11},{10,... | collective-permute-start | bytes 393224 | tf_op jit(solution)/shard_map/ppermute | solution.py:182
  58.0 10.5 %collective-permute-start.3 = (f32[128,256]{1,0:T(8,128)S(1)}, f32[128,256]{1,0:T(8,128)S(1)}, u32[]{:S(2)}, u32[]{:S(2)}) collective-permute-start(f32[128,256]{1,0:T(8,128)S(1)} %add_add_fusion.1.refs_0_), channel_id=1, source_target_pairs={{0,1},{1,2},{2,3},{3,0},{4,5},{5,6},{6,7},{7,4},{8,9},{9,10},{10,1... | collective-permute-start | bytes 393224 | tf_op jit(solution)/shard_map/ppermute | solution.py:182
  59.0 13.1 %copy-start.3 = (f32[128,256]{1,0:T(8,128)}, f32[128,256]{1,0:T(8,128)S(1)}, u32[]{:S(2)}) copy-start(f32[128,256]{1,0:T(8,128)S(1)} %add_add_fusion.refs_1_) | copy-start | bytes 393220
  59.0 13.1 %collective-permute-start.11 = (f32[128,256]{1,0:T(8,128)S(1)}, f32[128,256]{1,0:T(8,128)S(1)}, u32[]{:S(2)}, u32[]{:S(2)}) collective-permute-start(f32[128,256]{1,0:T(8,128)S(1)} %add_add_fusion.refs_1_), channel_id=1, source_target_pairs={{0,3},{1,0},{2,1},{3,2},{4,7},{5,4},{6,5},{7,6},{8,11},{9,8},{10,9... | collective-permute-start | bytes 393224 | tf_op jit(solution)/shard_map/ppermute | solution.py:182
  62.3 9.8 %collective-permute-start.10 = (f32[128,256]{1,0:T(8,128)S(1)}, f32[128,256]{1,0:T(8,128)S(1)}, u32[]{:S(2)}, u32[]{:S(2)}) collective-permute-start(f32[128,256]{1,0:T(8,128)S(1)} %add_add_fusion.refs_1_), channel_id=1, source_target_pairs={{0,2},{1,3},{2,0},{3,1},{4,6},{5,7},{6,4},{7,5},{8,10},{9,11},{10,... | collective-permute-start | bytes 393224 | tf_op jit(solution)/shard_map/ppermute | solution.py:182
  62.3 9.8 %collective-permute-start.9 = (f32[128,256]{1,0:T(8,128)S(1)}, f32[128,256]{1,0:T(8,128)S(1)}, u32[]{:S(2)}, u32[]{:S(2)}) collective-permute-start(f32[128,256]{1,0:T(8,128)S(1)} %add_add_fusion.refs_1_), channel_id=1, source_target_pairs={{0,1},{1,2},{2,3},{3,0},{4,5},{5,6},{6,7},{7,4},{8,9},{9,10},{10,1... | collective-permute-start | bytes 393224 | tf_op jit(solution)/shard_map/ppermute | solution.py:182
  72.1 0.7 copy-start.4
  72.1 0.7 copy-start.5
  72.1 0.7 copy-start.6
  80.5 5.4 %collective-permute-start.12 = (f32[2048,256]{1,0:T(8,128)S(1)}, f32[2048,256]{1,0:T(8,128)S(1)}, u32[]{:S(2)}, u32[]{:S(2)}) collective-permute-start(f32[2048,256]{1,0:T(8,128)S(1)} %get-tuple-element.42), channel_id=1, source_target_pairs={{0,4},{4,0},{1,5},{5,1},{2,6},{6,2},{3,7},{7,3},{8,12},{12,8},{9,1... | collective-permute-start | bytes 6291464 | tf_op jit(solution)/shard_map/ppermute | solution.py:418

commit v7 on v6

--- a/solution.py
+++ b/solution.py
@@ -17,7 +17,8 @@
 CAP = 64
 BLOCK = CAP + 8
 SORT, RUNS = 512, 8
-WINDOW = 1472
+PARTS = 8
+WINDOW = 1024
 STEP = 256
 LIMIT = pltpu.CompilerParams(vmem_limit_bytes=16 * 2**20)
 KEYS = ("keys_0", "keys_1", "keys_2")
@@ -75,7 +76,7 @@
 
 def pack_kernel(with_group, me_ref, count_ref, table_ref, key_ref, mult_ref, *rest):
     group_ref = rest[0] if with_group else None
-    payload_hbm, out_ref, payload_ref, in_sem = rest[-4:]
+    payload_hbm, out_hbm, payload_ref, out_ref, in_sem, out_sems = rest[-6:]
     rows = DELTA_DEV
     fetch = pltpu.make_async_copy(payload_hbm, payload_ref, in_sem)
     fetch.start()
@@ -107,22 +108,32 @@
     for k in range(OWNERS):
         out_ref[pl.ds(k * BLOCK + CAP, 8), :] = fields[8 * k : 8 * k + 8]
     fetch.wait()
-    payload = payload_ref[...]
+    payload, sent = payload_ref[...], []
     for c in range(OWNERS // 4):
         chosen = onehot(4 * CAP, position - 4 * CAP * c, sign)
         packed = dot(chosen, payload).astype(BF16)
         for j in range(4):
             out_ref[pl.ds((4 * c + j) * BLOCK, CAP), :] = packed[CAP * j : CAP * (j + 1)]
+        part = pl.ds(4 * c * BLOCK, 4 * BLOCK)
+        sent.append(pltpu.make_async_copy(out_ref.at[part], out_hbm.at[part], out_sems.at[c]))
+        sent[-1].start()
+    for copy in sent:
+        copy.wait()
 
 
 def pack(me, count, table, key, mult, group, payload):
     extra = [] if group is None else [group.reshape(8, 128)]
     return pl.pallas_call(
         lambda *refs: pack_kernel(group is not None, *refs),
-        out_shape=jax.ShapeDtypeStruct((OWNERS * BLOCK, D), BF16),
+        out_shape=pltpu.HBM((OWNERS * BLOCK, D), BF16),
         in_specs=[SMEM, SMEM] + [VMEM] * (3 + len(extra)) + [HBM],
-        out_specs=VMEM,
-        scratch_shapes=[pltpu.VMEM((DELTA_DEV, D), BF16), pltpu.SemaphoreType.DMA],
+        out_specs=HBM,
+        scratch_shapes=[
+            pltpu.VMEM((DELTA_DEV, D), BF16),
+            pltpu.VMEM((OWNERS * BLOCK, D), BF16),
+            pltpu.SemaphoreType.DMA,
+            pltpu.SemaphoreType.DMA((OWNERS // 4,)),
+        ],
         compiler_params=LIMIT,
         name="pack_a" if extra else "pack_b",
     )(me, count, *map(in_hbm, (table, key.reshape(8, 128), mult.reshape(8, 128), *extra, payload)))
@@ -167,10 +178,10 @@
     spread(total_ref, view_ref[0], outs)
 
 
-def slices(kernel, view, *args):
+def slices(kernel, view, own, *args):
     return pl.pallas_call(
         kernel,
-        out_shape=[pltpu.HBM((128, D), F32)] + [jax.ShapeDtypeStruct((128, D), F32)] * 3,
+        out_shape=[own((128, D), F32)] + [jax.ShapeDtypeStruct((128, D), F32)] * 3,
         in_specs=[SMEM] + [VMEM] * len(args),
         out_specs=[VMEM] * 4,
         scratch_shapes=[pltpu.VMEM((KEYS_DEV, D), F32)],
@@ -220,7 +231,7 @@
             pltpu.make_async_copy(payload_hbm.at[part], payload_ref.at[part], sems.at[s])
         )
         fetched[-1].start()
-    buckets, quarter = GROUPS // 64, SORT // 4
+    buckets, part_rows = GROUPS // 64, SORT // PARTS
     places = place_of(group_ref[...], core_ref[0])
 
     def run_of(x, s):
@@ -236,26 +247,27 @@
         for s in range(RUNS)
     ]
     position = [p.astype(I32) for p in position]
-    row, found = rows_of((24, SORT)), []
+    row, found = rows_of((5 * PARTS, SORT)), []
     for s in range(RUNS):
         slot, weight, place = (run_of(x, s) for x in (slot_ref[...], weight_ref[...], places))
-        value = jnp.zeros((24, SORT), I32)
+        value = jnp.zeros((5 * PARTS, SORT), I32)
         for q, part in enumerate((slot & 255, slot >> 8, weight, place & 255, place >> 8)):
-            value = jnp.where((row >> 2) == q, part, value)
-        held = pick((row & 3) == position[s] // quarter, value.astype(F32))
-        found.append(dot(held, onehot(quarter, position[s] % quarter), NT).astype(I32))
-    for s in range(RUNS):
-        at, f = slice(quarter * s, quarter * (s + 1)), found[s]
-        field_ref[0:4, at] = f[0:4] + 256 * f[4:8]
-        field_ref[4:8, at] = f[8:12]
-        field_ref[8:12, at] = f[12:16] + 256 * f[16:20]
-        field_ref[12:16, at] = jnp.zeros((4, quarter), I32)
+            value = jnp.where((row >> 3) == q, part, value)
+        held = pick((row & 7) == position[s] >> 6, value.astype(F32))
+        lane = (position[s] & 63) + part_rows * (s % 2)
+        found.append(dot(held, onehot(2 * part_rows, lane), NT))
+    for s in range(0, RUNS, 2):
+        at = slice(part_rows * s, part_rows * (s + 2))
+        f = (found[s] + found[s + 1]).astype(I32)
+        field_ref[0:8, at] = f[0:8] + 256 * f[8:16]
+        field_ref[8:16, at] = f[16:24]
+        field_ref[16:24, at] = f[24:32] + 256 * f[32:40]
     for s in range(RUNS):
         fetched[s].wait()
         moved = dot(onehot(SORT, position[s]), payload_ref[SORT * s : SORT * (s + 1), :])
-        for j in range(4):
-            out_ref[j, quarter * s : quarter * (s + 1), :] = moved[
-                quarter * j : quarter * (j + 1)
+        for j in range(PARTS):
+            out_ref[j, part_rows * s : part_rows * (s + 1), :] = moved[
+                part_rows * j : part_rows * (j + 1)
             ].astype(BF16)
 
 
@@ -263,8 +275,8 @@
     return pl.pallas_call(
         sort_kernel,
         out_shape=[
-            jax.ShapeDtypeStruct((4, A_DEV // 4, D), BF16),
-            jax.ShapeDtypeStruct((16, A_DEV // 4), I32),
+            jax.ShapeDtypeStruct((PARTS, A_DEV // PARTS, D), BF16),
+            jax.ShapeDtypeStruct((3 * PARTS, A_DEV // PARTS), I32),
         ],
         in_specs=[SMEM] + [VMEM] * 3 + [HBM],
         out_specs=[VMEM] * 2,
@@ -277,15 +289,15 @@
 def join_a_kernel(view_ref, *refs):
     db, (sorted_ref, field_ref), (terms_hbm, field_hbm, table_hbm) = refs[:4], refs[4:6], refs[6:9]
     table_ref, rows_ref, sems = refs[9:]
-    sent = [pltpu.make_async_copy(field_ref, field_hbm, sems.at[8])]
+    sent = [pltpu.make_async_copy(field_ref, field_hbm, sems.at[PARTS])]
     for s in range(4):
         at = pl.ds(((view_ref[0] + 4 - s) % 4) * 128, 128)
-        sent.append(pltpu.make_async_copy(db[s], table_hbm.at[at], sems.at[4 + s]))
+        sent.append(pltpu.make_async_copy(db[s], table_hbm.at[at], sems.at[PARTS + 1 + s]))
     for copy in sent:
         copy.start()
     fill(table_ref, view_ref[0], lambda s: db[s][...])
-    for j in range(4):
-        weight = field_ref[4 + j : 5 + j, :].astype(F32)
+    for j in range(PARTS):
+        weight = field_ref[PARTS + j : PARTS + j + 1, :].astype(F32)
         rows_ref[j] = terms_of(table_ref, field_ref[j : j + 1, :], weight, sorted_ref[j])
         sent.append(pltpu.make_async_copy(rows_ref.at[j], terms_hbm.at[j], sems.at[j]))
         sent[-1].start()
@@ -300,11 +312,11 @@
         chosen = onehot(size, line_ref[j : j + 1, :] - at)
         total_ref[pl.ds(pl.multiple_of(at - base, 64), size), :] += dot(chosen, rows_ref[j])
 
-    near = (2 * half, 2 * half + 1)
+    near = range(PARTS // 2 * half, PARTS // 2 * (half + 1))
     first = [jnp.clip(start, base, base + GROUPS // 2) for start in starts]
     for j in near:
         window(j, first[j], WINDOW)
-    for j in range(4):
+    for j in range(PARTS):
         begin = first[j] + (WINDOW if j in near else 0)
         last = jnp.minimum(ends[j], base + GROUPS // 2 - 1)
 
@@ -351,12 +363,12 @@
         delta_ref[at, :] = terms_of(whole_ref, slots[c], None, payload_of(in_ref, c))
     fields.wait()
     starts, ends = [], []
-    for j in range(4):
-        line = field_ref[8 + j : 9 + j, :]
+    for j in range(PARTS):
+        line = field_ref[2 * PARTS + j : 2 * PARTS + j + 1, :]
         line_ref[j : j + 1, :] = line
         starts.append((jnp.min(line) >> 6) << 6)
         ends.append(jnp.max(line))
-        bound_ref[j], bound_ref[4 + j] = starts[j], ends[j]
+        bound_ref[j], bound_ref[PARTS + j] = starts[j], ends[j]
     add_deltas(0, total_ref, place_ref, delta_ref)
     terms.wait()
     add_windows(0, total_ref, rows_ref, line_ref, starts, ends)
@@ -365,7 +377,8 @@
 
 def own_kernel(bound_ref, delta_ref, place_ref, rows_ref, line_ref, out_ref, total_ref):
     add_deltas(1, total_ref, place_ref, delta_ref)
-    starts, ends = [bound_ref[j] for j in range(4)], [bound_ref[4 + j] for j in range(4)]
+    starts = [bound_ref[j] for j in range(PARTS)]
+    ends = [bound_ref[PARTS + j] for j in range(PARTS)]
     add_windows(1, total_ref, rows_ref, line_ref, starts, ends)
     out_ref[...] = total_ref[: GROUPS // 2, :]
 
@@ -378,16 +391,16 @@
     terms, fields, db_table = pl.pallas_call(
         join_a_kernel,
         out_shape=[
-            pltpu.HBM((4, A_DEV // 4, D), BF16),
-            pltpu.HBM((16, A_DEV // 4), I32),
+            pltpu.HBM((PARTS, A_DEV // PARTS, D), BF16),
+            pltpu.HBM((3 * PARTS, A_DEV // PARTS), I32),
             pltpu.HBM((KEYS_DEV, D), F32),
         ],
         in_specs=[SMEM] + [VMEM] * 6,
         out_specs=[HBM] * 3,
         scratch_shapes=[
             table,
-            pltpu.VMEM((4, A_DEV // 4, D), BF16),
-            pltpu.SemaphoreType.DMA((9,)),
+            pltpu.VMEM((PARTS, A_DEV // PARTS, D), BF16),
+            pltpu.SemaphoreType.DMA((PARTS + 5,)),
         ],
         compiler_params=LIMIT,
         name="join_a",
@@ -398,9 +411,9 @@
             half,
             jax.ShapeDtypeStruct((rows, D), BF16),
             jax.ShapeDtypeStruct((1, rows), I32),
-            jax.ShapeDtypeStruct((4, A_DEV // 4, D), BF16),
-            jax.ShapeDtypeStruct((4, A_DEV // 4), I32),
-            jax.ShapeDtypeStruct((8,), I32),
+            jax.ShapeDtypeStruct((PARTS, A_DEV // PARTS, D), BF16),
+            jax.ShapeDtypeStruct((PARTS, A_DEV // PARTS), I32),
+            jax.ShapeDtypeStruct((2 * PARTS,), I32),
         ],
         in_specs=[SMEM] * 2 + [HBM] * 7 + [VMEM],
         out_specs=[VMEM] * 5 + [SMEM],
@@ -409,7 +422,7 @@
             total,
             pltpu.VMEM((KEYS_DEV, D), F32),
             pltpu.VMEM((KEYS_DEV, D), F32),
-            pltpu.VMEM((16, A_DEV // 4), I32),
+            pltpu.VMEM((3 * PARTS, A_DEV // PARTS), I32),
             pltpu.SemaphoreType.DMA((7,)),
         ],
         compiler_params=pltpu.CompilerParams(vmem_limit_bytes=28 * 2**20),
@@ -461,10 +474,15 @@
     db_in = exchange(db_out)
     da_in = exchange(da_out)
     b_parts = slices(
-        sum_b_kernel, view, b_slot.reshape(32, 128), b_weight.reshape(32, 128), b_payload
+        sum_b_kernel,
+        view,
+        jax.ShapeDtypeStruct,
+        b_slot.reshape(32, 128),
+        b_weight.reshape(32, 128),
+        b_payload,
     )
     b = everyone(own_total(b_parts))
-    db = everyone(own_total(slices(sum_db_kernel, view, db_in)))
+    db = everyone(own_total(slices(sum_db_kernel, view, pltpu.HBM, db_in)))
     sorted_rows = sort(core, a_slot, a_group, a_weight, a_payload)
     partial = join(view, core, db, b, sorted_rows, da_in)
     blocks = partial.reshape(GROUPS // 2 // GROUPS_DEV, GROUPS_DEV, D)

time: 116 us -> 115 us (level)
  Pallas kernels: 33.6 us -> 31.5 us
  transfers between devices with their start and end apart: 15 -> 15, of which waited for: 2 -> 2; matrix products, arithmetic and copies ran while one was open for 1% -> 0% of each run, Pallas kernels for 19% -> 18%
where the time goes in v7:
time: 115 us; the launch traced here: 114 us
  Pallas kernels  31.5 us (27%)
  blocking collectives  29.2 us (25%)
  starting transfers between devices  28.8 us (25%)
  waiting for transfers between devices  19.3 us (17%)
  local copies, waits for them, and re-layouts  2.31 us (2%)
  between operations  1.53 us (1%)
  other arithmetic  1.25 us (1%)
    all_to_all x1, blocking collectives, shards(): lax.all_to_all(blocks, ('keys_0', 'keys_1', 'view'), 0, 0, tiled=True)  29.2 us
    ppermute x12, starting transfers between devices, shift(): return lax.ppermute(x, 'view', [(j, (j + s) % 4) for j in range(4)])  16.3 us
    all_to_all x2, waiting for transfers between devices, exchange(): lax.all_to_all(blocks, KEYS, 0, 0, tiled=True).reshape(OWNERS * BLOCK, D)  13.5 us
    all_to_all x2, starting transfers between devices, exchange(): lax.all_to_all(blocks, KEYS, 0, 0, tiled=True).reshape(OWNERS * BLOCK, D)  12.5 us
    pallas_call x2, Pallas kernels, pack(): pl.pallas_call(lambda *refs: pack_kernel(group is not None, *refs), out_s...  8.11 us
    pallas_call x1, Pallas kernels, join(): pl.pallas_call(join_d_kernel, out_shape=[half, jax.ShapeDtypeStruct((rows...  7.22 us
    ppermute x12, waiting for transfers between devices, shift(): return lax.ppermute(x, 'view', [(j, (j + s) % 4) for j in range(4)])  5.76 us
    pallas_call x1, Pallas kernels, sort(): pl.pallas_call(sort_kernel, out_shape=[jax.ShapeDtypeStruct((PARTS, A_DEV...  5.26 us
  transfers between devices with their start and end apart: 15, of which 2 were waited for; matrix products, arithmetic and copies ran while one was open for 0% of the time, Pallas kernels for 18%

profile of v7, /device:TPU:0, one launch (start us, length us, event | category | flops | bytes accessed | tf_op | source)
XLA Modules:
  0.0 113.9 jit_solution(15258850708446751679)
XLA Ops:
  0.7 4.0 %pack_b.1 = bf16[2304,256]{1,0:T(8,128)(2,1)} custom-call(s32[1]{0:T(128)} %bitcast.2.refs_0_, s32[1]{0:T(128)S(6)} %copy.19.refs_1_, s32[128,128]{1,0:T(8,128)} %bitcast.26, s32[8,128]{1,0:T(8,128)} %bitcast.31, s32[8,128]{1,0:T(8,128)} %bitcast.32, bf16[1024,256]{1,0:T(8,128)(2,1)} %refs_5_.1), custom_call_target="tpu_custom_call" | custom-call | tf_op jit(solution)/shard_map/pack_b/pallas_call | solution.py:126
  4.7 8.5 %all-to-all-start = ((bf16[32,72,256]{2,1,0:T(8,128)(2,1)}), bf16[32,72,256]{2,1,0:T(8,128)(2,1)S(1)}, u32[]{:S(2)}, u32[]{:S(2)}) async-start(bf16[32,72,256]{2,1,0:T(8,128)(2,1)} %bitcast.24), calls=%async_computation | async-start | bytes 2359296 | tf_op jit(solution)/shard_map/all_to_all | solution.py:446
  13.8 4.1 %pack_a.1 = bf16[2304,256]{1,0:T(8,128)(2,1)} custom-call(s32[1]{0:T(128)} %bitcast.2.refs_0_, s32[1]{0:T(128)S(6)} %copy.18.refs_1_, s32[128,128]{1,0:T(8,128)} %bitcast.27, s32[8,128]{1,0:T(8,128)} %bitcast.33, s32[8,128]{1,0:T(8,128)} %bitcast.34, s32[8,128]{1,0:T(8,128)} %bitcast.35, bf16[1024,256]{1,0:T(8,128)(2,1)} %refs_6_.1), custom_call_target="tpu_custom_call" | custom-call | tf_op jit(solution)/shard_map/pack_a/pallas_call | solution.py:126
  17.9 0.0 copy-start.1
  17.9 0.0 copy-start.2
  17.9 13.5 %all-to-all-done = bf16[32,72,256]{2,1,0:T(8,128)(2,1)S(1)} async-done(((bf16[32,72,256]{2,1,0:T(8,128)(2,1)}), bf16[32,72,256]{2,1,0:T(8,128)(2,1)S(1)}, u32[]{:S(2)}, u32[]{:S(2)}) %all-to-all-start) | async-done | bytes 1179680 | tf_op jit(solution)/shard_map/all_to_all | solution.py:446
  31.4 4.0 %all-to-all-start.1 = ((bf16[32,72,256]{2,1,0:T(8,128)(2,1)}), bf16[32,72,256]{2,1,0:T(8,128)(2,1)S(1)}, u32[]{:S(2)}, u32[]{:S(2)}) async-start(bf16[32,72,256]{2,1,0:T(8,128)(2,1)} %bitcast.23), calls=%async_computation.1 | async-start | bytes 2359296 | tf_op jit(solution)/shard_map/all_to_all | solution.py:446
  35.4 1.4 %shard_map.163 = (f32[128,256]{1,0:T(8,128)}, f32[128,256]{1,0:T(8,128)S(1)}, f32[128,256]{1,0:T(8,128)S(1)}, f32[128,256]{1,0:T(8,128)S(1)}) custom-call(s32[1]{0:T(128)} %bitcast.view_ref, bf16[2304,256]{1,0:T(8,128)(2,1)S(1)} %bitcast.20), custom_call_target="tpu_custom_call" | custom-call | tf_op jit(solution)/shard_map/pallas_call | solution.py:182
  36.8 1.5 %collective-permute-start = (f32[128,256]{1,0:T(8,128)S(1)}, f32[128,256]{1,0:T(8,128)S(1)}, u32[]{:S(2)}, u32[]{:S(2)}) collective-permute-start(f32[128,256]{1,0:T(8,128)S(1)} %get-tuple-element.25), channel_id=1, source_target_pairs={{0,1},{1,2},{2,3},{3,0},{4,5},{5,6},{6,7},{7,4},{8,9},{9,10},{10,1... | collective-permute-start | bytes 393224 | tf_op jit(solution)/shard_map/ppermute | solution.py:193
  38.3 2.7 %collective-permute-start.1 = (f32[128,256]{1,0:T(8,128)S(1)}, f32[128,256]{1,0:T(8,128)S(1)}, u32[]{:S(2)}, u32[]{:S(2)}) collective-permute-start(f32[128,256]{1,0:T(8,128)S(1)} %get-tuple-element.26), channel_id=1, source_target_pairs={{0,2},{1,3},{2,0},{3,1},{4,6},{5,7},{6,4},{7,5},{8,10},{9,11},{10,... | collective-permute-start | bytes 393224 | tf_op jit(solution)/shard_map/ppermute | solution.py:193
  41.1 1.4 %collective-permute-start.2 = (f32[128,256]{1,0:T(8,128)S(1)}, f32[128,256]{1,0:T(8,128)S(1)}, u32[]{:S(2)}, u32[]{:S(2)}) collective-permute-start(f32[128,256]{1,0:T(8,128)S(1)} %get-tuple-element.27), channel_id=1, source_target_pairs={{0,3},{1,0},{2,1},{3,2},{4,7},{5,4},{6,5},{7,6},{8,11},{9,8},{10,9... | collective-permute-start | bytes 393224 | tf_op jit(solution)/shard_map/ppermute | solution.py:193
  42.5 1.6 %copy-done = bf16[4096,256]{1,0:T(8,128)(2,1)S(1)} copy-done((bf16[4096,256]{1,0:T(8,128)(2,1)S(1)}, bf16[4096,256]{1,0:T(8,128)(2,1)}, u32[]{:S(2)}) %copy-start) | copy-done | bytes 2097176
  44.1 1.3 %shard_map.164 = (f32[128,256]{1,0:T(8,128)S(1)}, f32[128,256]{1,0:T(8,128)S(1)}, f32[128,256]{1,0:T(8,128)S(1)}, f32[128,256]{1,0:T(8,128)S(1)}) custom-call(s32[1]{0:T(128)} %bitcast.view_ref, s32[32,128]{1,0:T(8,128)S(1)} %bitcast.21, s32[32,128]{1,0:T(8,128)S(1)} %bitcast.22, bf16[4096,256]{1,0:T(8,128)(2,1)S(1)} %copy-done), custom_call_target="tpu_custom_call" | custom-call | tf_op jit(solution)/shard_map/pallas_call | solution.py:182
  45.4 0.7 collective-permute-start.6
  46.0 0.9 collective-permute-start.7
  46.9 1.9 %collective-permute-start.8 = (f32[128,256]{1,0:T(8,128)S(1)}, f32[128,256]{1,0:T(8,128)S(1)}, u32[]{:S(2)}, u32[]{:S(2)}) collective-permute-start(f32[128,256]{1,0:T(8,128)S(1)} %get-tuple-element.34), channel_id=1, source_target_pairs={{0,3},{1,0},{2,1},{3,2},{4,7},{5,4},{6,5},{7,6},{8,11},{9,8},{10,9... | collective-permute-start | bytes 393224 | tf_op jit(solution)/shard_map/ppermute | solution.py:193
  48.9 1.4 %collective-permute-start.5 = (f32[128,256]{1,0:T(8,128)S(1)}, f32[128,256]{1,0:T(8,128)S(1)}, u32[]{:S(2)}, u32[]{:S(2)}) collective-permute-start(f32[128,256]{1,0:T(8,128)S(1)} %add_add_fusion.1.refs_0_), channel_id=1, source_target_pairs={{0,3},{1,0},{2,1},{3,2},{4,7},{5,4},{6,5},{7,6},{8,11},{9,8},{10,9... | collective-permute-start | bytes 393224 | tf_op jit(solution)/shard_map/ppermute | solution.py:193
  50.3 1.6 %collective-permute-start.4 = (f32[128,256]{1,0:T(8,128)S(1)}, f32[128,256]{1,0:T(8,128)S(1)}, u32[]{:S(2)}, u32[]{:S(2)}) collective-permute-start(f32[128,256]{1,0:T(8,128)S(1)} %add_add_fusion.1.refs_0_), channel_id=1, source_target_pairs={{0,2},{1,3},{2,0},{3,1},{4,6},{5,7},{6,4},{7,5},{8,10},{9,11},{10,... | collective-permute-start | bytes 393224 | tf_op jit(solution)/shard_map/ppermute | solution.py:193
  51.8 5.7 %collective-permute-done.6 = f32[128,256]{1,0:T(8,128)S(1)} collective-permute-done((f32[128,256]{1,0:T(8,128)S(1)}, f32[128,256]{1,0:T(8,128)S(1)}, u32[]{:S(2)}, u32[]{:S(2)}) %collective-permute-start.6) | collective-permute-done | bytes 131104 | tf_op jit(solution)/shard_map/ppermute | solution.py:193
  57.6 3.3 %collective-permute-start.11 = (f32[128,256]{1,0:T(8,128)S(1)}, f32[128,256]{1,0:T(8,128)S(1)}, u32[]{:S(2)}, u32[]{:S(2)}) collective-permute-start(f32[128,256]{1,0:T(8,128)S(1)} %add_add_fusion.refs_1_), channel_id=1, source_target_pairs={{0,3},{1,0},{2,1},{3,2},{4,7},{5,4},{6,5},{7,6},{8,11},{9,8},{10,9... | collective-permute-start | bytes 393224 | tf_op jit(solution)/shard_map/ppermute | solution.py:193
  60.9 0.9 collective-permute-start.9
  61.9 5.3 %sort.1 = (bf16[8,512,256]{2,1,0:T(8,128)(2,1)S(1)}, s32[24,512]{1,0:T(8,128)S(1)}) custom-call(s32[1]{0:T(128)} %bitcast.1.core_ref, s32[32,128]{1,0:T(8,128)} %bitcast.28, s32[32,128]{1,0:T(8,128)} %bitcast.29, s32[32,128]{1,0:T(8,128)} %bitcast.30, bf16[4096,256]{1,0:T(8,128)(2,1)} %payload_hbm.1), custom_call_target="tpu_custom_call" | custom-call | tf_op jit(solution)/shard_map/sort/pallas_call | solution.py:275
  67.2 3.4 %join_a.1 = (bf16[8,512,256]{2,1,0:T(8,128)(2,1)}, s32[24,512]{1,0:T(8,128)}, f32[512,256]{1,0:T(8,128)}) custom-call(s32[1]{0:T(128)} %bitcast.view_ref, f32[128,256]{1,0:T(8,128)S(1)} %add_add_fusion.1.refs_0_, f32[128,256]{1,0:T(8,128)S(1)} %collective-permute-done.3.refs_1_, f32[128,256]{1,0:T(8,128)S(1)} %collective-permute-done.4.refs_2_, ...), custom_call_target="tpu_custom_call" | custom-call | tf_op jit(solution)/shard_map/join_a/pallas_call | solution.py:391
  70.7 0.6 copy-done.4
  71.3 0.0 copy-done.5
  71.3 0.1 copy-done.6
  71.4 7.2 %join_d.1 = (f32[2048,256]{1,0:T(8,128)S(1)}, bf16[2048,256]{1,0:T(8,128)(2,1)S(1)}, s32[1,2048]{1,0:T(1,128)S(1)}, bf16[8,512,256]{2,1,0:T(8,128)(2,1)S(1)}, s32[8,512]{1,0:T(8,128)S(1)}, /*index=5*/s32[16]{0:T(128)S(1)}) custom-call(s32[1]{0:T(128)} %bitcast.view_ref, s32[1]{0:T(128)} %bitcast.1.core_ref, f32[512,256]{1,0:T(8,128)} %get-tuple-element.30.refs_0_, ...), custom_call_target="tpu_custom_call" | custom-call | tf_op jit(solution)/shard_map/join_d/pallas_call | solution.py:408
  78.6 0.1 collective-permute-start.12
  78.7 4.8 %join_own.1 = f32[2048,256]{1,0:T(8,128)S(1)} custom-call(s32[16]{0:T(128)S(1)} %get-tuple-element.37.bound_ref, bf16[2048,256]{1,0:T(8,128)(2,1)S(1)} %get-tuple-element.38.delta_ref, s32[1,2048]{1,0:T(1,128)S(1)} %get-tuple-element.39.place_ref, bf16[8,512,256]{2,1,0:T(8,128)(2,1)S(1)} %get-tuple-element.40.rows_ref, s32[8,512]{1,0:T(8,128)S(1)} %get-tuple-element.41.line_ref), custom_call_target="tpu_custom_call" | custom-call | tf_op jit(solution)/shard_map/join_own/pallas_call | solution.py:432
  83.5 0.4 add_convert_fusion
  83.9 29.2 %all_to_all.15 = bf16[64,32,256]{2,1,0:T(8,128)(2,1)S(1)} all-to-all(bf16[64,32,256]{2,1,0:T(8,128)(2,1)S(1)} %bitcast.25), channel_id=1, replica_groups=mesh['keys_0'=4,'keys_1'=4,'keys_2'=2,'view'=4] {'keys_0','keys_1','view'}, dimensions={0} | all-to-all | bytes 2097152 | tf_op jit(solution)/shard_map/all_to_all | solution.py:489
  113.1 0.8 convert_reduce_fusion
  (27 shorter events, 0.1 us)
Async XLA Ops:
  4.7 26.7 %all-to-all-start = ((bf16[32,72,256]{2,1,0:T(8,128)(2,1)}), bf16[32,72,256]{2,1,0:T(8,128)(2,1)S(1)}, u32[]{:S(2)}, u32[]{:S(2)}) async-start(bf16[32,72,256]{2,1,0:T(8,128)(2,1)} %bitcast.24), calls=%async_computation | async-start | bytes 2359296 | tf_op jit(solution)/shard_map/all_to_all | solution.py:446
  17.9 24.6 %copy-start.1 = (s32[4096]{0:T(1024)S(1)}, s32[4096]{0:T(1024)}, u32[]{:S(2)}) copy-start(s32[4096]{0:T(1024)} %param.22) | copy-start | bytes 49156
  17.9 24.6 %copy-start.2 = (s32[4096]{0:T(1024)S(1)}, s32[4096]{0:T(1024)}, u32[]{:S(2)}) copy-start(s32[4096]{0:T(1024)} %param.23) | copy-start | bytes 49156
  31.4 39.3 %all-to-all-start.1 = ((bf16[32,72,256]{2,1,0:T(8,128)(2,1)}), bf16[32,72,256]{2,1,0:T(8,128)(2,1)S(1)}, u32[]{:S(2)}, u32[]{:S(2)}) async-start(bf16[32,72,256]{2,1,0:T(8,128)(2,1)} %bitcast.23), calls=%async_computation.1 | async-start | bytes 2359296 | tf_op jit(solution)/shard_map/all_to_all | solution.py:446
  36.8 10.1 %collective-permute-start = (f32[128,256]{1,0:T(8,128)S(1)}, f32[128,256]{1,0:T(8,128)S(1)}, u32[]{:S(2)}, u32[]{:S(2)}) collective-permute-start(f32[128,256]{1,0:T(8,128)S(1)} %get-tuple-element.25), channel_id=1, source_target_pairs={{0,1},{1,2},{2,3},{3,0},{4,5},{5,6},{6,7},{7,4},{8,9},{9,10},{10,1... | collective-permute-start | bytes 393224 | tf_op jit(solution)/shard_map/ppermute | solution.py:193
  38.3 10.5 %collective-permute-start.1 = (f32[128,256]{1,0:T(8,128)S(1)}, f32[128,256]{1,0:T(8,128)S(1)}, u32[]{:S(2)}, u32[]{:S(2)}) collective-permute-start(f32[128,256]{1,0:T(8,128)S(1)} %get-tuple-element.26), channel_id=1, source_target_pairs={{0,2},{1,3},{2,0},{3,1},{4,6},{5,7},{6,4},{7,5},{8,10},{9,11},{10,... | collective-permute-start | bytes 393224 | tf_op jit(solution)/shard_map/ppermute | solution.py:193
  41.1 7.8 %collective-permute-start.2 = (f32[128,256]{1,0:T(8,128)S(1)}, f32[128,256]{1,0:T(8,128)S(1)}, u32[]{:S(2)}, u32[]{:S(2)}) collective-permute-start(f32[128,256]{1,0:T(8,128)S(1)} %get-tuple-element.27), channel_id=1, source_target_pairs={{0,3},{1,0},{2,1},{3,2},{4,7},{5,4},{6,5},{7,6},{8,11},{9,8},{10,9... | collective-permute-start | bytes 393224 | tf_op jit(solution)/shard_map/ppermute | solution.py:193
  42.5 1.6 %copy-start = (bf16[4096,256]{1,0:T(8,128)(2,1)S(1)}, bf16[4096,256]{1,0:T(8,128)(2,1)}, u32[]{:S(2)}) copy-start(bf16[4096,256]{1,0:T(8,128)(2,1)} %payload_ref.1) | copy-start | bytes 6291460
  44.1 4.7 %copy-start.7 = (f32[128,256]{1,0:T(8,128)S(1)}, f32[128,256]{1,0:T(8,128)}, u32[]{:S(2)}) copy-start(f32[128,256]{1,0:T(8,128)} %get-tuple-element.24) | copy-start | bytes 393220
  45.4 12.2 %collective-permute-start.6 = (f32[128,256]{1,0:T(8,128)S(1)}, f32[128,256]{1,0:T(8,128)S(1)}, u32[]{:S(2)}, u32[]{:S(2)}) collective-permute-start(f32[128,256]{1,0:T(8,128)S(1)} %get-tuple-element.32), channel_id=1, source_target_pairs={{0,1},{1,2},{2,3},{3,0},{4,5},{5,6},{6,7},{7,4},{8,9},{9,10},{10,1... | collective-permute-start | bytes 393224 | tf_op jit(solution)/shard_map/ppermute | solution.py:193
  46.0 11.5 %collective-permute-start.7 = (f32[128,256]{1,0:T(8,128)S(1)}, f32[128,256]{1,0:T(8,128)S(1)}, u32[]{:S(2)}, u32[]{:S(2)}) collective-permute-start(f32[128,256]{1,0:T(8,128)S(1)} %get-tuple-element.33), channel_id=1, source_target_pairs={{0,2},{1,3},{2,0},{3,1},{4,6},{5,7},{6,4},{7,5},{8,10},{9,11},{10,... | collective-permute-start | bytes 393224 | tf_op jit(solution)/shard_map/ppermute | solution.py:193
  46.9 10.6 %collective-permute-start.8 = (f32[128,256]{1,0:T(8,128)S(1)}, f32[128,256]{1,0:T(8,128)S(1)}, u32[]{:S(2)}, u32[]{:S(2)}) collective-permute-start(f32[128,256]{1,0:T(8,128)S(1)} %get-tuple-element.34), channel_id=1, source_target_pairs={{0,3},{1,0},{2,1},{3,2},{4,7},{5,4},{6,5},{7,6},{8,11},{9,8},{10,9... | collective-permute-start | bytes 393224 | tf_op jit(solution)/shard_map/ppermute | solution.py:193
  48.9 12.1 %collective-permute-start.5 = (f32[128,256]{1,0:T(8,128)S(1)}, f32[128,256]{1,0:T(8,128)S(1)}, u32[]{:S(2)}, u32[]{:S(2)}) collective-permute-start(f32[128,256]{1,0:T(8,128)S(1)} %add_add_fusion.1.refs_0_), channel_id=1, source_target_pairs={{0,3},{1,0},{2,1},{3,2},{4,7},{5,4},{6,5},{7,6},{8,11},{9,8},{10,9... | collective-permute-start | bytes 393224 | tf_op jit(solution)/shard_map/ppermute | solution.py:193
  50.3 16.9 %collective-permute-start.4 = (f32[128,256]{1,0:T(8,128)S(1)}, f32[128,256]{1,0:T(8,128)S(1)}, u32[]{:S(2)}, u32[]{:S(2)}) collective-permute-start(f32[128,256]{1,0:T(8,128)S(1)} %add_add_fusion.1.refs_0_), channel_id=1, source_target_pairs={{0,2},{1,3},{2,0},{3,1},{4,6},{5,7},{6,4},{7,5},{8,10},{9,11},{10,... | collective-permute-start | bytes 393224 | tf_op jit(solution)/shard_map/ppermute | solution.py:193
  57.6 9.6 %collective-permute-start.3 = (f32[128,256]{1,0:T(8,128)S(1)}, f32[128,256]{1,0:T(8,128)S(1)}, u32[]{:S(2)}, u32[]{:S(2)}) collective-permute-start(f32[128,256]{1,0:T(8,128)S(1)} %add_add_fusion.1.refs_0_), channel_id=1, source_target_pairs={{0,1},{1,2},{2,3},{3,0},{4,5},{5,6},{6,7},{7,4},{8,9},{9,10},{10,1... | collective-permute-start | bytes 393224 | tf_op jit(solution)/shard_map/ppermute | solution.py:193
  57.6 13.0 %copy-start.3 = (f32[128,256]{1,0:T(8,128)}, f32[128,256]{1,0:T(8,128)S(1)}, u32[]{:S(2)}) copy-start(f32[128,256]{1,0:T(8,128)S(1)} %add_add_fusion.refs_1_) | copy-start | bytes 393220
  57.6 13.0 %collective-permute-start.11 = (f32[128,256]{1,0:T(8,128)S(1)}, f32[128,256]{1,0:T(8,128)S(1)}, u32[]{:S(2)}, u32[]{:S(2)}) collective-permute-start(f32[128,256]{1,0:T(8,128)S(1)} %add_add_fusion.refs_1_), channel_id=1, source_target_pairs={{0,3},{1,0},{2,1},{3,2},{4,7},{5,4},{6,5},{7,6},{8,11},{9,8},{10,9... | collective-permute-start | bytes 393224 | tf_op jit(solution)/shard_map/ppermute | solution.py:193
  60.9 9.7 %collective-permute-start.10 = (f32[128,256]{1,0:T(8,128)S(1)}, f32[128,256]{1,0:T(8,128)S(1)}, u32[]{:S(2)}, u32[]{:S(2)}) collective-permute-start(f32[128,256]{1,0:T(8,128)S(1)} %add_add_fusion.refs_1_), channel_id=1, source_target_pairs={{0,2},{1,3},{2,0},{3,1},{4,6},{5,7},{6,4},{7,5},{8,10},{9,11},{10,... | collective-permute-start | bytes 393224 | tf_op jit(solution)/shard_map/ppermute | solution.py:193
  60.9 9.7 %collective-permute-start.9 = (f32[128,256]{1,0:T(8,128)S(1)}, f32[128,256]{1,0:T(8,128)S(1)}, u32[]{:S(2)}, u32[]{:S(2)}) collective-permute-start(f32[128,256]{1,0:T(8,128)S(1)} %add_add_fusion.refs_1_), channel_id=1, source_target_pairs={{0,1},{1,2},{2,3},{3,0},{4,5},{5,6},{6,7},{7,4},{8,9},{9,10},{10,1... | collective-permute-start | bytes 393224 | tf_op jit(solution)/shard_map/ppermute | solution.py:193
  70.6 0.7 copy-start.4
  70.6 0.7 copy-start.5
  70.7 0.7 copy-start.6
  78.6 4.9 %collective-permute-start.12 = (f32[2048,256]{1,0:T(8,128)S(1)}, f32[2048,256]{1,0:T(8,128)S(1)}, u32[]{:S(2)}, u32[]{:S(2)}) collective-permute-start(f32[2048,256]{1,0:T(8,128)S(1)} %get-tuple-element.42), channel_id=1, source_target_pairs={{0,4},{4,0},{1,5},{5,1},{2,6},{6,2},{3,7},{7,3},{8,12},{12,8},{9,1... | collective-permute-start | bytes 6291464 | tf_op jit(solution)/shard_map/ppermute | solution.py:431

commit v8 on v7

--- a/solution.py
+++ b/solution.py
@@ -287,20 +287,24 @@
 
 
 def join_a_kernel(view_ref, *refs):
-    db, (sorted_ref, field_ref), (terms_hbm, field_hbm, table_hbm) = refs[:4], refs[4:6], refs[6:9]
-    table_ref, rows_ref, sems = refs[9:]
+    db, b, (sorted_ref, field_ref) = refs[:4], refs[4:8], refs[8:10]
+    terms_hbm, field_hbm, whole_hbm, bound_ref = refs[10:14]
+    table_ref, whole_ref, rows_ref, sems = refs[14:]
     sent = [pltpu.make_async_copy(field_ref, field_hbm, sems.at[PARTS])]
-    for s in range(4):
-        at = pl.ds(((view_ref[0] + 4 - s) % 4) * 128, 128)
-        sent.append(pltpu.make_async_copy(db[s], table_hbm.at[at], sems.at[PARTS + 1 + s]))
-    for copy in sent:
-        copy.start()
+    sent[0].start()
     fill(table_ref, view_ref[0], lambda s: db[s][...])
+    fill(whole_ref, view_ref[0], lambda s: b[s][...] + db[s][...])
+    sent.append(pltpu.make_async_copy(whole_ref, whole_hbm, sems.at[PARTS + 1]))
+    sent[1].start()
     for j in range(PARTS):
         weight = field_ref[PARTS + j : PARTS + j + 1, :].astype(F32)
         rows_ref[j] = terms_of(table_ref, field_ref[j : j + 1, :], weight, sorted_ref[j])
         sent.append(pltpu.make_async_copy(rows_ref.at[j], terms_hbm.at[j], sems.at[j]))
         sent[-1].start()
+    for j in range(PARTS):
+        line = field_ref[2 * PARTS + j : 2 * PARTS + j + 1, :]
+        bound_ref[j] = (jnp.min(line) >> 6) << 6
+        bound_ref[PARTS + j] = jnp.max(line)
     for copy in sent:
         copy.wait()
 
@@ -334,52 +338,47 @@
     total_ref[GROUPS // 2 :, :] = jnp.zeros((WINDOW, D), F32)
 
 
-def join_d_kernel(view_ref, core_ref, *refs):
-    db_hbm, b, (field_hbm, terms_hbm, in_ref) = refs[0], refs[1:5], refs[5:8]
-    peer_ref, delta_ref, place_ref, rows_ref, line_ref, bound_ref = refs[8:14]
-    whole_ref, total_ref, db_ref, b_ref, field_ref, sems = refs[14:]
-    view, core = view_ref[0], core_ref[0]
-    tables = [pltpu.make_async_copy(db_hbm, db_ref, sems.at[0])]
-    for s in range(4):
-        at = pl.ds(((view + 4 - s) % 4) * 128, 128)
-        tables.append(pltpu.make_async_copy(b[s], b_ref.at[at], sems.at[1 + s]))
-    fields = pltpu.make_async_copy(field_hbm, field_ref, sems.at[5])
-    terms = pltpu.make_async_copy(terms_hbm, rows_ref, sems.at[6])
-    for copy in (*tables, fields, terms):
+def bounds(bound_ref):
+    return [[bound_ref[h * PARTS + j] for j in range(PARTS)] for h in (0, 1)]
+
+
+def join_d_kernel(core_ref, *refs):
+    bound_hbm, whole_hbm, field_hbm, terms_hbm, in_ref = refs[:5]
+    peer_ref, delta_ref, place_ref, rows_ref, line_ref, bound_ref = refs[5:11]
+    whole_ref, total_ref, sems = refs[11:]
+    lines = field_hbm.at[pl.ds(2 * PARTS, PARTS)]
+    copies = [
+        pltpu.make_async_copy(source, target, sems.at[n])
+        for n, (source, target) in enumerate(
+            (
+                (whole_hbm, whole_ref),
+                (lines, line_ref),
+                (bound_hbm, bound_ref),
+                (terms_hbm, rows_ref),
+            )
+        )
+    ]
+    for copy in copies:
         copy.start()
     slots = []
     for c in range(8):
         slot, group = fields_of(in_ref, c)
-        place_ref[:, 256 * c : 256 * (c + 1)] = place_of(group, core)
+        place_ref[:, 256 * c : 256 * (c + 1)] = place_of(group, core_ref[0])
         slots.append(slot)
-    for copy in tables:
-        copy.wait()
-    whole = b_ref[...] + db_ref[...]
-    high = whole.astype(BF16)
-    whole_ref[:, :D] = high
-    whole_ref[:, D:] = (whole - high.astype(F32)).astype(BF16)
+    copies[0].wait()
     for c in range(8):
         at = slice(256 * c, 256 * (c + 1))
         delta_ref[at, :] = terms_of(whole_ref, slots[c], None, payload_of(in_ref, c))
-    fields.wait()
-    starts, ends = [], []
-    for j in range(PARTS):
-        line = field_ref[2 * PARTS + j : 2 * PARTS + j + 1, :]
-        line_ref[j : j + 1, :] = line
-        starts.append((jnp.min(line) >> 6) << 6)
-        ends.append(jnp.max(line))
-        bound_ref[j], bound_ref[PARTS + j] = starts[j], ends[j]
     add_deltas(0, total_ref, place_ref, delta_ref)
-    terms.wait()
-    add_windows(0, total_ref, rows_ref, line_ref, starts, ends)
+    for copy in copies[1:]:
+        copy.wait()
+    add_windows(0, total_ref, rows_ref, line_ref, *bounds(bound_ref))
     peer_ref[...] = total_ref[: GROUPS // 2, :]
 
 
 def own_kernel(bound_ref, delta_ref, place_ref, rows_ref, line_ref, out_ref, total_ref):
     add_deltas(1, total_ref, place_ref, delta_ref)
-    starts = [bound_ref[j] for j in range(PARTS)]
-    ends = [bound_ref[PARTS + j] for j in range(PARTS)]
-    add_windows(1, total_ref, rows_ref, line_ref, starts, ends)
+    add_windows(1, total_ref, rows_ref, line_ref, *bounds(bound_ref))
     out_ref[...] = total_ref[: GROUPS // 2, :]
 
 
@@ -388,23 +387,25 @@
     table = pltpu.VMEM((KEYS_DEV, 2 * D), BF16)
     total = pltpu.VMEM((GROUPS // 2 + WINDOW, D), F32)
     half = jax.ShapeDtypeStruct((GROUPS // 2, D), F32)
-    terms, fields, db_table = pl.pallas_call(
+    terms, fields, whole, bound = pl.pallas_call(
         join_a_kernel,
         out_shape=[
             pltpu.HBM((PARTS, A_DEV // PARTS, D), BF16),
             pltpu.HBM((3 * PARTS, A_DEV // PARTS), I32),
-            pltpu.HBM((KEYS_DEV, D), F32),
+            pltpu.HBM((KEYS_DEV, 2 * D), BF16),
+            pltpu.HBM((2 * PARTS,), I32),
         ],
-        in_specs=[SMEM] + [VMEM] * 6,
-        out_specs=[HBM] * 3,
+        in_specs=[SMEM] + [VMEM] * 10,
+        out_specs=[HBM] * 3 + [SMEM],
         scratch_shapes=[
             table,
+            table,
             pltpu.VMEM((PARTS, A_DEV // PARTS, D), BF16),
-            pltpu.SemaphoreType.DMA((PARTS + 5,)),
+            pltpu.SemaphoreType.DMA((PARTS + 2,)),
         ],
         compiler_params=LIMIT,
         name="join_a",
-    )(view, *db, *sorted_rows)
+    )(view, *db, *b, *sorted_rows)
     peer, delta, place, term_rows, line, bound = pl.pallas_call(
         join_d_kernel,
         out_shape=[
@@ -415,19 +416,12 @@
             jax.ShapeDtypeStruct((PARTS, A_DEV // PARTS), I32),
             jax.ShapeDtypeStruct((2 * PARTS,), I32),
         ],
-        in_specs=[SMEM] * 2 + [HBM] * 7 + [VMEM],
+        in_specs=[SMEM] + [HBM] * 4 + [VMEM],
         out_specs=[VMEM] * 5 + [SMEM],
-        scratch_shapes=[
-            table,
-            total,
-            pltpu.VMEM((KEYS_DEV, D), F32),
-            pltpu.VMEM((KEYS_DEV, D), F32),
-            pltpu.VMEM((3 * PARTS, A_DEV // PARTS), I32),
-            pltpu.SemaphoreType.DMA((7,)),
-        ],
+        scratch_shapes=[table, total, pltpu.SemaphoreType.DMA((4,))],
         compiler_params=pltpu.CompilerParams(vmem_limit_bytes=28 * 2**20),
         name="join_d",
-    )(view, core, *map(in_hbm, (db_table, *b, fields, terms)), received)
+    )(core, *map(in_hbm, (bound, whole, fields, terms)), received)
     other = lax.ppermute(peer, "keys_2", [(0, 1), (1, 0)])
     own = pl.pallas_call(
         own_kernel,

time: 115 us -> 114 us (level)
    unnamed x16 -> x6, local copies, waits for them, and re-layouts: 2.31 us -> 1.6 us
  transfers between devices with their start and end apart: 15 -> 15, of which waited for: 2 -> 6; matrix products, arithmetic and copies ran while one was open for 0% -> 1% of each run, Pallas kernels for 18% -> 18%
where the time goes in v8:
time: 114 us; the launch traced here: 113 us
  Pallas kernels  31.5 us (28%)
  starting transfers between devices  28.7 us (25%)
  blocking collectives  28.1 us (25%)
  waiting for transfers between devices  19.7 us (17%)
  other arithmetic  2.15 us (2%)
  local copies, waits for them, and re-layouts  1.6 us (1%)
  between operations  1.5 us (1%)
    all_to_all x1, blocking collectives, shards(): lax.all_to_all(blocks, ('keys_0', 'keys_1', 'view'), 0, 0, tiled=True)  28.1 us
    ppermute x12, starting transfers between devices, shift(): return lax.ppermute(x, 'view', [(j, (j + s) % 4) for j in range(4)])  16 us
    all_to_all x2, waiting for transfers between devices, exchange(): lax.all_to_all(blocks, KEYS, 0, 0, tiled=True).reshape(OWNERS * BLOCK, D)  13.5 us
    all_to_all x2, starting transfers between devices, exchange(): lax.all_to_all(blocks, KEYS, 0, 0, tiled=True).reshape(OWNERS * BLOCK, D)  12.5 us
    pallas_call x2, Pallas kernels, pack(): pl.pallas_call(lambda *refs: pack_kernel(group is not None, *refs), out_s...  8.12 us
    pallas_call x1, Pallas kernels, join(): pl.pallas_call(join_d_kernel, out_shape=[half, jax.ShapeDtypeStruct((rows...  6.89 us
    ppermute x12, waiting for transfers between devices, shift(): return lax.ppermute(x, 'view', [(j, (j + s) % 4) for j in range(4)])  6.18 us
    pallas_call x1, Pallas kernels, sort(): pl.pallas_call(sort_kernel, out_shape=[jax.ShapeDtypeStruct((PARTS, A_DEV...  5.26 us
  transfers between devices with their start and end apart: 15, of which 6 were waited for; matrix products, arithmetic and copies ran while one was open for 1% of the time, Pallas kernels for 18%

profile of v8, /device:TPU:0, one launch (start us, length us, event | category | flops | bytes accessed | tf_op | source)
XLA Modules:
  0.0 113.3 jit_solution(2793011168656496116)
XLA Ops:
  0.7 4.1 %pack_b.1 = bf16[2304,256]{1,0:T(8,128)(2,1)} custom-call(s32[1]{0:T(128)} %bitcast.2.refs_0_, s32[1]{0:T(128)S(6)} %copy.19.refs_1_, s32[128,128]{1,0:T(8,128)} %bitcast.26, s32[8,128]{1,0:T(8,128)} %bitcast.31, s32[8,128]{1,0:T(8,128)} %bitcast.32, bf16[1024,256]{1,0:T(8,128)(2,1)} %refs_5_.1), custom_call_target="tpu_custom_call" | custom-call | tf_op jit(solution)/shard_map/pack_b/pallas_call | solution.py:126
  4.7 8.5 %all-to-all-start = ((bf16[32,72,256]{2,1,0:T(8,128)(2,1)}), bf16[32,72,256]{2,1,0:T(8,128)(2,1)S(1)}, u32[]{:S(2)}, u32[]{:S(2)}) async-start(bf16[32,72,256]{2,1,0:T(8,128)(2,1)} %bitcast.24), calls=%async_computation | async-start | bytes 2359296 | tf_op jit(solution)/shard_map/all_to_all | solution.py:440
  13.9 4.1 %pack_a.1 = bf16[2304,256]{1,0:T(8,128)(2,1)} custom-call(s32[1]{0:T(128)} %bitcast.2.refs_0_, s32[1]{0:T(128)S(6)} %copy.18.refs_1_, s32[128,128]{1,0:T(8,128)} %bitcast.27, s32[8,128]{1,0:T(8,128)} %bitcast.33, s32[8,128]{1,0:T(8,128)} %bitcast.34, s32[8,128]{1,0:T(8,128)} %bitcast.35, bf16[1024,256]{1,0:T(8,128)(2,1)} %refs_6_.1), custom_call_target="tpu_custom_call" | custom-call | tf_op jit(solution)/shard_map/pack_a/pallas_call | solution.py:126
  17.9 13.5 %all-to-all-done = bf16[32,72,256]{2,1,0:T(8,128)(2,1)S(1)} async-done(((bf16[32,72,256]{2,1,0:T(8,128)(2,1)}), bf16[32,72,256]{2,1,0:T(8,128)(2,1)S(1)}, u32[]{:S(2)}, u32[]{:S(2)}) %all-to-all-start) | async-done | bytes 1179680 | tf_op jit(solution)/shard_map/all_to_all | solution.py:440
  31.4 4.0 %all-to-all-start.1 = ((bf16[32,72,256]{2,1,0:T(8,128)(2,1)}), bf16[32,72,256]{2,1,0:T(8,128)(2,1)S(1)}, u32[]{:S(2)}, u32[]{:S(2)}) async-start(bf16[32,72,256]{2,1,0:T(8,128)(2,1)} %bitcast.23), calls=%async_computation.1 | async-start | bytes 2359296 | tf_op jit(solution)/shard_map/all_to_all | solution.py:440
  35.5 1.6 %copy-done = bf16[4096,256]{1,0:T(8,128)(2,1)S(1)} copy-done((bf16[4096,256]{1,0:T(8,128)(2,1)S(1)}, bf16[4096,256]{1,0:T(8,128)(2,1)}, u32[]{:S(2)}) %copy-start) | copy-done | bytes 2097176
  37.1 1.3 %shard_map.164 = (f32[128,256]{1,0:T(8,128)S(1)}, f32[128,256]{1,0:T(8,128)S(1)}, f32[128,256]{1,0:T(8,128)S(1)}, f32[128,256]{1,0:T(8,128)S(1)}) custom-call(s32[1]{0:T(128)} %bitcast.1.view_ref, s32[32,128]{1,0:T(8,128)S(1)} %bitcast.21, s32[32,128]{1,0:T(8,128)S(1)} %bitcast.22, bf16[4096,256]{1,0:T(8,128)(2,1)S(1)} %copy-done), custom_call_target="tpu_custom_call" | custom-call | tf_op jit(solution)/shard_map/pallas_call | solution.py:182
  38.3 1.6 %collective-permute-start.6 = (f32[128,256]{1,0:T(8,128)S(1)}, f32[128,256]{1,0:T(8,128)S(1)}, u32[]{:S(2)}, u32[]{:S(2)}) collective-permute-start(f32[128,256]{1,0:T(8,128)S(1)} %get-tuple-element.30), channel_id=1, source_target_pairs={{0,1},{1,2},{2,3},{3,0},{4,5},{5,6},{6,7},{7,4},{8,9},{9,10},{10,1... | collective-permute-start | bytes 393224 | tf_op jit(solution)/shard_map/ppermute | solution.py:193
  39.9 2.7 %collective-permute-start.7 = (f32[128,256]{1,0:T(8,128)S(1)}, f32[128,256]{1,0:T(8,128)S(1)}, u32[]{:S(2)}, u32[]{:S(2)}) collective-permute-start(f32[128,256]{1,0:T(8,128)S(1)} %get-tuple-element.31), channel_id=1, source_target_pairs={{0,2},{1,3},{2,0},{3,1},{4,6},{5,7},{6,4},{7,5},{8,10},{9,11},{10,... | collective-permute-start | bytes 393224 | tf_op jit(solution)/shard_map/ppermute | solution.py:193
  42.6 1.4 %collective-permute-start.8 = (f32[128,256]{1,0:T(8,128)S(1)}, f32[128,256]{1,0:T(8,128)S(1)}, u32[]{:S(2)}, u32[]{:S(2)}) collective-permute-start(f32[128,256]{1,0:T(8,128)S(1)} %get-tuple-element.32), channel_id=1, source_target_pairs={{0,3},{1,0},{2,1},{3,2},{4,7},{5,4},{6,5},{7,6},{8,11},{9,8},{10,9... | collective-permute-start | bytes 393224 | tf_op jit(solution)/shard_map/ppermute | solution.py:193
  44.1 1.4 %shard_map.163 = (f32[128,256]{1,0:T(8,128)}, f32[128,256]{1,0:T(8,128)S(1)}, f32[128,256]{1,0:T(8,128)S(1)}, f32[128,256]{1,0:T(8,128)S(1)}) custom-call(s32[1]{0:T(128)} %bitcast.1.view_ref, bf16[2304,256]{1,0:T(8,128)(2,1)S(1)} %bitcast.19), custom_call_target="tpu_custom_call" | custom-call | tf_op jit(solution)/shard_map/pallas_call | solution.py:182
  45.5 0.6 collective-permute-start
  46.1 0.9 collective-permute-start.1
  46.9 1.8 %collective-permute-start.2 = (f32[128,256]{1,0:T(8,128)S(1)}, f32[128,256]{1,0:T(8,128)S(1)}, u32[]{:S(2)}, u32[]{:S(2)}) collective-permute-start(f32[128,256]{1,0:T(8,128)S(1)} %get-tuple-element.28), channel_id=1, source_target_pairs={{0,3},{1,0},{2,1},{3,2},{4,7},{5,4},{6,5},{7,6},{8,11},{9,8},{10,9... | collective-permute-start | bytes 393224 | tf_op jit(solution)/shard_map/ppermute | solution.py:193
  48.7 1.1 collective-permute-done.7
  49.8 1.6 %collective-permute-start.11 = (f32[128,256]{1,0:T(8,128)S(1)}, f32[128,256]{1,0:T(8,128)S(1)}, u32[]{:S(2)}, u32[]{:S(2)}) collective-permute-start(f32[128,256]{1,0:T(8,128)S(1)} %add_add_fusion.refs_4_), channel_id=1, source_target_pairs={{0,3},{1,0},{2,1},{3,2},{4,7},{5,4},{6,5},{7,6},{8,11},{9,8},{10,9... | collective-permute-start | bytes 393224 | tf_op jit(solution)/shard_map/ppermute | solution.py:193
  51.5 1.4 %collective-permute-start.10 = (f32[128,256]{1,0:T(8,128)S(1)}, f32[128,256]{1,0:T(8,128)S(1)}, u32[]{:S(2)}, u32[]{:S(2)}) collective-permute-start(f32[128,256]{1,0:T(8,128)S(1)} %add_add_fusion.refs_4_), channel_id=1, source_target_pairs={{0,2},{1,3},{2,0},{3,1},{4,6},{5,7},{6,4},{7,5},{8,10},{9,11},{10,... | collective-permute-start | bytes 393224 | tf_op jit(solution)/shard_map/ppermute | solution.py:193
  52.9 3.4 %collective-permute-done = f32[128,256]{1,0:T(8,128)S(1)} collective-permute-done((f32[128,256]{1,0:T(8,128)S(1)}, f32[128,256]{1,0:T(8,128)S(1)}, u32[]{:S(2)}, u32[]{:S(2)}) %collective-permute-start) | collective-permute-done | bytes 131104 | tf_op jit(solution)/shard_map/ppermute | solution.py:193
  56.3 0.4 collective-permute-done.2
  56.7 0.9 add_add_fusion.1.refs_0_
  57.7 2.9 %collective-permute-start.5 = (f32[128,256]{1,0:T(8,128)S(1)}, f32[128,256]{1,0:T(8,128)S(1)}, u32[]{:S(2)}, u32[]{:S(2)}) collective-permute-start(f32[128,256]{1,0:T(8,128)S(1)} %add_add_fusion.1.refs_0_), channel_id=1, source_target_pairs={{0,3},{1,0},{2,1},{3,2},{4,7},{5,4},{6,5},{7,6},{8,11},{9,8},{10,9... | collective-permute-start | bytes 393224 | tf_op jit(solution)/shard_map/ppermute | solution.py:193
  60.6 0.9 collective-permute-start.3
  61.5 5.3 %sort.1 = (bf16[8,512,256]{2,1,0:T(8,128)(2,1)S(1)}, s32[24,512]{1,0:T(8,128)S(1)}) custom-call(s32[1]{0:T(128)} %bitcast.core_ref, s32[32,128]{1,0:T(8,128)} %bitcast.28, s32[32,128]{1,0:T(8,128)} %bitcast.29, s32[32,128]{1,0:T(8,128)} %bitcast.30, bf16[4096,256]{1,0:T(8,128)(2,1)} %payload_hbm.1), custom_call_target="tpu_custom_call" | custom-call | tf_op jit(solution)/shard_map/sort/pallas_call | solution.py:275
  66.8 0.3 collective-permute-done.4.refs_2_
  67.1 1.0 collective-permute-done.3.refs_1_
  68.2 4.0 %join_a.1 = (bf16[8,512,256]{2,1,0:T(8,128)(2,1)}, s32[24,512]{1,0:T(8,128)}, bf16[512,512]{1,0:T(8,128)(2,1)}, s32[16]{0:T(128)}) custom-call(s32[1]{0:T(128)} %bitcast.1.view_ref, f32[128,256]{1,0:T(8,128)S(1)} %add_add_fusion.1.refs_0_, f32[128,256]{1,0:T(8,128)S(1)} %collective-permute-done.3.refs_1_, f32[128,256]{1,0:T(8,128)S(1)} %collective-permute-done.4.refs_2_, ...), custom_call_target="tpu_custom_call" | custom-call | tf_op jit(solution)/shard_map/join_a/pallas_call | solution.py:390
  72.2 6.9 %join_d.1 = (f32[2048,256]{1,0:T(8,128)S(1)}, bf16[2048,256]{1,0:T(8,128)(2,1)S(1)}, s32[1,2048]{1,0:T(1,128)S(1)}, bf16[8,512,256]{2,1,0:T(8,128)(2,1)S(1)}, s32[8,512]{1,0:T(8,128)S(1)}, /*index=5*/s32[16]{0:T(128)S(1)}) custom-call(s32[1]{0:T(128)} %bitcast.core_ref, s32[16]{0:T(128)} %get-tuple-element.35.refs_0_, ...), custom_call_target="tpu_custom_call" | custom-call | tf_op jit(solution)/shard_map/join_d/pallas_call | solution.py:409
  79.1 0.3 collective-permute-start.12
  79.4 4.6 %join_own.1 = f32[2048,256]{1,0:T(8,128)S(1)} custom-call(s32[16]{0:T(128)S(1)} %get-tuple-element.39.bound_ref, bf16[2048,256]{1,0:T(8,128)(2,1)S(1)} %get-tuple-element.40.delta_ref, s32[1,2048]{1,0:T(1,128)S(1)} %get-tuple-element.41.place_ref, bf16[8,512,256]{2,1,0:T(8,128)(2,1)S(1)} %get-tuple-element.42.rows_ref, s32[8,512]{1,0:T(8,128)S(1)} %get-tuple-element.43.line_ref), custom_call_target="tpu_custom_call" | custom-call | tf_op jit(solution)/shard_map/join_own/pallas_call | solution.py:426
  84.0 0.4 add_convert_fusion
  84.4 28.1 %all_to_all.15 = bf16[64,32,256]{2,1,0:T(8,128)(2,1)S(1)} all-to-all(bf16[64,32,256]{2,1,0:T(8,128)(2,1)S(1)} %bitcast.25), channel_id=1, replica_groups=mesh['keys_0'=4,'keys_1'=4,'keys_2'=2,'view'=4] {'keys_0','keys_1','view'}, dimensions={0} | all-to-all | bytes 2097152 | tf_op jit(solution)/shard_map/all_to_all | solution.py:483
  112.5 0.8 convert_reduce_fusion
  (17 shorter events, 0.1 us)
Async XLA Ops:
  4.7 26.7 %all-to-all-start = ((bf16[32,72,256]{2,1,0:T(8,128)(2,1)}), bf16[32,72,256]{2,1,0:T(8,128)(2,1)S(1)}, u32[]{:S(2)}, u32[]{:S(2)}) async-start(bf16[32,72,256]{2,1,0:T(8,128)(2,1)} %bitcast.24), calls=%async_computation | async-start | bytes 2359296 | tf_op jit(solution)/shard_map/all_to_all | solution.py:440
  13.2 22.3 %copy-start.1 = (s32[4096]{0:T(1024)S(1)}, s32[4096]{0:T(1024)}, u32[]{:S(2)}) copy-start(s32[4096]{0:T(1024)} %param.22) | copy-start | bytes 49156
  13.2 22.2 %copy-start.2 = (s32[4096]{0:T(1024)S(1)}, s32[4096]{0:T(1024)}, u32[]{:S(2)}) copy-start(s32[4096]{0:T(1024)} %param.23) | copy-start | bytes 49156
  31.4 40.8 %all-to-all-start.1 = ((bf16[32,72,256]{2,1,0:T(8,128)(2,1)}), bf16[32,72,256]{2,1,0:T(8,128)(2,1)S(1)}, u32[]{:S(2)}, u32[]{:S(2)}) async-start(bf16[32,72,256]{2,1,0:T(8,128)(2,1)} %bitcast.23), calls=%async_computation.1 | async-start | bytes 2359296 | tf_op jit(solution)/shard_map/all_to_all | solution.py:440
  35.5 1.6 %copy-start = (bf16[4096,256]{1,0:T(8,128)(2,1)S(1)}, bf16[4096,256]{1,0:T(8,128)(2,1)}, u32[]{:S(2)}) copy-start(bf16[4096,256]{1,0:T(8,128)(2,1)} %payload_ref.1) | copy-start | bytes 6291460
  38.3 8.6 %collective-permute-start.6 = (f32[128,256]{1,0:T(8,128)S(1)}, f32[128,256]{1,0:T(8,128)S(1)}, u32[]{:S(2)}, u32[]{:S(2)}) collective-permute-start(f32[128,256]{1,0:T(8,128)S(1)} %get-tuple-element.30), channel_id=1, source_target_pairs={{0,1},{1,2},{2,3},{3,0},{4,5},{5,6},{6,7},{7,4},{8,9},{9,10},{10,1... | collective-permute-start | bytes 393224 | tf_op jit(solution)/shard_map/ppermute | solution.py:193
  39.9 9.9 %collective-permute-start.7 = (f32[128,256]{1,0:T(8,128)S(1)}, f32[128,256]{1,0:T(8,128)S(1)}, u32[]{:S(2)}, u32[]{:S(2)}) collective-permute-start(f32[128,256]{1,0:T(8,128)S(1)} %get-tuple-element.31), channel_id=1, source_target_pairs={{0,2},{1,3},{2,0},{3,1},{4,6},{5,7},{6,4},{7,5},{8,10},{9,11},{10,... | collective-permute-start | bytes 393224 | tf_op jit(solution)/shard_map/ppermute | solution.py:193
  42.6 7.2 %collective-permute-start.8 = (f32[128,256]{1,0:T(8,128)S(1)}, f32[128,256]{1,0:T(8,128)S(1)}, u32[]{:S(2)}, u32[]{:S(2)}) collective-permute-start(f32[128,256]{1,0:T(8,128)S(1)} %get-tuple-element.32), channel_id=1, source_target_pairs={{0,3},{1,0},{2,1},{3,2},{4,7},{5,4},{6,5},{7,6},{8,11},{9,8},{10,9... | collective-permute-start | bytes 393224 | tf_op jit(solution)/shard_map/ppermute | solution.py:193
  45.5 10.9 %collective-permute-start = (f32[128,256]{1,0:T(8,128)S(1)}, f32[128,256]{1,0:T(8,128)S(1)}, u32[]{:S(2)}, u32[]{:S(2)}) collective-permute-start(f32[128,256]{1,0:T(8,128)S(1)} %get-tuple-element.26), channel_id=1, source_target_pairs={{0,1},{1,2},{2,3},{3,0},{4,5},{5,6},{6,7},{7,4},{8,9},{9,10},{10,1... | collective-permute-start | bytes 393224 | tf_op jit(solution)/shard_map/ppermute | solution.py:193
  46.1 10.3 %collective-permute-start.1 = (f32[128,256]{1,0:T(8,128)S(1)}, f32[128,256]{1,0:T(8,128)S(1)}, u32[]{:S(2)}, u32[]{:S(2)}) collective-permute-start(f32[128,256]{1,0:T(8,128)S(1)} %get-tuple-element.27), channel_id=1, source_target_pairs={{0,2},{1,3},{2,0},{3,1},{4,6},{5,7},{6,4},{7,5},{8,10},{9,11},{10,... | collective-permute-start | bytes 393224 | tf_op jit(solution)/shard_map/ppermute | solution.py:193
  46.9 9.8 %collective-permute-start.2 = (f32[128,256]{1,0:T(8,128)S(1)}, f32[128,256]{1,0:T(8,128)S(1)}, u32[]{:S(2)}, u32[]{:S(2)}) collective-permute-start(f32[128,256]{1,0:T(8,128)S(1)} %get-tuple-element.28), channel_id=1, source_target_pairs={{0,3},{1,0},{2,1},{3,2},{4,7},{5,4},{6,5},{7,6},{8,11},{9,8},{10,9... | collective-permute-start | bytes 393224 | tf_op jit(solution)/shard_map/ppermute | solution.py:193
  49.8 10.7 %collective-permute-start.11 = (f32[128,256]{1,0:T(8,128)S(1)}, f32[128,256]{1,0:T(8,128)S(1)}, u32[]{:S(2)}, u32[]{:S(2)}) collective-permute-start(f32[128,256]{1,0:T(8,128)S(1)} %add_add_fusion.refs_4_), channel_id=1, source_target_pairs={{0,3},{1,0},{2,1},{3,2},{4,7},{5,4},{6,5},{7,6},{8,11},{9,8},{10,9... | collective-permute-start | bytes 393224 | tf_op jit(solution)/shard_map/ppermute | solution.py:193
  51.5 15.3 %collective-permute-start.10 = (f32[128,256]{1,0:T(8,128)S(1)}, f32[128,256]{1,0:T(8,128)S(1)}, u32[]{:S(2)}, u32[]{:S(2)}) collective-permute-start(f32[128,256]{1,0:T(8,128)S(1)} %add_add_fusion.refs_4_), channel_id=1, source_target_pairs={{0,2},{1,3},{2,0},{3,1},{4,6},{5,7},{6,4},{7,5},{8,10},{9,11},{10,... | collective-permute-start | bytes 393224 | tf_op jit(solution)/shard_map/ppermute | solution.py:193
  56.3 10.5 %collective-permute-start.9 = (f32[128,256]{1,0:T(8,128)S(1)}, f32[128,256]{1,0:T(8,128)S(1)}, u32[]{:S(2)}, u32[]{:S(2)}) collective-permute-start(f32[128,256]{1,0:T(8,128)S(1)} %add_add_fusion.refs_4_), channel_id=1, source_target_pairs={{0,1},{1,2},{2,3},{3,0},{4,5},{5,6},{6,7},{7,4},{8,9},{9,10},{10,1... | collective-permute-start | bytes 393224 | tf_op jit(solution)/shard_map/ppermute | solution.py:193
  57.7 9.2 %collective-permute-start.5 = (f32[128,256]{1,0:T(8,128)S(1)}, f32[128,256]{1,0:T(8,128)S(1)}, u32[]{:S(2)}, u32[]{:S(2)}) collective-permute-start(f32[128,256]{1,0:T(8,128)S(1)} %add_add_fusion.1.refs_0_), channel_id=1, source_target_pairs={{0,3},{1,0},{2,1},{3,2},{4,7},{5,4},{6,5},{7,6},{8,11},{9,8},{10,9... | collective-permute-start | bytes 393224 | tf_op jit(solution)/shard_map/ppermute | solution.py:193
  60.6 6.6 %collective-permute-start.4 = (f32[128,256]{1,0:T(8,128)S(1)}, f32[128,256]{1,0:T(8,128)S(1)}, u32[]{:S(2)}, u32[]{:S(2)}) collective-permute-start(f32[128,256]{1,0:T(8,128)S(1)} %add_add_fusion.1.refs_0_), channel_id=1, source_target_pairs={{0,2},{1,3},{2,0},{3,1},{4,6},{5,7},{6,4},{7,5},{8,10},{9,11},{10,... | collective-permute-start | bytes 393224 | tf_op jit(solution)/shard_map/ppermute | solution.py:193
  60.6 7.6 %collective-permute-start.3 = (f32[128,256]{1,0:T(8,128)S(1)}, f32[128,256]{1,0:T(8,128)S(1)}, u32[]{:S(2)}, u32[]{:S(2)}) collective-permute-start(f32[128,256]{1,0:T(8,128)S(1)} %add_add_fusion.1.refs_0_), channel_id=1, source_target_pairs={{0,1},{1,2},{2,3},{3,0},{4,5},{5,6},{6,7},{7,4},{8,9},{9,10},{10,1... | collective-permute-start | bytes 393224 | tf_op jit(solution)/shard_map/ppermute | solution.py:193
  79.1 4.9 %collective-permute-start.12 = (f32[2048,256]{1,0:T(8,128)S(1)}, f32[2048,256]{1,0:T(8,128)S(1)}, u32[]{:S(2)}, u32[]{:S(2)}) collective-permute-start(f32[2048,256]{1,0:T(8,128)S(1)} %get-tuple-element.44), channel_id=1, source_target_pairs={{0,4},{4,0},{1,5},{5,1},{2,6},{6,2},{3,7},{7,3},{8,12},{12,8},{9,1... | collective-permute-start | bytes 6291464 | tf_op jit(solution)/shard_map/ppermute | solution.py:425
